TPU v7x, 512 devices: a whole 4x8x8 slice. The times are simulated.
512 devices in a mesh: seq: 32 (over y, x), dp: 16 (over z, core).
Axes of the slice: x: 4, y: 8, z: 8, core: 2. Of those that a mesh axis runs over, the one named last changes fastest.
Arguments:
- layer_input: bfloat16 [16, 8192, 2560], P('dp', 'seq'), may hold values from -14400 to 14400
- scan_input: bfloat16 [16, 8192, 2560], P('dp', 'seq'), may hold values from -0.75 to 0.75
- scan_cotangent: bfloat16 [16, 8192, 2560], P('dp', 'seq'), may hold values from -0.03125 to 0.03125
- step_size: float32 [16, 40, 8192], P('dp', None, 'seq'), may hold values from 0.5 to 2
- log_decay: float32 [16, 40, 8192], P('dp', None, 'seq'), may hold values from -2.25 to 0
- state_inputs: bfloat16 [16, 8192, 256], P('dp', 'seq'), may hold values from -4 to 4
- entry_state: bfloat16 [16, 32, 2560, 128], P('dp', 'seq'), may hold values from -8 to 8
Outputs:
- state_input_grad: bfloat16 [16, 8192, 256], P('dp', 'seq')
- weight_grad: float32 [2560, 256], P(('seq', 'dp'))
All inputs are finite; a program needn't handle non-finite values. Where the computation divides by a largest or mean magnitude, that divisor is 1e-20 or more.
Results may differ from a plain program's by a relative error of at most 0.013.
Values may be sent and summed in bfloat16 or wider, within the bound.
No kernel may reach another device: no remote copies, remote signals or barrier semaphores. Data moves between devices by JAX's collectives and lax.ppermute only.
A program may use at most 128 MiB of HBM per device.

v0:
```python
import functools

import jax
import jax.numpy as jnp
from jax import lax
from jax.sharding import Mesh
from jax.sharding import PartitionSpec as P

STRETCH = 256
SEQ_DP = ("seq_0", "seq_1", "dp_0", "dp_1")
SEQ = ("seq_0", "seq_1")
DP = ("dp_0", "dp_1")


epsilon = 1e-06


def by_axis(x, axes):
    return functools.reduce(lax.pmax, axes, x)


def filled_with(x, identity):
    return jax.tree.map(
        lambda part, zero: jnp.zeros_like(part) + jnp.asarray(zero, part.dtype), x, identity
    )


def prefix_by_axis(x, axes, combine, identity):
    before = start = filled_with(x, identity)
    running = x
    for axis in reversed(axes):
        length, place = (lax.axis_size(axis), lax.axis_index(axis))
        pieces = jax.tree.map(
            lambda part, kind: lax.all_gather(part.astype(kind), axis),
            running,
            (jnp.bfloat16, jnp.bfloat16),
        )
        inside, running = (start, start)
        for k in reversed(range(length)):
            passed = k > place
            running = combine(
                running, jax.tree.map(lambda part, own: part[k].astype(own.dtype), pieces, x)
            )
            inside = jax.tree.map(lambda new, old: jnp.where(passed, new, old), running, inside)
        before = combine(inside, before)
    return before


def in_blocks(x, dim, length):
    lengths = x.shape
    tiles = x.reshape(*lengths[:dim], length, lengths[dim] // length, *lengths[dim + 1 :])
    return jnp.moveaxis(tiles, dim, 0)


def sent_and_summed(x, axis, dim):
    tiles = in_blocks(x, dim, lax.axis_size(axis))
    arrived = lax.all_to_all(tiles, axis, split_axis=0, concat_axis=0, tiled=True)
    return arrived.astype(jnp.float32).sum(axis=0)


def summed_on_arrival(x, axis, dim):
    length = lax.axis_size(axis)
    tiles = lax.all_to_all(in_blocks(x, dim, length), axis, 0, 0, tiled=True)
    return jnp.sum(tiles, axis=0)


def silu_slope(value):
    sigma = jax.nn.sigmoid(value)
    return sigma * (1.0 + value * (1.0 - sigma))


def compose(earlier, later):
    return (earlier[0] * later[0], later[1] + later[0][:, :, None, None] * earlier[1])


def block_summary(pieces):
    inputs, cotangents, steps, cumulative, writes, reads = pieces
    weighted_cot = (cotangents * jnp.exp(cumulative).T[:, :, None]).astype(jnp.bfloat16)
    weighted_in = (
        inputs * (steps * jnp.exp(cumulative[:, -1:] - cumulative)).T[:, :, None]
    ).astype(jnp.bfloat16)
    from_later = jnp.einsum("thp,tn->hpn", weighted_cot, reads, preferred_element_type=jnp.float32)
    from_earlier = jnp.einsum(
        "thp,tn->hpn", weighted_in, writes, preferred_element_type=jnp.float32
    )
    return (weighted_cot, weighted_in, from_later, from_earlier, jnp.exp(cumulative[:, -1]))


def block_inner(pieces):
    inputs, cotangents, steps, cumulative, writes, reads = pieces
    length = inputs.shape[0]
    later = lax.broadcasted_iota(jnp.int32, (length, length), 0) >= lax.broadcasted_iota(
        jnp.int32, (length, length), 1
    )
    scores = jnp.einsum("shp,thp->hst", cotangents, inputs, preferred_element_type=jnp.float32)
    spread = jnp.where(later[None], cumulative[:, :, None] - cumulative[:, None, :], 0.0)
    decay = jnp.where(later[None], jnp.exp(spread), 0.0)
    mixing = (scores * decay * steps[:, None, :]).astype(jnp.bfloat16)
    inner_write = jnp.einsum("hst,sn->tn", mixing, reads, preferred_element_type=jnp.float32)
    inner_read = jnp.einsum("hst,tn->sn", mixing, writes, preferred_element_type=jnp.float32)
    return (inner_write, inner_read)


def block_both(pieces):
    return block_summary(pieces) + block_inner(pieces)


def on_device(
    layer_input, scan_input, scan_cotangent, step_size, log_decay, state_inputs, entry_state
):
    seq_local, tokens, width = layer_input.shape
    heads = step_size.shape[1]
    channels = scan_input.shape[2]
    head_size = channels // heads
    states = state_inputs.shape[2] // 2
    blocks = tokens // STRETCH
    count = seq_local * blocks
    local_peaks = jnp.max(jnp.abs(layer_input), axis=(0, 1))
    peaks = by_axis(local_peaks, SEQ_DP).astype(jnp.float32)
    inputs = scan_input.reshape(count, STRETCH, heads, head_size)
    cotangents = scan_cotangent.reshape(count, STRETCH, heads, head_size)
    steps = (
        step_size.reshape(seq_local, heads, blocks, STRETCH)
        .transpose(0, 2, 1, 3)
        .reshape(count, heads, STRETCH)
    )
    decays = (
        log_decay.reshape(seq_local, heads, blocks, STRETCH)
        .transpose(0, 2, 1, 3)
        .reshape(count, heads, STRETCH)
    )
    cumulative = jnp.cumsum(decays, axis=2)
    preact = state_inputs.astype(jnp.float32)
    activated = jax.nn.silu(preact).astype(jnp.bfloat16)
    writes = activated[:, :, :states]
    reads = activated[:, :, states:]
    pieces = (inputs, cotangents, steps, cumulative, writes, reads)
    weighted_cot, weighted_in, from_later, from_earlier, totals, inner_write, inner_read = lax.map(
        block_both, pieces
    )
    from_later = from_later.reshape(seq_local, blocks, heads, head_size, states)
    from_earlier = from_earlier.reshape(seq_local, blocks, heads, head_size, states)
    totals = totals.reshape(seq_local, blocks, heads)
    later_sum = from_later[:, blocks - 1]
    device_decay = jnp.prod(totals, axis=1)
    identity = (jnp.ones_like(device_decay), jnp.zeros_like(later_sum))
    beyond = prefix_by_axis((device_decay, later_sum), SEQ, compose, identity)[1]
    weighted_in = weighted_in.reshape(seq_local, blocks, STRETCH, channels)
    weighted_cot = weighted_cot.reshape(seq_local, blocks, STRETCH, channels)
    carried_write = []
    state_now = beyond
    block_index = 0
    operand = state_now.astype(jnp.bfloat16).reshape(seq_local, channels, states)
    carried_write.append(
        jnp.einsum(
            "btk,bkn->btn", weighted_in[:, block_index], operand, preferred_element_type=jnp.float32
        )
    )
    carried_write = jnp.stack(carried_write[::-1], axis=1).reshape(seq_local, tokens, states)
    carried_read = []
    state_now = entry_state.reshape(seq_local, heads, head_size, states).astype(jnp.float32)
    block_index = 0
    operand = state_now.astype(jnp.bfloat16).reshape(seq_local, channels, states)
    carried_read.append(
        jnp.einsum(
            "btk,bkn->btn",
            weighted_cot[:, block_index],
            operand,
            preferred_element_type=jnp.float32,
        )
    )
    carried_read = jnp.stack(carried_read, axis=1).reshape(seq_local, tokens, states)
    grad_write = inner_write + carried_write
    grad_read = inner_read + carried_read
    state_input_grad = (
        jnp.concatenate([grad_write, grad_read], axis=2) * silu_slope(preact)
    ).astype(jnp.bfloat16)
    factor = 1.0 / (peaks + epsilon)
    quantized = (layer_input.reshape(seq_local * tokens, width) * factor).astype(jnp.bfloat16)
    grads = state_input_grad.reshape(seq_local * tokens, 2 * states)
    partial_rows = sent_and_summed(
        lax.dot_general(
            quantized, grads, (((0,), (0,)), ((), ())), preferred_element_type=jnp.float32
        ).astype(jnp.bfloat16),
        SEQ,
        0,
    )
    summed = summed_on_arrival(partial_rows, DP, 0)
    return (state_input_grad, summed)


def solution(mesh):
    torus = Mesh(mesh.devices.reshape(8, 4, 8, 2), ("seq_0", "seq_1", "dp_0", "dp_1"))
    placed = (
        P(DP, SEQ, None),
        P(DP, SEQ, None),
        P(DP, SEQ, None),
        P(DP, None, SEQ),
        P(DP, None, SEQ),
        P(DP, SEQ, None),
        P(DP, SEQ, None, None),
    )
    return jax.shard_map(
        on_device,
        mesh=torus,
        in_specs=placed,
        out_specs=(P(DP, SEQ, None), P(SEQ_DP, None)),
        check_vma=False,
    )
```

profile of v0, /device:TPU:1, one launch (start us, length us, event | category | flops | bytes accessed | tf_op | source)
XLA Modules:
  0.0 214.3 jit_solution(10862501995342099276)
XLA Ops:
  7.2 0.0 copy-start
  7.2 0.0 all-gather.7.cloned.1.call-start
  7.2 0.8 copy_bitcast_fusion
  8.1 0.6 reduce-window.6
  8.6 0.2 slice_reduce_fusion
  8.9 0.1 copy.33
  9.0 1.0 copy.34
  10.0 0.1 fusion.36
  10.1 1.6 copy.29
  11.7 0.0 copy-start.2
  11.7 0.1 broadcast.284
  11.8 0.8 exponential_bitcast_fusion
  12.6 0.3 fusion
  12.9 0.0 copy-done.2
  12.9 0.0 copy-start.7
  12.9 1.4 convolution_convert_fusion.1
  14.3 0.0 all-gather.7.cloned.1.call-update
  14.3 0.0 all-gather.5.cloned.1.call-start
  14.4 1.3 dynamic-slice
  16.3 0.0 copy-done.7
  16.3 0.2 fusion.48
  16.5 0.2 dynamic-update-slice
  16.7 9.3 %all-reduce = bf16[160]{0:T(256)(128)(2,1)S(1)} all-reduce(bf16[160]{0:T(256)(128)(2,1)S(1)} %dynamic-update-slice), channel_id=3, replica_groups=mesh['seq_0'=8,'seq_1'=4,'dp_0'=8,'dp_1'=2] {'seq_1'}, use_global_device_ids=true, to_apply=%add | all-reduce | flops 160 | bytes 640
  26.0 0.6 broadcast_select_fusion.3
  26.6 0.6 slice_convert_fusion.3
  27.2 33.0 %all-gather.7.cloned.1.call-done = bf16[160,64,128]{2,1,0:T(8,128)(2,1)} async-done(((bf16[40,64,128]{2,1,0:T(8,128)(2,1)}), bf16[160,64,128]{2,1,0:T(8,128)(2,1)}) %all-gather.7.cloned.1.call-update) | async-done | bytes 2621456 | tf_op jit(solution)/shard_map/all_gather | solution.py:34
  60.2 3.4 %fusion.19 = bf16[1,1,40,64,128]{4,3,2,1,0:T(8,128)(2,1)} fusion(f32[40]{0:T(128)S(1)} %get-tuple-element.59, f32[40]{0:T(128)} %get-tuple-element.60, f32[40]{0:T(128)S(1)} %get-tuple-element.58, f32[40]{0:T(128)S(1)} %get-tuple-element.57, bf16[160,64,128]{2,1,0:T(8,128)(2,1)} %all-gather.7.cloned.1.call-done), kind=kLoop, calls=%fused_computation.29 | loop fusion | flops 3932160 | bytes 3277440 | tf_op jit(solution)/shard_map/convert_element_type | solution.py:34
  63.6 0.0 copy-done.10
  63.6 0.0 copy-done.12
  63.6 0.0 copy-done.13
  63.6 0.0 all-gather.5.cloned.1.call-update
  63.6 1.4 copy.30
  65.1 0.9 slice_reduce_fusion.1
  66.0 0.9 multiply_bitcast_fusion
  66.9 0.0 copy-start.1
  66.9 2.8 %fusion.1 = bf16[1,256,2560]{1,2,0:T(8,128)(2,1)} fusion(bf16[1,256,2560]{1,2,0:T(8,128)(2,1)} %copy.30, f32[256,40]{0,1:T(8,128)S(1)} %multiply_bitcast_fusion), kind=kLoop, calls=%fused_computation.6 | loop fusion | flops 1966080 | bytes 2662400 | tf_op jit(solution)/shard_map/while/body/eval_jaxpr/convert_element_type | solution.py:81
  69.7 0.1 fusion.59
  69.8 13.3 %all_gather.22 = bf16[8,1,40]{2,1,0:T(2,128)(2,1)} all-gather(bf16[1,1,40]{2,1,0:T(2,128)(2,1)S(1)} %fusion.59), channel_id=1, replica_groups=mesh['seq_0'=8,'seq_1'=4,'dp_0'=8,'dp_1'=2] {'seq_0'}, dimensions={0}, use_global_device_ids=true | all-gather | bytes 720 | tf_op jit(solution)/shard_map/all_gather | solution.py:34
  83.1 0.2 abs_reduce_fusion
  83.2 14.4 %pmax.28 = bf16[2560]{0:T(1024)(128)(2,1)S(1)} all-reduce(bf16[2560]{0:T(1024)(128)(2,1)S(1)} %abs_reduce_fusion), channel_id=1, replica_groups=mesh['seq_0'=8,'seq_1'=4,'dp_0'=8,'dp_1'=2] {'seq_0'}, use_global_device_ids=true, to_apply=%region_4.0 | all-reduce | flops 2560 | bytes 10240 | tf_op jit(solution)/shard_map/pmax | solution.py:19
  97.7 7.1 %pmax.29 = bf16[2560]{0:T(1024)(128)(2,1)S(1)} all-reduce(bf16[2560]{0:T(1024)(128)(2,1)S(1)} %pmax.28), channel_id=1, replica_groups=mesh['seq_0'=8,'seq_1'=4,'dp_0'=8,'dp_1'=2] {'seq_1'}, use_global_device_ids=true, to_apply=%region_5.0 | all-reduce | flops 2560 | bytes 10240 | tf_op jit(solution)/shard_map/pmax | solution.py:19
  104.8 16.2 %pmax.30 = bf16[2560]{0:T(1024)(128)(2,1)S(1)} all-reduce(bf16[2560]{0:T(1024)(128)(2,1)S(1)} %pmax.29), channel_id=1, replica_groups=mesh['seq_0'=8,'seq_1'=4,'dp_0'=8,'dp_1'=2] {'dp_0'}, use_global_device_ids=true, to_apply=%region_6.7 | all-reduce | flops 2560 | bytes 10240 | tf_op jit(solution)/shard_map/pmax | solution.py:19
  121.0 13.7 %pmax.31 = bf16[2560]{0:T(1024)(128)(2,1)} all-reduce(bf16[2560]{0:T(1024)(128)(2,1)S(1)} %pmax.30), channel_id=1, replica_groups=mesh['seq_0'=8,'seq_1'=4,'dp_0'=8,'dp_1'=2] {'dp_1'}, use_global_device_ids=true, to_apply=%region_7.8 | all-reduce | flops 2560 | bytes 10240 | tf_op jit(solution)/shard_map/pmax | solution.py:19
  134.8 5.7 %convert_reduce_fusion = bf16[256,256]{1,0:T(8,128)(2,1)S(1)} fusion(f32[40,256]{1,0:T(8,128)} %bitcast.162, f32[40,256]{1,0:T(8,128)} %get-tuple-element.35, pred[256,256]{1,0:T(8,128)(4,1)S(1)} %iota_compare_fusion, bf16[256,40,64]{0,2,1:T(8,128)(2,1)} %bitcast.156, bf16[256,40,64]{0,2,1:T(8,128)(2,1)} %bitcast.157), kind=kOutput, calls=%fused_computation | convolution fusion | flops 356450304 | bytes 2899968 | tf_op jit(solution)/shard_map/while/body/eval_jaxpr/shp,thp->hst/dot_general | solution.py:95
  140.5 0.0 copy-start.8
  140.6 0.2 fusion.42
  140.8 1.1 fusion.29
  141.8 0.5 fusion.50
  142.4 0.6 fusion.57
  143.0 0.0 copy-done.8
  143.0 0.8 fusion.44
  143.8 6.1 %fusion.11 = bf16[1,1,40,64,128]{4,3,2,1,0:T(8,128)(2,1)S(1)} fusion(bf16[8,1,40,64,128]{4,3,2,1,0:T(8,128)(2,1)} %all-gather.5.cloned.1.call-done, f32[40]{0:T(128)} %copy-done.13, f32[40]{0:T(128)} %get-tuple-element.60, f32[40]{0:T(128)} %copy-done.12, f32[40]{0:T(128)} %fusion.50, f32[40]{0:T(128)} %get-tuple-element.37, f32[40]{0:T(128)} %get-tuple-element.38, ...), kind=kLoop, calls=%fused_computation.19 | loop fusion | flops 16056320 | bytes 8521772 | tf_op jit(solution)/shard_map/convert_element_type | solution.py:153
  149.9 0.0 copy-start.6
  149.9 0.4 fusion.23
  150.4 0.4 copy-done.6
  150.8 0.1 fusion.40
  150.9 0.6 convolution_convert_fusion
  151.5 39.4 %all_to_all.10 = bf16[32,80,256]{2,1,0:T(8,128)(2,1)S(1)} all-to-all(bf16[32,80,256]{2,1,0:T(8,128)(2,1)S(1)} %bitcast.158), channel_id=1, replica_groups=mesh['seq_0'=8,'seq_1'=4,'dp_0'=8,'dp_1'=2] {'seq_0','seq_1'}, dimensions={0} | all-to-all | bytes 2621440 | tf_op jit(solution)/shard_map/all_to_all | solution.py:57
  190.9 0.2 convert_reduce_fusion.1
  191.1 0.7 reshape.515
  191.7 6.2 %all-to-all-start.1 = ((f32[16,5,256]{2,1,0:T(8,128)}), f32[16,5,256]{2,1,0:T(8,128)S(1)}, u32[]{:S(2)}, u32[]{:S(2)}) async-start(f32[16,5,256]{2,1,0:T(8,128)} %reshape.515), calls=%async_computation.1 | async-start | bytes 262144 | tf_op jit(solution)/shard_map/all_to_all | solution.py:63
  197.9 0.8 copy.38
  198.7 8.1 %all-to-all-done.1 = f32[16,5,256]{2,1,0:T(8,128)S(1)} async-done(((f32[16,5,256]{2,1,0:T(8,128)}), f32[16,5,256]{2,1,0:T(8,128)S(1)}, u32[]{:S(2)}, u32[]{:S(2)}) %all-to-all-start.1) | async-done | bytes 81952 | tf_op jit(solution)/shard_map/all_to_all | solution.py:63
  206.8 0.6 reduce_sum.34
  (22 shorter events, 0.1 us)
Async XLA Ops:
  7.2 133.6 %copy-start = (bf16[1,1,2560,128]{3,2,1,0:T(8,128)(2,1)S(1)}, bf16[1,1,2560,128]{3,2,1,0:T(8,128)(2,1)}, u32[]{:S(2)}) copy-start(bf16[1,1,2560,128]{3,2,1,0:T(8,128)(2,1)} %param.13) | copy-start | bytes 1966084
  7.2 53.0 %all-gather.7.cloned.1.call-start = ((), (), s32[]{:S(2)}) async-start(), calls=%async_computation.3 | async-start | bytes 3276800 | tf_op jit(solution)/shard_map/all_gather | solution.py:34
  11.7 1.2 copy-start.2
  12.9 3.4 %copy-start.7 = (f32[40,256]{1,0:T(8,128)S(1)}, f32[40,256]{1,0:T(8,128)}, u32[]{:S(2)}) copy-start(f32[40,256]{1,0:T(8,128)} %get-tuple-element.35) | copy-start | bytes 122884
  14.3 129.5 %all-gather.5.cloned.1.call-start = ((), (), s32[]{:S(2)}) async-start(), calls=%async_computation.2 | async-start | bytes 5898240 | tf_op jit(solution)/shard_map/all_gather | solution.py:34
  26.6 37.0 %copy-start.10 = (f32[40]{0:T(128)}, f32[40]{0:T(128)S(1)}, u32[]{:S(2)}) copy-start(f32[40]{0:T(128)S(1)} %get-tuple-element.57) | copy-start | bytes 484
  27.2 36.4 %copy-start.12 = (f32[40]{0:T(128)}, f32[40]{0:T(128)S(1)}, u32[]{:S(2)}) copy-start(f32[40]{0:T(128)S(1)} %get-tuple-element.58) | copy-start | bytes 484
  27.2 36.4 %copy-start.13 = (f32[40]{0:T(128)}, f32[40]{0:T(128)S(1)}, u32[]{:S(2)}) copy-start(f32[40]{0:T(128)S(1)} %get-tuple-element.59) | copy-start | bytes 484
  60.2 3.4 %copy-start.4 = (bf16[1,256,2560]{2,1,0:T(8,128)(2,1)S(1)}, bf16[1,256,2560]{2,1,0:T(8,128)(2,1)}, u32[]{:S(2)}) copy-start(bf16[1,256,2560]{2,1,0:T(8,128)(2,1)} %param.8) | copy-start | bytes 3932164
  66.9 16.2 %copy-start.1 = (bf16[1,256,2560]{2,1,0:T(8,128)(2,1)S(1)}, bf16[1,256,2560]{2,1,0:T(8,128)(2,1)}, u32[]{:S(2)}) copy-start(bf16[1,256,2560]{2,1,0:T(8,128)(2,1)} %param.7) | copy-start | bytes 3932164
  140.5 1.3 copy-start.9
  140.5 2.4 %copy-start.8 = (bf16[2560]{0:T(1024)(128)(2,1)S(1)}, bf16[2560]{0:T(1024)(128)(2,1)}, u32[]{:S(2)}) copy-start(bf16[2560]{0:T(1024)(128)(2,1)} %pmax.31) | copy-start | bytes 15364
  140.8 3.1 %copy-start.11 = (f32[40]{0:T(128)S(1)}, f32[40]{0:T(128)}, u32[]{:S(2)}) copy-start(f32[40]{0:T(128)} %copy-done.10) | copy-start | bytes 484
  143.8 6.1 %copy-start.3 = (bf16[1,256,2560]{1,2,0:T(8,128)(2,1)S(1)}, bf16[1,256,2560]{1,2,0:T(8,128)(2,1)}, u32[]{:S(2)}) copy-start(bf16[1,256,2560]{1,2,0:T(8,128)(2,1)} %fusion.1) | copy-start | bytes 3932164
  143.8 6.1 %copy-start.5 = (f32[256,128]{0,1:T(8,128)S(1)}, f32[256,128]{0,1:T(8,128)}, u32[]{:S(2)}) copy-start(f32[256,128]{0,1:T(8,128)} %fusion.44) | copy-start | bytes 393220
  149.9 0.9 copy-start.6
  191.7 15.1 %all-to-all-start.1 = ((f32[16,5,256]{2,1,0:T(8,128)}), f32[16,5,256]{2,1,0:T(8,128)S(1)}, u32[]{:S(2)}, u32[]{:S(2)}) async-start(f32[16,5,256]{2,1,0:T(8,128)} %reshape.515), calls=%async_computation.1 | async-start | bytes 262144 | tf_op jit(solution)/shard_map/all_to_all | solution.py:63
Sparse Core Ops, SparseCore 0:
  14.4 45.7 all-gather.6
  63.7 67.7 all-gather.4
where the time goes:
time: 215 us; the launch traced here: 214 us
  blocking collectives  113 us (53%)
  waiting for transfers between devices  41.2 us (19%)
  other arithmetic  18.6 us (9%)
  between operations  15 us (7%)
  matrix products  10.2 us (5%)
  local copies, waits for them, and re-layouts  9.6 us (4%)
  starting transfers between devices  6.31 us (3%)
    pmax x4, blocking collectives, by_axis(): return functools.reduce(lax.pmax, axes, x)  51.5 us
    all_to_all x1, blocking collectives, sent_and_summed(): lax.all_to_all(tiles, axis, split_axis=0, concat_axis=0, tiled=True)  39.4 us
    all_gather x2, waiting for transfers between devices, prefix_by_axis(): lax.all_gather(part.astype(kind), axis)  33 us
    all_gather x1, blocking collectives, prefix_by_axis(): lax.all_gather(part.astype(kind), axis)  13.3 us
    unnamed x1, blocking collectives  9.26 us
    all_to_all x1, waiting for transfers between devices, summed_on_arrival(): tiles = lax.all_to_all(in_blocks(x, dim, length), axis, 0, 0, tiled=True)  8.13 us
    unnamed x35, local copies, waits for them, and re-layouts  6.82 us
    all_to_all x1, starting transfers between devices, summed_on_arrival(): tiles = lax.all_to_all(in_blocks(x, dim, length), axis, 0, 0, tiled=True)  6.23 us
  transfers between devices with their start and end apart: 3, of which 2 were waited for; matrix products, arithmetic and copies ran while one was open for 9% of the time, Pallas kernels for 0%

commit v1 on v0

v1 whole, which is shorter than its diff:
```python
import functools

import jax
import jax.numpy as jnp
from jax import lax
from jax.experimental import pallas as pl
from jax.experimental.pallas import tpu as pltpu
from jax.sharding import Mesh
from jax.sharding import PartitionSpec as P

SEQ = ("seq_0", "seq_1")
DP = ("dp_0", "dp_1")
SEQ_DP = SEQ + DP

epsilon = 1e-06
f32 = jnp.float32
bf16 = jnp.bfloat16


def silu_slope(value):
    sigma = jax.nn.sigmoid(value)
    return sigma * (1.0 + value * (1.0 - sigma))


def exchange(x, axes):
    return lax.all_to_all(x, axes, 0, 0, tiled=True)


def scan_body(bound_ref, got_ref, out_ref, peak_ref):
    blocks, _, states = got_ref.shape
    rows = out_ref.shape[1]
    first = lax.broadcasted_iota(jnp.int32, (rows, states), 0) < bound_ref[0]
    state = jnp.zeros((rows, states), f32)
    peak = jnp.zeros((1, states), f32)
    for k in reversed(range(blocks)):
        out_ref[k] = state.astype(bf16)
        extra = got_ref[k, rows : rows + 8, :].astype(f32)
        peak = jnp.maximum(peak, extra[4:5])
        total = jnp.where(first, extra[0:1] + extra[1:2], extra[2:3] + extra[3:4])
        state = got_ref[k, :rows, :].astype(f32) + total * state
    peak_ref[...] = peak


def scan_states(got, bound, rows):
    blocks, _, states = got.shape
    return pl.pallas_call(
        scan_body,
        in_specs=[
            pl.BlockSpec(memory_space=pltpu.SMEM),
            pl.BlockSpec(memory_space=pltpu.VMEM),
        ],
        out_specs=[
            pl.BlockSpec(memory_space=pltpu.VMEM),
            pl.BlockSpec(memory_space=pltpu.VMEM),
        ],
        out_shape=[
            jax.ShapeDtypeStruct((blocks, rows, states), bf16),
            jax.ShapeDtypeStruct((1, states), f32),
        ],
        name="scan_states",
    )(bound, got)


def on_device(
    layer_input, scan_input, scan_cotangent, step_size, log_decay, state_inputs, entry_state
):
    _, tokens, width = layer_input.shape
    heads = step_size.shape[1]
    channels = scan_input.shape[2]
    head_size = channels // heads
    states = state_inputs.shape[2] // 2
    n_y, n_x, n_z, n_c = (lax.axis_size(a) for a in SEQ_DP)
    n_seq = n_y * n_x
    n_dp = n_z * n_c
    slice_rows = channels // n_seq
    own_rows = width // (n_seq * n_dp)
    place = lax.axis_index("seq_0") * n_x + lax.axis_index("seq_1")

    rows_in = layer_input.reshape(tokens, width)
    inputs = scan_input.reshape(tokens, heads, head_size)
    cotangents = scan_cotangent.reshape(tokens, heads, head_size)
    steps = step_size.reshape(heads, tokens)
    cumulative = jnp.cumsum(log_decay.reshape(heads, tokens), axis=1)
    preact = state_inputs.reshape(tokens, 2 * states).astype(f32)
    activated = jax.nn.silu(preact).astype(bf16)
    writes = activated[:, :states]
    reads = activated[:, states:]

    weighted_cot = (cotangents * jnp.exp(cumulative).T[:, :, None]).astype(bf16)
    from_later = jnp.einsum("thp,tn->hpn", weighted_cot, reads, preferred_element_type=f32)
    totals = jnp.exp(cumulative[:, -1])
    local_peaks = jnp.max(jnp.abs(rows_in), axis=0)
    head0 = [slice_rows * d // head_size for d in range(n_seq)]
    head1 = [min(h + 1, heads - 1) for h in head0]
    ones = jnp.ones((1, states), f32)
    first_heads = jnp.stack([totals[h] for h in head0])
    second_heads = jnp.stack([totals[h] for h in head1])

    def two(values):
        high = lax.reduce_precision(values, 8, 7)
        return high[:, None, None] * ones, (values - high)[:, None, None] * ones

    peak_rows = jnp.pad(
        local_peaks.reshape(n_seq, slice_rows), ((0, 0), (0, states - slice_rows))
    )[:, None, :]
    extras = jnp.concatenate(
        [
            *two(first_heads),
            *two(second_heads),
            peak_rows.astype(f32),
            jnp.zeros((n_seq, 3, states), f32),
        ],
        axis=1,
    ).astype(bf16)
    sent = jnp.concatenate(
        [from_later.astype(bf16).reshape(n_seq, slice_rows, states), extras], axis=1
    )
    got = exchange(sent, SEQ)
    bound = (head_size - (place * slice_rows) % head_size).astype(jnp.int32).reshape(1)
    slices, seq_peaks = scan_states(got, bound, slice_rows)
    beyond = exchange(slices, SEQ).reshape(channels, states)

    later = lax.broadcasted_iota(jnp.int32, (tokens, tokens), 0) >= lax.broadcasted_iota(
        jnp.int32, (tokens, tokens), 1
    )
    scores = jnp.einsum("shp,thp->hst", cotangents, inputs, preferred_element_type=f32)
    spread = jnp.where(later[None], cumulative[:, :, None] - cumulative[:, None, :], 0.0)
    decay = jnp.where(later[None], jnp.exp(spread), 0.0)
    mixing = (scores * decay * steps[:, None, :]).astype(bf16)
    inner_write = jnp.einsum("hst,sn->tn", mixing, reads, preferred_element_type=f32)
    inner_read = jnp.einsum("hst,tn->sn", mixing, writes, preferred_element_type=f32)
    weighted_in = (
        inputs * (steps * jnp.exp(cumulative[:, -1:] - cumulative)).T[:, :, None]
    ).astype(bf16)
    carried_read = jnp.dot(
        weighted_cot.reshape(tokens, channels),
        entry_state.reshape(channels, states),
        preferred_element_type=f32,
    )
    slope = silu_slope(preact)
    grad_read = ((inner_read + carried_read) * slope[:, states:]).astype(bf16)

    carried_write = jnp.dot(
        weighted_in.reshape(tokens, channels), beyond, preferred_element_type=f32
    )
    grad_write = ((inner_write + carried_write) * slope[:, :states]).astype(bf16)
    state_input_grad = jnp.concatenate([grad_write, grad_read], axis=1)

    def product(grads):
        return lax.dot_general(
            rows_in, grads, (((0,), (0,)), ((), ())), preferred_element_type=f32
        ).astype(bf16)

    halves = jnp.stack([product(grad_write), product(grad_read)])
    half = exchange(halves, "dp_1").astype(f32).sum(axis=0).astype(bf16)
    by_x = half.reshape(n_y, n_x, slice_rows, states).transpose(1, 0, 2, 3)
    quarter = exchange(by_x, "seq_1").astype(f32).sum(axis=0).astype(bf16)
    pieces = quarter.reshape(n_y * n_dp, own_rows, states)
    peak_part = jnp.broadcast_to(seq_peaks.astype(bf16)[None], (n_y * n_dp, 1, states))
    pieces = jnp.concatenate(
        [pieces, peak_part, jnp.zeros((n_y * n_dp, 8 - own_rows - 1, states), bf16)], axis=1
    )
    arrived = exchange(pieces, ("seq_0",) + DP).astype(f32)
    arrived = arrived.reshape(n_y, n_z, n_c, 8, states)
    summed = arrived[..., :own_rows, :].sum(axis=(0, 1))
    own_y = lax.axis_index("seq_0")
    own_q = lax.axis_index("dp_0") * n_c + lax.axis_index("dp_1")
    peaks = lax.dynamic_index_in_dim(arrived[..., own_rows, :], own_y, 0, keepdims=False)
    peaks = jnp.max(peaks, axis=(0, 1))
    peaks = lax.dynamic_slice_in_dim(peaks, own_q * own_rows, own_rows)
    factor = 1.0 / (peaks + epsilon)
    weight_grad = summed.transpose(1, 0, 2).reshape(own_rows, n_c * states) * factor[:, None]
    return state_input_grad[None], weight_grad


def solution(mesh):
    torus = Mesh(mesh.devices.reshape(8, 4, 8, 2), SEQ_DP)
    placed = (
        P(DP, SEQ, None),
        P(DP, SEQ, None),
        P(DP, SEQ, None),
        P(DP, None, SEQ),
        P(DP, None, SEQ),
        P(DP, SEQ, None),
        P(DP, SEQ, None, None),
    )
    return jax.shard_map(
        on_device,
        mesh=torus,
        in_specs=placed,
        out_specs=(P(DP, SEQ, None), P(SEQ_DP, None)),
        check_vma=False,
    )
```

time: 215 us -> 135 us (0.63)
  blocking collectives: 113 us -> 8.02 us
  starting transfers between devices: 6.31 us -> 34.4 us
  between operations: 15 us -> 1.02 us
  other arithmetic: 18.6 us -> 8.59 us
  local copies, waits for them, and re-layouts: 9.6 us -> 18.9 us
  waiting for transfers between devices: 41.2 us -> 49.4 us
  Pallas kernels: 0 us -> 2.17 us
    pmax x4 -> x0, blocking collectives: 51.5 us -> none  [by_axis(): return functools.reduce(lax.pmax, axes, x)]
    all_to_all x1 -> x4, waiting for transfers between devices: 8.13 us -> 49.4 us  [exchange(): return lax.all_to_all(x, axes, 0, 0, tiled=True)]
    all_gather x2 -> x0, waiting for transfers between devices: 33 us -> none  [prefix_by_axis(): lax.all_gather(part.astype(kind), axis)]
    all_to_all x1, blocking collectives: 39.4 us -> 8.02 us  [exchange(): return lax.all_to_all(x, axes, 0, 0, tiled=True)]
    all_to_all x1 -> x4, starting transfers between devices: 6.23 us -> 34.4 us  [exchange(): return lax.all_to_all(x, axes, 0, 0, tiled=True)]
    all_gather x1 -> x0, blocking collectives: 13.3 us -> none  [prefix_by_axis(): lax.all_gather(part.astype(kind), axis)]
    convert_element_type x10 -> x2, other arithmetic: 14.2 us -> 2.09 us  [the longest x1 1.7 us: on_device(): weighted_cot = (cotangents * jnp.exp(cumulative).T[:, :, None]).astype(bf16)]
    unnamed x1 -> x0, blocking collectives: 9.26 us -> none
  transfers between devices with their start and end apart: 3 -> 4, of which waited for: 2 -> 4; matrix products, arithmetic and copies ran while one was open for 9% -> 10% of each run, Pallas kernels for 0% -> 0%
where the time goes in v1:
time: 135 us; the launch traced here: 134 us
  waiting for transfers between devices  49.4 us (37%)
  starting transfers between devices  34.4 us (25%)
  local copies, waits for them, and re-layouts  18.9 us (14%)
  matrix products  11.7 us (9%)
  other arithmetic  8.59 us (6%)
  blocking collectives  8.02 us (6%)
  Pallas kernels  2.17 us (2%)
    all_to_all x4, waiting for transfers between devices, exchange(): return lax.all_to_all(x, axes, 0, 0, tiled=True)  49.4 us
    all_to_all x4, starting transfers between devices, exchange(): return lax.all_to_all(x, axes, 0, 0, tiled=True)  34.4 us
    all_to_all x1, blocking collectives, exchange(): return lax.all_to_all(x, axes, 0, 0, tiled=True)  8.02 us
    unnamed x42, local copies, waits for them, and re-layouts  7.27 us
    dot_general x1, matrix products, on_device(): jnp.einsum('shp,thp->hst', cotangents, inputs, preferred_element_type=f32)  5.83 us
    concatenate x1, local copies, waits for them, and re-layouts, on_device(): jnp.concatenate([from_later.astype(bf16).reshape(n_seq, slice_rows, state...  5.2 us
    mul x4, local copies, waits for them, and re-layouts, two(): return (high[:, None, None] * ones, (values - high)[:, None, None] * ones)  2.81 us
  transfers between devices with their start and end apart: 4, of which 4 were waited for; matrix products, arithmetic and copies ran while one was open for 10% of the time, Pallas kernels for 0%

profile of v1, /device:TPU:1, one launch (start us, length us, event | category | flops | bytes accessed | tf_op | source)
XLA Modules:
  0.0 134.1 jit_solution(17696925311127580029)
XLA Ops:
  0.6 0.0 copy-start
  0.6 0.9 reshape.421
  1.5 0.6 reduce-window.6
  2.1 0.2 slice_reduce_fusion.1
  2.3 0.1 copy_bitcast_fusion
  2.4 0.0 copy-start.12
  2.4 0.0 copy-start.13
  2.5 0.0 copy-start.1
  2.5 2.5 %copy.34 = bf16[1,256,2560]{1,2,0:T(8,128)(2,1)} copy(bf16[1,256,2560]{2,1,0:T(8,128)(2,1)} %param.9) | data formatting | bytes 2621440 | tf_op args[2]
  5.0 0.1 copy.38
  5.1 0.8 fusion.15
  5.9 0.2 slice_reduce_fusion.2
  6.1 0.7 multiply_bitcast_fusion
  6.8 0.1 fusion.24
  6.9 0.1 stack.17
  7.0 0.6 fusion.22
  7.6 0.1 stack.18
  7.6 0.6 fusion.23
  8.2 0.2 fusion.4
  8.4 0.1 reshape.426
  8.5 0.0 copy-start.4
  8.5 1.7 %multiply_convert_fusion.1 = bf16[256,40,64]{0,2,1:T(8,128)(2,1)S(1)} fusion(bf16[256,40,64]{0,2,1:T(8,128)(2,1)} %bitcast.76, f32[256,40]{0,1:T(8,128)} %get-tuple-element.17), kind=kLoop, calls=%fused_computation.6 | loop fusion | flops 1966080 | bytes 2662400 | tf_op jit(solution)/shard_map/convert_element_type | solution.py:89
  10.3 1.4 %convolution_convert_fusion.2 = bf16[40,64,128]{2,1,0:T(8,128)(2,1)} fusion(bf16[256,40,64]{0,2,1:T(8,128)(2,1)S(1)} %multiply_convert_fusion.1, bf16[256,256]{0,1:T(8,128)(2,1)S(1)} %copy-done.4), kind=kOutput, calls=%fused_computation.8 | convolution fusion | flops 168099840 | bytes 2031616 | tf_op jit(solution)/shard_map/thp,tn->hpn/dot_general | solution.py:90
  11.7 0.7 mul.116
  12.4 0.7 mul.117
  13.1 0.7 mul.118
  13.8 0.7 mul.119
  14.5 0.6 broadcast_in_dim.49
  15.1 5.2 %concatenate.32 = bf16[32,88,128]{2,1,0:T(8,128)(2,1)} concatenate(bf16[32,80,128]{2,1,0:T(8,128)(2,1)} %bitcast.81, bf16[32,1,128]{2,1,0:T(2,128)(2,1)} %mul.116, bf16[32,1,128]{2,1,0:T(2,128)(2,1)} %mul.117, bf16[32,1,128]{2,1,0:T(2,128)(2,1)} %mul.118, bf16[32,1,128]{2,1,0:T(2,128)(2,1)} %mul.119, bf16[32,1,128]{2,1,0:T(2,128)(2,1)S(1)} %copy.40, ...), dimensions={1} | concatenate | bytes 1441792 | tf_op jit(solution)/shard_map/concatenate | solution.py:115
  20.3 10.6 %all-to-all-start = ((bf16[32,88,128]{2,1,0:T(8,128)(2,1)}), bf16[32,88,128]{2,1,0:T(8,128)(2,1)}, u32[]{:S(2)}, u32[]{:S(2)}) async-start(bf16[32,88,128]{2,1,0:T(8,128)(2,1)} %concatenate.32), calls=%async_computation | async-start | bytes 1441792 | tf_op jit(solution)/shard_map/all_to_all | solution.py:26
  30.9 2.4 %copy.35 = bf16[1,256,2560]{1,2,0:T(8,128)(2,1)} copy(bf16[1,256,2560]{2,1,0:T(8,128)(2,1)} %param.8) | data formatting | bytes 2621440 | tf_op args[1]
  33.4 0.6 iota_compare_fusion
  34.0 16.9 %all-to-all-done.got_ref = bf16[32,88,128]{2,1,0:T(8,128)(2,1)} async-done(((bf16[32,88,128]{2,1,0:T(8,128)(2,1)}), bf16[32,88,128]{2,1,0:T(8,128)(2,1)}, u32[]{:S(2)}, u32[]{:S(2)}) %all-to-all-start) | async-done | bytes 720928 | tf_op jit(solution)/shard_map/all_to_all | solution.py:26
  50.9 2.2 %scan_states.1 = (bf16[32,80,128]{2,1,0:T(8,128)(2,1)}, f32[1,128]{1,0:T(1,128)}) custom-call(s32[1]{0:T(128)} %bitcast.7.bound_ref, bf16[32,88,128]{2,1,0:T(8,128)(2,1)} %all-to-all-done.got_ref), custom_call_target="tpu_custom_call" | custom-call | tf_op jit(solution)/shard_map/scan_states/pallas_call | solution.py:46
  53.1 5.6 %all-to-all-start.1 = ((bf16[32,80,128]{2,1,0:T(8,128)(2,1)}), bf16[32,80,128]{2,1,0:T(8,128)(2,1)}, u32[]{:S(2)}, u32[]{:S(2)}) async-start(bf16[32,80,128]{2,1,0:T(8,128)(2,1)} %get-tuple-element.4), calls=%async_computation.1 | async-start | bytes 1310720 | tf_op jit(solution)/shard_map/all_to_all | solution.py:26
  58.7 5.8 %convert_reduce_fusion = bf16[256,256]{1,0:T(8,128)(2,1)S(1)} fusion(f32[40,256]{1,0:T(8,128)} %bitcast.83, f32[40,256]{1,0:T(8,128)} %copy-done.12, pred[256,256]{1,0:T(8,128)(4,1)} %iota_compare_fusion, bf16[256,40,64]{0,2,1:T(8,128)(2,1)} %bitcast.77, bf16[256,40,64]{0,2,1:T(8,128)(2,1)} %bitcast.78), kind=kOutput, calls=%fused_computation | convolution fusion | flops 356450304 | bytes 2899968 | tf_op jit(solution)/shard_map/shp,thp->hst/dot_general | solution.py:126
  64.6 0.2 fusion.16
  64.8 0.4 fusion.7
  65.2 1.2 fusion.1
  66.4 0.8 fusion.20
  67.3 0.4 multiply_convert_fusion.2
  67.7 8.8 %all-to-all-done.1 = bf16[32,80,128]{2,1,0:T(8,128)(2,1)} async-done(((bf16[32,80,128]{2,1,0:T(8,128)(2,1)}), bf16[32,80,128]{2,1,0:T(8,128)(2,1)}, u32[]{:S(2)}, u32[]{:S(2)}) %all-to-all-start.1) | async-done | bytes 655392 | tf_op jit(solution)/shard_map/all_to_all | solution.py:26
  76.5 1.5 %fusion.8 = bf16[256,128]{0,1:T(8,128)(2,1)S(1)} fusion(f32[256,128]{0,1:T(8,128)} %fusion.20, bf16[256,2560]{0,1:T(8,128)(2,1)S(1)} %bitcast.80, bf16[2560,128]{1,0:T(8,128)(2,1)} %bitcast.13, f32[256,256]{0,1:T(8,128)S(1)} %get-tuple-element.14), kind=kOutput, calls=%fused_computation.19 | convolution fusion | flops 167870464 | bytes 2293760 | tf_op jit(solution)/shard_map/dot_general | solution.py:143
  78.0 0.6 copy-done.8
  78.6 0.3 fusion
  79.0 0.7 copy-done.3
  79.7 0.1 pad_maximum_fusion
  79.8 8.0 %all_to_all.25 = bf16[2,2560,128]{1,2,0:T(8,128)(2,1)S(1)} all-to-all(bf16[2,2560,128]{1,2,0:T(8,128)(2,1)S(1)} %pad_maximum_fusion), channel_id=1, replica_groups=mesh['seq_0'=8,'seq_1'=4,'dp_0'=8,'dp_1'=2] {'dp_1'}, dimensions={0} | all-to-all | bytes 2621440 | tf_op jit(solution)/shard_map/all_to_all | solution.py:26
  87.9 0.3 reduce_sum.47
  88.2 0.3 copy.41
  88.5 0.9 copy.42
  89.4 3.5 %all-to-all-start.3 = ((bf16[4,8,80,128]{3,2,1,0:T(8,128)(2,1)}), bf16[4,8,80,128]{3,2,1,0:T(8,128)(2,1)S(1)}, u32[]{:S(2)}, u32[]{:S(2)}) async-start(bf16[4,8,80,128]{3,2,1,0:T(8,128)(2,1)} %copy.42), calls=%async_computation.3 | async-start | bytes 1310720 | tf_op jit(solution)/shard_map/all_to_all | solution.py:26
  92.9 0.1 pad.7.clone
  93.0 10.2 %all-to-all-done.3 = bf16[4,8,80,128]{3,2,1,0:T(8,128)(2,1)S(1)} async-done(((bf16[4,8,80,128]{3,2,1,0:T(8,128)(2,1)}), bf16[4,8,80,128]{3,2,1,0:T(8,128)(2,1)S(1)}, u32[]{:S(2)}, u32[]{:S(2)}) %all-to-all-start.3) | async-done | bytes 655392 | tf_op jit(solution)/shard_map/all_to_all | solution.py:26
  103.2 0.1 reduce_sum.48
  103.3 0.1 reshape.430
  103.4 0.9 maximum_maximum_fusion
  104.3 14.6 %all-to-all-start.4 = ((bf16[128,8,128]{2,1,0:T(8,128)(2,1)}), bf16[128,8,128]{2,1,0:T(8,128)(2,1)S(1)}, u32[]{:S(2)}, u32[]{:S(2)}) async-start(bf16[128,8,128]{2,1,0:T(8,128)(2,1)} %maximum_maximum_fusion), calls=%async_computation.4 | async-start | bytes 524288 | tf_op jit(solution)/shard_map/all_to_all | solution.py:26
  119.0 0.8 copy.43
  119.7 13.4 %all-to-all-done.4 = bf16[128,8,128]{2,1,0:T(8,128)(2,1)S(1)} async-done(((bf16[128,8,128]{2,1,0:T(8,128)(2,1)}), bf16[128,8,128]{2,1,0:T(8,128)(2,1)S(1)}, u32[]{:S(2)}, u32[]{:S(2)}) %all-to-all-start.4) | async-done | bytes 262176 | tf_op jit(solution)/shard_map/all_to_all | solution.py:26
  133.2 0.1 slice_reduce_fusion
  133.2 0.1 slice.172
  133.3 0.1 add_divide_fusion
  133.4 0.7 bitcast_multiply_fusion
  (43 shorter events, 0.3 us)
Async XLA Ops:
  0.6 64.2 %copy-start = (bf16[1,1,2560,128]{3,2,1,0:T(8,128)(2,1)S(1)}, bf16[1,1,2560,128]{3,2,1,0:T(8,128)(2,1)}, u32[]{:S(2)}) copy-start(bf16[1,1,2560,128]{3,2,1,0:T(8,128)(2,1)} %param.13) | copy-start | bytes 1966084
  2.4 3.5 %copy-start.12 = (f32[40,256]{1,0:T(8,128)}, f32[40,256]{1,0:T(8,128)S(1)}, u32[]{:S(2)}) copy-start(f32[40,256]{1,0:T(8,128)S(1)} %copy_bitcast_fusion) | copy-start | bytes 122884
  2.4 2.6 %copy-start.11 = (bf16[1,256,256]{2,1,0:T(8,128)(2,1)S(1)}, bf16[1,256,256]{2,1,0:T(8,128)(2,1)}, u32[]{:S(2)}) copy-start(bf16[1,256,256]{2,1,0:T(8,128)(2,1)} %param.12) | copy-start | bytes 393220
  2.4 3.6 %copy-start.13 = (f32[1,40,256]{2,1,0:T(8,128)S(1)}, f32[1,40,256]{2,1,0:T(8,128)}, u32[]{:S(2)}) copy-start(f32[1,40,256]{2,1,0:T(8,128)} %param.10) | copy-start | bytes 122884
  2.5 5.8 %copy-start.1 = (bf16[1,256,2560]{2,1,0:T(8,128)(2,1)S(1)}, bf16[1,256,2560]{2,1,0:T(8,128)(2,1)}, u32[]{:S(2)}) copy-start(bf16[1,256,2560]{2,1,0:T(8,128)(2,1)} %param.7) | copy-start | bytes 3932164
  8.5 1.8 %copy-start.4 = (bf16[256,256]{0,1:T(8,128)(2,1)S(1)}, bf16[256,256]{0,1:T(8,128)(2,1)}, u32[]{:S(2)}) copy-start(bf16[256,256]{0,1:T(8,128)(2,1)} %get-tuple-element.15) | copy-start | bytes 393220
  10.2 1.4 %copy-start.15 = (bf16[32]{0:T(256)(128)(2,1)S(1)}, bf16[32]{0:T(256)(128)(2,1)}, u32[]{:S(2)}) copy-start(bf16[32]{0:T(256)(128)(2,1)} %get-tuple-element.37) | copy-start | bytes 196
  10.3 2.1 %copy-start.14 = (bf16[32]{0:T(256)(128)(2,1)S(1)}, bf16[32]{0:T(256)(128)(2,1)}, u32[]{:S(2)}) copy-start(bf16[32]{0:T(256)(128)(2,1)} %get-tuple-element.36) | copy-start | bytes 196
  10.3 2.8 %copy-start.17 = (bf16[32]{0:T(256)(128)(2,1)S(1)}, bf16[32]{0:T(256)(128)(2,1)}, u32[]{:S(2)}) copy-start(bf16[32]{0:T(256)(128)(2,1)} %get-tuple-element.19) | copy-start | bytes 196
  10.3 3.5 %copy-start.16 = (bf16[32]{0:T(256)(128)(2,1)S(1)}, bf16[32]{0:T(256)(128)(2,1)}, u32[]{:S(2)}) copy-start(bf16[32]{0:T(256)(128)(2,1)} %get-tuple-element.18) | copy-start | bytes 196
  20.3 30.6 %all-to-all-start = ((bf16[32,88,128]{2,1,0:T(8,128)(2,1)}), bf16[32,88,128]{2,1,0:T(8,128)(2,1)}, u32[]{:S(2)}, u32[]{:S(2)}) async-start(bf16[32,88,128]{2,1,0:T(8,128)(2,1)} %concatenate.32), calls=%async_computation | async-start | bytes 1441792 | tf_op jit(solution)/shard_map/all_to_all | solution.py:26
  53.1 23.4 %all-to-all-start.1 = ((bf16[32,80,128]{2,1,0:T(8,128)(2,1)}), bf16[32,80,128]{2,1,0:T(8,128)(2,1)}, u32[]{:S(2)}, u32[]{:S(2)}) async-start(bf16[32,80,128]{2,1,0:T(8,128)(2,1)} %get-tuple-element.4), calls=%async_computation.1 | async-start | bytes 1310720 | tf_op jit(solution)/shard_map/all_to_all | solution.py:26
  58.7 5.9 %copy-start.5 = (bf16[256,256]{0,1:T(8,128)(2,1)S(1)}, bf16[256,256]{0,1:T(8,128)(2,1)}, u32[]{:S(2)}) copy-start(bf16[256,256]{0,1:T(8,128)(2,1)} %get-tuple-element.15) | copy-start | bytes 393220
  65.2 2.0 %copy-start.6 = (bf16[256,128]{0,1:T(8,128)(2,1)}, bf16[256,128]{0,1:T(8,128)(2,1)S(1)}, u32[]{:S(2)}) copy-start(bf16[256,128]{0,1:T(8,128)(2,1)S(1)} %fusion.7) | copy-start | bytes 196612
  65.2 2.0 %copy-start.2 = (bf16[1,256,2560]{1,2,0:T(8,128)(2,1)S(1)}, bf16[1,256,2560]{1,2,0:T(8,128)(2,1)}, u32[]{:S(2)}) copy-start(bf16[1,256,2560]{1,2,0:T(8,128)(2,1)} %copy.35) | copy-start | bytes 3932164
  65.2 2.0 %copy-start.10 = (f32[256,40]{0,1:T(8,128)S(1)}, f32[256,40]{0,1:T(8,128)}, u32[]{:S(2)}) copy-start(f32[256,40]{0,1:T(8,128)} %get-tuple-element.16) | copy-start | bytes 122884
  78.0 0.6 copy-start.8
  78.6 1.1 copy-start.3
  88.5 4.5 %copy-start.18 = (f32[1,128]{1,0:T(1,128)S(1)}, f32[1,128]{1,0:T(1,128)}, u32[]{:S(2)}) copy-start(f32[1,128]{1,0:T(1,128)} %get-tuple-element.5) | copy-start | bytes 1540
  89.4 13.8 %all-to-all-start.3 = ((bf16[4,8,80,128]{3,2,1,0:T(8,128)(2,1)}), bf16[4,8,80,128]{3,2,1,0:T(8,128)(2,1)S(1)}, u32[]{:S(2)}, u32[]{:S(2)}) async-start(bf16[4,8,80,128]{3,2,1,0:T(8,128)(2,1)} %copy.42), calls=%async_computation.3 | async-start | bytes 1310720 | tf_op jit(solution)/shard_map/all_to_all | solution.py:26
  92.9 26.0 %copy-start.7 = (bf16[256,128]{0,1:T(8,128)(2,1)S(1)}, bf16[256,128]{0,1:T(8,128)(2,1)}, u32[]{:S(2)}) copy-start(bf16[256,128]{0,1:T(8,128)(2,1)} %copy-done.6) | copy-start | bytes 196612
  92.9 26.0 %copy-start.9 = (bf16[256,128]{0,1:T(8,128)(2,1)S(1)}, bf16[256,128]{0,1:T(8,128)(2,1)}, u32[]{:S(2)}) copy-start(bf16[256,128]{0,1:T(8,128)(2,1)} %copy-done.8) | copy-start | bytes 196612
  104.3 28.8 %all-to-all-start.4 = ((bf16[128,8,128]{2,1,0:T(8,128)(2,1)}), bf16[128,8,128]{2,1,0:T(8,128)(2,1)S(1)}, u32[]{:S(2)}, u32[]{:S(2)}) async-start(bf16[128,8,128]{2,1,0:T(8,128)(2,1)} %maximum_maximum_fusion), calls=%async_computation.4 | async-start | bytes 524288 | tf_op jit(solution)/shard_map/all_to_all | solution.py:26

commit v2 on v1

v2 whole, which is shorter than its diff:
```python
import functools

import jax
import jax.numpy as jnp
from jax import lax
from jax.experimental import pallas as pl
from jax.experimental.pallas import tpu as pltpu
from jax.sharding import Mesh
from jax.sharding import PartitionSpec as P

SEQ = ("seq_0", "seq_1")
DP = ("dp_0", "dp_1")
SEQ_DP = SEQ + DP

epsilon = 1e-06
f32 = jnp.float32
bf16 = jnp.bfloat16


def silu_slope(value):
    sigma = jax.nn.sigmoid(value)
    return sigma * (1.0 + value * (1.0 - sigma))


def exchange(x, axes):
    return lax.all_to_all(x, axes, 0, 0, tiled=True)


def scan_body(bound_ref, got_ref, out_ref, peak_ref):
    blocks, _, states = got_ref.shape
    rows = out_ref.shape[1]
    first = lax.broadcasted_iota(jnp.int32, (rows, states), 0) < bound_ref[0]
    state = jnp.zeros((rows, states), f32)
    peak = jnp.zeros((1, states), f32)
    for k in reversed(range(blocks)):
        out_ref[k] = state.astype(bf16)
        extra = got_ref[k, rows : rows + 8, :].astype(f32)
        peak = jnp.maximum(peak, extra[4:5])
        total = jnp.where(first, extra[0:1] + extra[1:2], extra[2:3] + extra[3:4])
        state = got_ref[k, :rows, :].astype(f32) + total * state
    peak_ref[...] = peak


def scan_states(got, bound, rows):
    blocks, _, states = got.shape
    return pl.pallas_call(
        scan_body,
        in_specs=[
            pl.BlockSpec(memory_space=pltpu.SMEM),
            pl.BlockSpec(memory_space=pltpu.VMEM),
        ],
        out_specs=[
            pl.BlockSpec(memory_space=pltpu.VMEM),
            pl.BlockSpec(memory_space=pltpu.VMEM),
        ],
        out_shape=[
            jax.ShapeDtypeStruct((blocks, rows, states), bf16),
            jax.ShapeDtypeStruct((1, states), f32),
        ],
        name="scan_states",
    )(bound, got)


def summary_body(in_ref, cot_ref, decay_ref, pre_ref, sent_ref, cum_ref, reads_ref, spread_ref):
    step = pl.program_id(0)
    heads, tokens = decay_ref.shape
    chunks, rows_all, states = sent_ref.shape
    span = cot_ref.shape[1]
    rows = span // chunks
    head_size = span * pl.num_programs(0) // heads

    @pl.when(step == 0)
    def _():
        below = lax.broadcasted_iota(jnp.int32, (tokens, tokens), 0)
        above = lax.broadcasted_iota(jnp.int32, (tokens, tokens), 1)
        cum = jnp.dot(
            decay_ref[...],
            (below <= above).astype(f32),
            precision=lax.Precision.HIGHEST,
            preferred_element_type=f32,
        )
        cum_ref[...] = cum
        grown = jnp.exp(cum)
        high = grown.astype(bf16)
        spread_ref[0] = high
        spread_ref[1] = (grown - high.astype(f32)).astype(bf16)
        value = pre_ref[:, states:].astype(f32)
        reads_ref[...] = (value / (1.0 + jnp.exp(-value))).astype(bf16)

    owner = lax.broadcasted_iota(jnp.int32, (heads, span), 0) * head_size - step * span
    lane = lax.broadcasted_iota(jnp.int32, (heads, span), 1)
    hot = jnp.where((lane >= owner) & (lane < owner + head_size), 1.0, 0.0).astype(bf16)
    both = (((0,), (0,)), ((), ()))
    scale = lax.dot_general(spread_ref[0], hot, both, preferred_element_type=f32)
    scale += lax.dot_general(spread_ref[1], hot, both, preferred_element_type=f32)
    weighted = (cot_ref[...].astype(f32) * scale).astype(bf16)
    later = lax.dot_general(weighted, reads_ref[...], both, preferred_element_type=f32)
    later = later.astype(bf16)
    peak = jnp.max(jnp.abs(in_ref[...]).astype(f32), axis=0, keepdims=True)
    peak = jnp.broadcast_to(peak, (8, span))
    last = scale[tokens - 1 :, :]
    row = lax.broadcasted_iota(jnp.int32, (rows_all - rows, states), 0)
    for d in range(chunks):
        sent_ref[d, :rows, :] = later[d * rows : (d + 1) * rows]
        first = jnp.broadcast_to(last[:, d * rows : d * rows + 1], (8, states))
        second = jnp.broadcast_to(last[:, (d + 1) * rows - 1 : (d + 1) * rows], (8, states))
        first_high = first.astype(bf16).astype(f32)
        second_high = second.astype(bf16).astype(f32)
        turned = pltpu.roll(peak, span - d * rows, 1) if d else peak
        extra = jnp.where(row == 0, first_high, first - first_high)
        extra = jnp.where(row == 2, second_high, extra)
        extra = jnp.where(row == 3, second - second_high, extra)
        extra = jnp.where(row >= 4, turned[:, :states], extra)
        sent_ref[d, rows:, :] = extra.astype(bf16)


def summarize(rows_in, cots, decays, pre, n_seq, head_states):
    tokens, channels = cots.shape
    heads = decays.shape[0]
    states = head_states
    grid = 4
    span = channels // grid
    rows = channels // n_seq
    return pl.pallas_call(
        summary_body,
        grid=(grid,),
        in_specs=[
            pl.BlockSpec((tokens, span), lambda i: (0, i)),
            pl.BlockSpec((tokens, span), lambda i: (0, i)),
            pl.BlockSpec((heads, tokens), lambda i: (0, 0)),
            pl.BlockSpec((tokens, 2 * states), lambda i: (0, 0)),
        ],
        out_specs=[
            pl.BlockSpec((n_seq // grid, rows + 8, states), lambda i: (i, 0, 0)),
            pl.BlockSpec((heads, tokens), lambda i: (0, 0)),
        ],
        out_shape=[
            jax.ShapeDtypeStruct((n_seq, rows + 8, states), bf16),
            jax.ShapeDtypeStruct((heads, tokens), f32),
        ],
        scratch_shapes=[
            pltpu.VMEM((tokens, states), bf16),
            pltpu.VMEM((2, heads, tokens), bf16),
        ],
        name="summarize",
    )(rows_in, cots, decays, pre)


def finish_body(win_ref, beyond_ref, inner_ref, slope_ref, read_ref, turned_ref, peak_ref, grad_ref, prod_ref):
    states = beyond_ref.shape[1]
    half = turned_ref.shape[0] // 2
    carried = jnp.dot(win_ref[...], beyond_ref[...], preferred_element_type=f32)
    grad_ref[:, :states] = ((inner_ref[...] + carried) * slope_ref[...]).astype(bf16)
    grad_ref[:, states:] = read_ref[...]
    for c in range(2):
        prod_ref[c, :half, :] = jnp.dot(
            turned_ref[c * half : (c + 1) * half, :], grad_ref[...], preferred_element_type=f32
        ).astype(bf16)
        prod_ref[c, half:, :states] = jnp.broadcast_to(peak_ref[...], (8, states)).astype(bf16)
        prod_ref[c, half:, states:] = jnp.zeros((8, states), bf16)


def finish(weighted_in, beyond, inner, slope, grad_read, turned, peak):
    tokens = weighted_in.shape[0]
    width = turned.shape[0]
    states = beyond.shape[1]
    return pl.pallas_call(
        finish_body,
        out_shape=[
            jax.ShapeDtypeStruct((tokens, 2 * states), bf16),
            jax.ShapeDtypeStruct((2, width // 2 + 8, 2 * states), bf16),
        ],
        name="finish",
    )(weighted_in, beyond, inner, slope, grad_read, turned, peak)


def pair_body(got_ref, sum_ref, peak_ref):
    half = sum_ref.shape[0]
    sum_ref[...] = (got_ref[0, :half].astype(f32) + got_ref[1, :half].astype(f32)).astype(bf16)
    peak_ref[...] = jnp.maximum(got_ref[0, half:].astype(f32), got_ref[1, half:].astype(f32))


def add_pair(got):
    _, rows, cols = got.shape
    return pl.pallas_call(
        pair_body,
        out_shape=[
            jax.ShapeDtypeStruct((rows - 8, cols), bf16),
            jax.ShapeDtypeStruct((8, cols), f32),
        ],
        name="add_pair",
    )(got)


def split_body(got_ref, peak_ref, out_ref, sum_ref):
    count, rows, cols = got_ref.shape
    pieces = out_ref.shape[0]
    own = rows // pieces
    total = got_ref[0].astype(f32)
    for k in range(1, count):
        total += got_ref[k].astype(f32)
    sum_ref[:rows] = total
    sum_ref[rows:] = jnp.zeros((8, cols), f32)
    row = lax.broadcasted_iota(jnp.int32, (8, cols), 0)
    peak = peak_ref[...]
    for q in range(pieces):
        out_ref[q] = jnp.where(row < own, sum_ref[own * q : own * q + 8, :], peak).astype(bf16)


def add_split(got, peak, pieces):
    _, rows, cols = got.shape
    return pl.pallas_call(
        split_body,
        out_shape=jax.ShapeDtypeStruct((pieces, 8, cols), bf16),
        scratch_shapes=[pltpu.VMEM((rows + 8, cols), f32)],
        name="add_split",
    )(got, peak)


def close_body(place_ref, got_ref, out_ref):
    count, rows, cols = got_ref.shape
    own = out_ref.shape[0]
    total = got_ref[0].astype(f32)
    for k in range(1, count):
        total += got_ref[k].astype(f32)
    peak = jnp.zeros((rows, cols), f32)
    for z in range(8):
        peak = jnp.maximum(peak, got_ref[place_ref[0] * 8 + z].astype(f32))
    lane = lax.broadcasted_iota(jnp.int32, (rows, cols), 1)
    row = lax.broadcasted_iota(jnp.int32, (rows, cols), 0)
    line = jnp.broadcast_to(peak[own : own + 1, :], (rows, cols))
    column = jnp.sum(jnp.where(lane == place_ref[1] * own + row, line, 0.0), axis=1, keepdims=True)
    out_ref[...] = (total * (1.0 / (column + epsilon)))[:own]


def close(got, place, own):
    cols = got.shape[2]
    return pl.pallas_call(
        close_body,
        in_specs=[
            pl.BlockSpec(memory_space=pltpu.SMEM),
            pl.BlockSpec(memory_space=pltpu.VMEM),
        ],
        out_shape=jax.ShapeDtypeStruct((own, cols), f32),
        name="close",
    )(place, got)


def on_device(
    layer_input, scan_input, scan_cotangent, step_size, log_decay, state_inputs, entry_state
):
    _, tokens, width = layer_input.shape
    heads = step_size.shape[1]
    channels = scan_input.shape[2]
    head_size = channels // heads
    states = state_inputs.shape[2] // 2
    n_y, n_x, n_z, n_c = (lax.axis_size(a) for a in SEQ_DP)
    n_seq = n_y * n_x
    slice_rows = channels // n_seq
    own_rows = width // (n_seq * n_z * n_c)
    y, x, z, c = (lax.axis_index(a) for a in SEQ_DP)

    rows_in = layer_input.reshape(tokens, width)
    flat_cot = scan_cotangent.reshape(tokens, channels)
    flat_pre = state_inputs.reshape(tokens, 2 * states)
    sent, cumulative = summarize(
        rows_in, flat_cot, log_decay.reshape(heads, tokens), flat_pre, n_seq, states
    )
    got = exchange(sent, SEQ)
    bound = head_size - ((y * n_x + x) * slice_rows) % head_size
    slices, seq_peaks = scan_states(got, bound.astype(jnp.int32).reshape(1), slice_rows)
    beyond = exchange(slices, SEQ).reshape(channels, states)

    inputs = scan_input.reshape(tokens, heads, head_size)
    cotangents = scan_cotangent.reshape(tokens, heads, head_size)
    steps = step_size.reshape(heads, tokens)
    preact = flat_pre.astype(f32)
    activated = jax.nn.silu(preact).astype(bf16)
    writes = activated[:, :states]
    reads = activated[:, states:]
    weighted_cot = (cotangents * jnp.exp(cumulative).T[:, :, None]).astype(bf16)
    later = lax.broadcasted_iota(jnp.int32, (tokens, tokens), 0) >= lax.broadcasted_iota(
        jnp.int32, (tokens, tokens), 1
    )
    scores = jnp.einsum("shp,thp->hst", cotangents, inputs, preferred_element_type=f32)
    spread = jnp.where(later[None], cumulative[:, :, None] - cumulative[:, None, :], 0.0)
    decay = jnp.where(later[None], jnp.exp(spread), 0.0)
    mixing = (scores * decay * steps[:, None, :]).astype(bf16)
    inner_write = jnp.einsum("hst,sn->tn", mixing, reads, preferred_element_type=f32)
    inner_read = jnp.einsum("hst,tn->sn", mixing, writes, preferred_element_type=f32)
    weighted_in = (
        inputs * (steps * jnp.exp(cumulative[:, -1:] - cumulative)).T[:, :, None]
    ).astype(bf16)
    carried_read = jnp.dot(
        weighted_cot.reshape(tokens, channels),
        entry_state.reshape(channels, states),
        preferred_element_type=f32,
    )
    slope = silu_slope(preact)
    grad_read = ((inner_read + carried_read) * slope[:, states:]).astype(bf16)
    turned = rows_in.reshape(tokens, n_y, n_x, n_z, n_c, own_rows)
    turned = turned.transpose(4, 2, 1, 3, 5, 0).reshape(width, tokens)

    state_input_grad, product = finish(
        weighted_in.reshape(tokens, channels),
        beyond,
        inner_write,
        slope[:, :states],
        grad_read,
        turned,
        seq_peaks,
    )
    half, peaks = add_pair(exchange(product, "dp_1"))
    quarter = exchange(half.reshape(n_x, width // (n_x * n_c), 2 * states), "seq_1")
    pieces = add_split(quarter, peaks, n_y * n_z)
    arrived = exchange(pieces, ("seq_0", "dp_0"))
    where = jnp.stack([y, z * n_c + c]).astype(jnp.int32)
    return state_input_grad[None], close(arrived, where, own_rows)


def solution(mesh):
    torus = Mesh(mesh.devices.reshape(8, 4, 8, 2), SEQ_DP)
    placed = (
        P(DP, SEQ, None),
        P(DP, SEQ, None),
        P(DP, SEQ, None),
        P(DP, None, SEQ),
        P(DP, None, SEQ),
        P(DP, SEQ, None),
        P(DP, SEQ, None, None),
    )
    return jax.shard_map(
        on_device,
        mesh=torus,
        in_specs=placed,
        out_specs=(P(DP, SEQ, None), P(SEQ_DP, None)),
        check_vma=False,
    )
```

time: 135 us -> 140 us (1.037)
  waiting for transfers between devices: 49.4 us -> 24 us
  blocking collectives: 8.02 us -> 24.4 us
  Pallas kernels: 2.17 us -> 17.9 us
  other arithmetic: 8.59 us -> 5.95 us
  local copies, waits for them, and re-layouts: 18.9 us -> 21 us
  starting transfers between devices: 34.4 us -> 32.8 us
    all_to_all x4 -> x3, waiting for transfers between devices: 49.4 us -> 24 us  [exchange(): return lax.all_to_all(x, axes, 0, 0, tiled=True)]
    all_to_all x1 -> x2, blocking collectives: 8.02 us -> 24.4 us  [exchange(): return lax.all_to_all(x, axes, 0, 0, tiled=True)]
    pallas_call x0 -> x5, Pallas kernels: none -> 15.7 us  [the longest x1 5.7 us: summarize(): pl.pallas_call(summary_body, grid=(grid,), in_specs=[pl.BlockSpec((tokens...]
    concatenate x2 -> x0, local copies, waits for them, and re-layouts: 5.28 us -> none  [the longest x1 5.2 us: on_device(): jnp.concatenate([from_later.astype(bf16).reshape(n_seq, slice_rows, state...]
    dot_general x4 -> x0, matrix products: 4.42 us -> none  [the longest x2 1.52 us: product(): lax.dot_general(rows_in, grads, (((0,), (0,)), ((), ())), preferred_eleme...]
    another operation x3 -> x1, local copies, waits for them, and re-layouts: 0.17 us -> 3.61 us  [on_device(): turned = rows_in.reshape(tokens, n_y, n_x, n_z, n_c, own_rows)]
    reshape x4 -> x1, local copies, waits for them, and re-layouts: 1.03 us -> 3.66 us  [on_device(): turned = turned.transpose(4, 2, 1, 3, 5, 0).reshape(width, tokens)]
    transpose x1, local copies, waits for them, and re-layouts: 0.88 us -> 3.19 us  [on_device(): turned = turned.transpose(4, 2, 1, 3, 5, 0).reshape(width, tokens)]
  transfers between devices with their start and end apart: 4 -> 3, of which waited for: 4 -> 2; matrix products, arithmetic and copies ran while one was open for 10% -> 27% of each run, Pallas kernels for 0% -> 0%
where the time goes in v2:
time: 140 us; the launch traced here: 138 us
  starting transfers between devices  32.8 us (23%)
  blocking collectives  24.4 us (17%)
  waiting for transfers between devices  24 us (17%)
  local copies, waits for them, and re-layouts  21 us (15%)
  Pallas kernels  17.9 us (13%)
  matrix products  11 us (8%)
  other arithmetic  5.95 us (4%)
    all_to_all x3, starting transfers between devices, exchange(): return lax.all_to_all(x, axes, 0, 0, tiled=True)  32.8 us
    all_to_all x2, blocking collectives, exchange(): return lax.all_to_all(x, axes, 0, 0, tiled=True)  24.4 us
    all_to_all x3, waiting for transfers between devices, exchange(): return lax.all_to_all(x, axes, 0, 0, tiled=True)  24 us
    dot_general x1, matrix products, on_device(): jnp.einsum('shp,thp->hst', cotangents, inputs, preferred_element_type=f32)  5.82 us
    pallas_call x1, Pallas kernels, summarize(): pl.pallas_call(summary_body, grid=(grid,), in_specs=[pl.BlockSpec((tokens...  5.7 us
    unnamed x27, local copies, waits for them, and re-layouts  5.1 us
    pallas_call x1, Pallas kernels, finish(): pl.pallas_call(finish_body, out_shape=[jax.ShapeDtypeStruct((tokens, 2 *...  4.05 us
    mul x2, local copies, waits for them, and re-layouts, on_device(): inputs * (steps * jnp.exp(cumulative[:, -1:] - cumulative)).T[:, :, None]  3.85 us
  transfers between devices with their start and end apart: 3, of which 2 were waited for; matrix products, arithmetic and copies ran while one was open for 27% of the time, Pallas kernels for 0%

profile of v2, /device:TPU:1, one launch (start us, length us, event | category | flops | bytes accessed | tf_op | source)
XLA Modules:
  0.0 137.9 jit_solution(110507546401632241)
XLA Ops:
  0.6 0.0 copy-start
  0.6 0.0 copy-start.3
  0.7 5.7 %summarize.1 = (bf16[32,88,128]{2,1,0:T(8,128)(2,1)}, f32[40,256]{1,0:T(8,128)}) custom-call(bf16[256,2560]{1,0:T(8,128)(2,1)} %bitcast.39, bf16[256,2560]{1,0:T(8,128)(2,1)} %bitcast.38, f32[40,256]{1,0:T(8,128)} %bitcast.47, bf16[256,256]{1,0:T(8,128)(2,1)} %bitcast.45), custom_call_target="tpu_custom_call" | custom-call | tf_op jit(solution)/shard_map/summarize/pallas_call | solution.py:124
  6.4 0.0 copy-start.4
  6.4 10.7 %all-to-all-start = ((bf16[32,88,128]{2,1,0:T(8,128)(2,1)}), bf16[32,88,128]{2,1,0:T(8,128)(2,1)}, u32[]{:S(2)}, u32[]{:S(2)}) async-start(bf16[32,88,128]{2,1,0:T(8,128)(2,1)} %get-tuple-element.11), calls=%async_computation | async-start | bytes 1441792 | tf_op jit(solution)/shard_map/all_to_all | solution.py:26
  17.1 0.0 copy-done.3
  17.1 1.4 %copy.15 = bf16[1,256,2560]{1,2,0:T(8,128)(2,1)} copy(bf16[1,256,2560]{2,1,0:T(8,128)(2,1)S(1)} %copy-done.3) | data formatting | bytes 2621440 | tf_op args[2]
  18.6 0.0 copy-start.1
  18.6 1.8 %fusion.9 = (f32[256,256]{1,0:T(8,128)S(1)}, bf16[256,256]{1,0:T(8,128)(2,1)}) fusion(bf16[1,256,256]{2,1,0:T(8,128)(2,1)} %param.12), kind=kLoop, calls=%fused_computation.17 | loop fusion | flops 655360 | bytes 524288 | tf_op jit(solution)/shard_map/mul | solution.py:22
  20.3 0.0 copy-done.4
  20.3 1.4 %copy.17 = bf16[1,256,2560]{1,2,0:T(8,128)(2,1)} copy(bf16[1,256,2560]{2,1,0:T(8,128)(2,1)S(1)} %copy-done.4) | data formatting | bytes 2621440 | tf_op args[0]
  21.8 0.0 copy-start.10
  21.8 0.0 copy-start.11
  21.8 1.0 slice_reduce_fusion
  22.8 0.0 copy-done.1
  22.8 1.5 %copy.16 = bf16[1,256,2560]{1,2,0:T(8,128)(2,1)} copy(bf16[1,256,2560]{2,1,0:T(8,128)(2,1)S(1)} %copy-done.1) | data formatting | bytes 2621440 | tf_op args[1]
  24.2 0.0 copy-done.10
  24.2 0.0 copy-done.11
  24.2 0.6 exponential_bitcast_fusion
  24.9 1.7 %mul.64 = f32[256,40,64]{0,2,1:T(8,128)} broadcast(f32[256,40]{0,1:T(8,128)S(1)} %get-tuple-element.21), dimensions={0,1} | broadcast | bytes 2662400 | tf_op jit(solution)/shard_map/mul | solution.py:292
  26.6 2.1 %copy.14 = f32[256,2560]{1,0:T(8,128)S(1)} copy(f32[256,2560]{0,1:T(8,128)} %bitcast.36) | data formatting | bytes 5242880 | tf_op jit(solution)/shard_map/mul | solution.py:292
  28.7 0.6 slice.21.slope_ref
  29.4 3.6 %reshape_reshape.3 = bf16[256,8,4,8,2,5]{0,5,4,3,2,1:T(8,128)(2,1)} reshape(bf16[1,256,2560]{1,2,0:T(8,128)(2,1)} %copy.17) | data formatting | bytes 2621440 | tf_op jit(solution)/shard_map/reshape;reshape | solution.py:301
  33.0 3.2 %copy.18 = bf16[2,4,8,8,5,256]{5,4,3,2,1,0:T(8,128)(2,1)} copy(bf16[2,4,8,8,5,256]{5,4,0,3,1,2:T(8,128)(2,1)} %bitcast.37) | data formatting | bytes 2621440 | tf_op jit(solution)/shard_map/transpose | solution.py:302
  36.2 3.7 %reshape.84.turned_ref = bf16[2560,256]{1,0:T(8,128)(2,1)} reshape(bf16[2,4,8,8,5,256]{5,4,3,2,1,0:T(8,128)(2,1)} %copy.18) | data formatting | bytes 2621440 | tf_op jit(solution)/shard_map/reshape | solution.py:302
  39.9 0.0 copy-start.7
  39.9 0.0 copy-start.5
  39.9 0.0 copy-start.9
  39.9 5.8 %convert_reduce_fusion = bf16[256,256]{1,0:T(8,128)(2,1)S(1)} fusion(f32[40,256]{1,0:T(8,128)} %bitcast.46, f32[40,256]{1,0:T(8,128)} %get-tuple-element.10, pred[256,256]{1,0:T(8,128)(4,1)S(1)} %iota_compare_fusion, bf16[256,40,64]{0,2,1:T(8,128)(2,1)} %bitcast.40, bf16[256,40,64]{0,2,1:T(8,128)(2,1)} %bitcast.43), kind=kOutput, calls=%fused_computation | convolution fusion | flops 356450304 | bytes 2899968 | tf_op jit(solution)/shard_map/shp,thp->hst/dot_general | solution.py:285
  45.7 0.0 copy-start.8
  45.8 0.0 copy-done.7
  45.8 0.8 fusion.10
  46.6 0.0 copy-done.8
  46.6 0.0 copy-done.5
  46.6 0.0 copy-done.9
  46.6 1.5 %multiply_convert_fusion.1 = bf16[256,40,64]{0,2,1:T(8,128)(2,1)} fusion(bf16[256,40,64]{0,2,1:T(8,128)(2,1)S(1)} %bitcast.41, f32[256,40]{0,1:T(8,128)S(1)} %copy-done.9), kind=kLoop, calls=%fused_computation.4 | loop fusion | flops 1966080 | bytes 2662400 | tf_op jit(solution)/shard_map/convert_element_type | solution.py:281
  48.1 0.0 all-to-all-done.got_ref
  48.1 2.2 %scan_states.1 = (bf16[32,80,128]{2,1,0:T(8,128)(2,1)}, f32[1,128]{1,0:T(1,128)}) custom-call(s32[1]{0:T(128)} %bitcast.8.bound_ref, bf16[32,88,128]{2,1,0:T(8,128)(2,1)} %all-to-all-done.got_ref), custom_call_target="tpu_custom_call" | custom-call | tf_op jit(solution)/shard_map/scan_states/pallas_call | solution.py:46
  50.2 9.3 %all-to-all-start.1 = ((bf16[32,80,128]{2,1,0:T(8,128)(2,1)}), bf16[32,80,128]{2,1,0:T(8,128)(2,1)}, u32[]{:S(2)}, u32[]{:S(2)}) async-start(bf16[32,80,128]{2,1,0:T(8,128)(2,1)} %get-tuple-element.12), calls=%async_computation.1 | async-start | bytes 1310720 | tf_op jit(solution)/shard_map/all_to_all | solution.py:26
  59.5 0.0 copy-start.2
  59.5 1.9 %fusion.12.inner_ref = f32[256,128]{1,0:T(8,128)} fusion(bf16[256,256]{1,0:T(8,128)(2,1)} %copy-done.8, bf16[256,256]{1,0:T(8,128)(2,1)} %get-tuple-element.19), kind=kOutput, calls=%fused_computation.21 | convolution fusion | flops 16777216 | bytes 327680 | tf_op jit(solution)/shard_map/hst,sn->tn/dot_general | solution.py:289
  61.4 0.0 copy-done
  61.4 2.5 %fusion.2.read_ref = bf16[256,128]{1,0:T(8,128)(2,1)} fusion(f32[256,128]{1,0:T(8,128)} %fusion.10, bf16[256,2560]{0,1:T(8,128)(2,1)} %bitcast.42, bf16[1,1,2560,128]{3,2,1,0:T(8,128)(2,1)S(1)} %copy-done, f32[256,256]{1,0:T(8,128)S(1)} %get-tuple-element.18), kind=kOutput, calls=%fused_computation.7 | convolution fusion | flops 167870464 | bytes 2293760 | tf_op jit(solution)/shard_map/dot_general | solution.py:294
  63.9 0.0 copy-done.2
  63.9 1.4 %fusion.win_ref = bf16[256,2560]{1,0:T(8,128)(2,1)} fusion(f32[256,2560]{1,0:T(8,128)S(1)} %copy.14, bf16[1,256,2560]{2,1,0:T(8,128)(2,1)S(1)} %copy-done.2), kind=kLoop, calls=%fused_computation.3 | loop fusion | flops 1966080 | bytes 5242880 | tf_op jit(solution)/shard_map/convert_element_type | solution.py:293
  65.3 12.2 %all-to-all-done.1 = bf16[32,80,128]{2,1,0:T(8,128)(2,1)} async-done(((bf16[32,80,128]{2,1,0:T(8,128)(2,1)}), bf16[32,80,128]{2,1,0:T(8,128)(2,1)}, u32[]{:S(2)}, u32[]{:S(2)}) %all-to-all-start.1) | async-done | bytes 655392 | tf_op jit(solution)/shard_map/all_to_all | solution.py:26
  77.5 4.1 %finish.1 = (bf16[256,256]{1,0:T(8,128)(2,1)}, bf16[2,1288,256]{2,1,0:T(8,128)(2,1)}) custom-call(bf16[256,2560]{1,0:T(8,128)(2,1)} %fusion.win_ref, bf16[2560,128]{1,0:T(8,128)(2,1)} %bitcast.9.beyond_ref, f32[256,128]{1,0:T(8,128)} %fusion.12.inner_ref, f32[256,128]{1,0:T(8,128)} %slice.21.slope_ref, bf16[256,128]{1,0:T(8,128)(2,1)} %fusion.2.read_ref, ...), custom_call_target="tpu_custom_call" | custom-call | tf_op jit(solution)/shard_map/finish/pallas_call | solution.py:167
  81.6 9.6 %all_to_all.25.got_ref = bf16[2,1288,256]{2,1,0:T(8,128)(2,1)} all-to-all(bf16[2,1288,256]{2,1,0:T(8,128)(2,1)} %get-tuple-element.15), channel_id=1, replica_groups=mesh['seq_0'=8,'seq_1'=4,'dp_0'=8,'dp_1'=2] {'dp_1'}, dimensions={0} | all-to-all | bytes 2637824 | tf_op jit(solution)/shard_map/all_to_all | solution.py:26
  91.2 2.3 %add_pair.1 = (bf16[1280,256]{1,0:T(8,128)(2,1)}, f32[8,256]{1,0:T(8,128)}) custom-call(bf16[2,1288,256]{2,1,0:T(8,128)(2,1)} %all_to_all.25.got_ref), custom_call_target="tpu_custom_call" | custom-call | tf_op jit(solution)/shard_map/add_pair/pallas_call | solution.py:185
  93.5 14.8 %all_to_all.26.got_ref = bf16[4,320,256]{2,1,0:T(8,128)(2,1)} all-to-all(bf16[4,320,256]{2,1,0:T(8,128)(2,1)} %bitcast.44), channel_id=1, replica_groups=mesh['seq_0'=8,'seq_1'=4,'dp_0'=8,'dp_1'=2] {'seq_1'}, dimensions={0} | all-to-all | bytes 1310720 | tf_op jit(solution)/shard_map/all_to_all | solution.py:26
  108.3 2.0 %add_split.1 = bf16[64,8,256]{2,1,0:T(8,128)(2,1)} custom-call(bf16[4,320,256]{2,1,0:T(8,128)(2,1)} %all_to_all.26.got_ref, f32[8,256]{1,0:T(8,128)} %get-tuple-element.17.peak_ref), custom_call_target="tpu_custom_call" | custom-call | tf_op jit(solution)/shard_map/add_split/pallas_call | solution.py:212
  110.3 12.8 %all-to-all-start.4 = ((bf16[64,8,256]{2,1,0:T(8,128)(2,1)}), bf16[64,8,256]{2,1,0:T(8,128)(2,1)S(1)}, u32[]{:S(2)}, u32[]{:S(2)}) async-start(bf16[64,8,256]{2,1,0:T(8,128)(2,1)} %add_split.1), calls=%async_computation.4 | async-start | bytes 524288 | tf_op jit(solution)/shard_map/all_to_all | solution.py:26
  123.1 0.6 pad_add_fusion.place_ref
  123.7 11.8 %all-to-all-done.4.got_ref = bf16[64,8,256]{2,1,0:T(8,128)(2,1)S(1)} async-done(((bf16[64,8,256]{2,1,0:T(8,128)(2,1)}), bf16[64,8,256]{2,1,0:T(8,128)(2,1)S(1)}, u32[]{:S(2)}, u32[]{:S(2)}) %all-to-all-start.4) | async-done | bytes 262176 | tf_op jit(solution)/shard_map/all_to_all | solution.py:26
  135.5 0.0 copy-start.6
  135.5 0.7 copy-done.6
  136.2 1.7 %close.1 = f32[5,256]{1,0:T(8,128)} custom-call(s32[2]{0:T(128)} %pad_add_fusion.place_ref, bf16[64,8,256]{2,1,0:T(8,128)(2,1)} %copy-done.6), custom_call_target="tpu_custom_call" | custom-call | tf_op jit(solution)/shard_map/close/pallas_call | solution.py:238
  (1 shorter events, 0.0 us)
Async XLA Ops:
  0.6 60.8 %copy-start = (bf16[1,1,2560,128]{3,2,1,0:T(8,128)(2,1)S(1)}, bf16[1,1,2560,128]{3,2,1,0:T(8,128)(2,1)}, u32[]{:S(2)}) copy-start(bf16[1,1,2560,128]{3,2,1,0:T(8,128)(2,1)} %param.13) | copy-start | bytes 1966084
  0.6 16.5 %copy-start.3 = (bf16[1,256,2560]{2,1,0:T(8,128)(2,1)S(1)}, bf16[1,256,2560]{2,1,0:T(8,128)(2,1)}, u32[]{:S(2)}) copy-start(bf16[1,256,2560]{2,1,0:T(8,128)(2,1)} %param.9) | copy-start | bytes 3932164
  6.4 14.0 %copy-start.4 = (bf16[1,256,2560]{2,1,0:T(8,128)(2,1)S(1)}, bf16[1,256,2560]{2,1,0:T(8,128)(2,1)}, u32[]{:S(2)}) copy-start(bf16[1,256,2560]{2,1,0:T(8,128)(2,1)} %param.7) | copy-start | bytes 3932164
  6.4 41.7 %all-to-all-start = ((bf16[32,88,128]{2,1,0:T(8,128)(2,1)}), bf16[32,88,128]{2,1,0:T(8,128)(2,1)}, u32[]{:S(2)}, u32[]{:S(2)}) async-start(bf16[32,88,128]{2,1,0:T(8,128)(2,1)} %get-tuple-element.11), calls=%async_computation | async-start | bytes 1441792 | tf_op jit(solution)/shard_map/all_to_all | solution.py:26
  18.6 4.2 %copy-start.1 = (bf16[1,256,2560]{2,1,0:T(8,128)(2,1)S(1)}, bf16[1,256,2560]{2,1,0:T(8,128)(2,1)}, u32[]{:S(2)}) copy-start(bf16[1,256,2560]{2,1,0:T(8,128)(2,1)} %param.8) | copy-start | bytes 3932164
  21.8 2.5 %copy-start.10 = (f32[40,256]{1,0:T(8,128)S(1)}, f32[40,256]{1,0:T(8,128)}, u32[]{:S(2)}) copy-start(f32[40,256]{1,0:T(8,128)} %get-tuple-element.10) | copy-start | bytes 122884
  21.8 2.5 %copy-start.11 = (f32[1,40,256]{2,1,0:T(8,128)S(1)}, f32[1,40,256]{2,1,0:T(8,128)}, u32[]{:S(2)}) copy-start(f32[1,40,256]{2,1,0:T(8,128)} %param.10) | copy-start | bytes 122884
  39.9 5.9 %copy-start.7 = (bf16[256,256]{1,0:T(8,128)(2,1)S(1)}, bf16[256,256]{1,0:T(8,128)(2,1)}, u32[]{:S(2)}) copy-start(bf16[256,256]{1,0:T(8,128)(2,1)} %get-tuple-element.19) | copy-start | bytes 393220
  39.9 6.7 %copy-start.5 = (bf16[1,256,2560]{1,2,0:T(8,128)(2,1)S(1)}, bf16[1,256,2560]{1,2,0:T(8,128)(2,1)}, u32[]{:S(2)}) copy-start(bf16[1,256,2560]{1,2,0:T(8,128)(2,1)} %copy.15) | copy-start | bytes 3932164
  39.9 6.7 %copy-start.9 = (f32[256,40]{0,1:T(8,128)S(1)}, f32[256,40]{0,1:T(8,128)}, u32[]{:S(2)}) copy-start(f32[256,40]{0,1:T(8,128)} %get-tuple-element.20) | copy-start | bytes 122884
  45.7 0.8 copy-start.8
  50.2 27.3 %all-to-all-start.1 = ((bf16[32,80,128]{2,1,0:T(8,128)(2,1)}), bf16[32,80,128]{2,1,0:T(8,128)(2,1)}, u32[]{:S(2)}, u32[]{:S(2)}) async-start(bf16[32,80,128]{2,1,0:T(8,128)(2,1)} %get-tuple-element.12), calls=%async_computation.1 | async-start | bytes 1310720 | tf_op jit(solution)/shard_map/all_to_all | solution.py:26
  59.5 4.4 %copy-start.2 = (bf16[1,256,2560]{2,1,0:T(8,128)(2,1)S(1)}, bf16[1,256,2560]{2,1,0:T(8,128)(2,1)}, u32[]{:S(2)}) copy-start(bf16[1,256,2560]{2,1,0:T(8,128)(2,1)} %param.8) | copy-start | bytes 3932164
  110.3 25.2 %all-to-all-start.4 = ((bf16[64,8,256]{2,1,0:T(8,128)(2,1)}), bf16[64,8,256]{2,1,0:T(8,128)(2,1)S(1)}, u32[]{:S(2)}, u32[]{:S(2)}) async-start(bf16[64,8,256]{2,1,0:T(8,128)(2,1)} %add_split.1), calls=%async_computation.4 | async-start | bytes 524288 | tf_op jit(solution)/shard_map/all_to_all | solution.py:26
  135.5 0.7 copy-start.6

commit v3 on v2

--- a/solution.py
+++ b/solution.py
@@ -1,5 +1,3 @@
-import functools
-
 import jax
 import jax.numpy as jnp
 from jax import lax
@@ -17,19 +15,18 @@
 bf16 = jnp.bfloat16
 
 
-def silu_slope(value):
-    sigma = jax.nn.sigmoid(value)
-    return sigma * (1.0 + value * (1.0 - sigma))
+def budget(mib):
+    return pltpu.CompilerParams(vmem_limit_bytes=mib * 2**20)
 
 
 def exchange(x, axes):
     return lax.all_to_all(x, axes, 0, 0, tiled=True)
 
 
-def scan_body(bound_ref, got_ref, out_ref, peak_ref):
+def scan_body(place_ref, got_ref, out_ref, peak_ref):
     blocks, _, states = got_ref.shape
     rows = out_ref.shape[1]
-    first = lax.broadcasted_iota(jnp.int32, (rows, states), 0) < bound_ref[0]
+    first = lax.broadcasted_iota(jnp.int32, (rows, states), 0) < place_ref[2]
     state = jnp.zeros((rows, states), f32)
     peak = jnp.zeros((1, states), f32)
     for k in reversed(range(blocks)):
@@ -41,7 +38,7 @@
     peak_ref[...] = peak
 
 
-def scan_states(got, bound, rows):
+def scan_states(got, place, rows):
     blocks, _, states = got.shape
     return pl.pallas_call(
         scan_body,
@@ -57,11 +54,12 @@
             jax.ShapeDtypeStruct((blocks, rows, states), bf16),
             jax.ShapeDtypeStruct((1, states), f32),
         ],
+        compiler_params=budget(8),
         name="scan_states",
-    )(bound, got)
-
-
-def summary_body(in_ref, cot_ref, decay_ref, pre_ref, sent_ref, cum_ref, reads_ref, spread_ref):
+    )(place, got)
+
+
+def summary_body(in_ref, cot_ref, decay_ref, pre_ref, sent_ref, reads_ref, spread_ref):
     step = pl.program_id(0)
     heads, tokens = decay_ref.shape
     chunks, rows_all, states = sent_ref.shape
@@ -79,7 +77,6 @@
             precision=lax.Precision.HIGHEST,
             preferred_element_type=f32,
         )
-        cum_ref[...] = cum
         grown = jnp.exp(cum)
         high = grown.astype(bf16)
         spread_ref[0] = high
@@ -130,20 +127,212 @@
             pl.BlockSpec((heads, tokens), lambda i: (0, 0)),
             pl.BlockSpec((tokens, 2 * states), lambda i: (0, 0)),
         ],
-        out_specs=[
-            pl.BlockSpec((n_seq // grid, rows + 8, states), lambda i: (i, 0, 0)),
-            pl.BlockSpec((heads, tokens), lambda i: (0, 0)),
-        ],
-        out_shape=[
-            jax.ShapeDtypeStruct((n_seq, rows + 8, states), bf16),
-            jax.ShapeDtypeStruct((heads, tokens), f32),
-        ],
+        out_specs=pl.BlockSpec((n_seq // grid, rows + 8, states), lambda i: (i, 0, 0)),
+        out_shape=jax.ShapeDtypeStruct((n_seq, rows + 8, states), bf16),
         scratch_shapes=[
             pltpu.VMEM((tokens, states), bf16),
             pltpu.VMEM((2, heads, tokens), bf16),
         ],
+        compiler_params=budget(60),
         name="summarize",
     )(rows_in, cots, decays, pre)
+
+
+def inner_body(
+    cot_ref,
+    in_ref,
+    decay_ref,
+    step_ref,
+    pre_ref,
+    entry_ref,
+    win_ref,
+    inner_ref,
+    slope_ref,
+    read_ref,
+    column_ref,
+    row_ref,
+    spread_ref,
+    mix_ref,
+    carry_ref,
+):
+    step = pl.program_id(0)
+    heads, tokens = decay_ref.shape
+    span = cot_ref.shape[1]
+    states = entry_ref.shape[1]
+    per_step = heads // pl.num_programs(0)
+    head_size = span // per_step
+    half = tokens // 2
+    both = (((0,), (0,)), ((), ()))
+    last = (((1,), (1,)), ((), ()))
+
+    @pl.when(step == 0)
+    def _():
+        one = lax.broadcasted_iota(jnp.int32, (tokens, tokens), 0)
+        two = lax.broadcasted_iota(jnp.int32, (tokens, tokens), 1)
+        cum = jnp.dot(
+            decay_ref[...],
+            (one <= two).astype(f32),
+            precision=lax.Precision.HIGHEST,
+            preferred_element_type=f32,
+        )
+        column_ref[...] = jnp.zeros_like(column_ref)
+        column_ref[:, :heads] = lax.dot_general(
+            (one >= two).astype(f32),
+            decay_ref[...],
+            last,
+            precision=lax.Precision.HIGHEST,
+            preferred_element_type=f32,
+        )
+        row_ref[...] = cum - jnp.log(step_ref[...])
+        grown = jnp.exp(cum)
+        shrunk = jnp.exp(cum[:, tokens - 1 :] - cum) * step_ref[...]
+        for k, value in enumerate((grown, shrunk)):
+            high = value.astype(bf16)
+            spread_ref[2 * k] = high
+            spread_ref[2 * k + 1] = (value - high.astype(f32)).astype(bf16)
+        mix_ref[...] = jnp.zeros_like(mix_ref)
+        carry_ref[...] = jnp.zeros_like(carry_ref)
+
+    owner = lax.broadcasted_iota(jnp.int32, (heads, span), 0) * head_size - step * span
+    lane = lax.broadcasted_iota(jnp.int32, (heads, span), 1)
+    hot = jnp.where((lane >= owner) & (lane < owner + head_size), 1.0, 0.0).astype(bf16)
+
+    def expanded(k):
+        scale = lax.dot_general(spread_ref[2 * k], hot, both, preferred_element_type=f32)
+        return scale + lax.dot_general(
+            spread_ref[2 * k + 1], hot, both, preferred_element_type=f32
+        )
+
+    win_ref[...] = (in_ref[...].astype(f32) * expanded(1)).astype(bf16)
+    weighted_cot = (cot_ref[...].astype(f32) * expanded(0)).astype(bf16)
+    carry_ref[...] += jnp.dot(weighted_cot, entry_ref[...], preferred_element_type=f32)
+
+    columns = pltpu.roll(column_ref[...], lax.rem(128 - per_step * step, 128), 1)
+    rows = [row_ref[pl.ds(per_step * step + j, 1), :] for j in range(per_step)]
+    low = lax.broadcasted_iota(jnp.int32, (half, 2 * head_size), 1) < head_size
+    later = lax.broadcasted_iota(jnp.int32, (half, half), 0) >= lax.broadcasted_iota(
+        jnp.int32, (half, half), 1
+    )
+    for s, t in ((0, 0), (1, 0), (1, 1)):
+        total = mix_ref[s * half : (s + 1) * half, t * half : (t + 1) * half]
+        for j in range(per_step):
+            lanes = slice(j // 2 * 2 * head_size, (j // 2 + 1) * 2 * head_size)
+            left = cot_ref[s * half : (s + 1) * half, lanes]
+            keep = low if j % 2 == 0 else jnp.logical_not(low)
+            left = jnp.where(keep, left.astype(f32), 0.0).astype(bf16)
+            right = in_ref[t * half : (t + 1) * half, lanes]
+            scores = lax.dot_general(left, right, last, preferred_element_type=f32)
+            gap = columns[s * half : (s + 1) * half, j : j + 1] - rows[j][
+                :, t * half : (t + 1) * half
+            ]
+            if s == t:
+                gap = jnp.where(later, gap, -1e30)
+            total += scores * jnp.exp(gap)
+        mix_ref[s * half : (s + 1) * half, t * half : (t + 1) * half] = total
+
+    @pl.when(step == pl.num_programs(0) - 1)
+    def _():
+        value = pre_ref[...].astype(f32)
+        sigma = 1.0 / (1.0 + jnp.exp(-value))
+        active = (value / (1.0 + jnp.exp(-value))).astype(bf16)
+        slope = sigma * (1.0 + value * (1.0 - sigma))
+        mixed = mix_ref[...].astype(bf16)
+        inner_ref[...] = lax.dot_general(
+            mixed, active[:, states:], both, preferred_element_type=f32
+        )
+        read = carry_ref[...] + jnp.dot(mixed, active[:, :states], preferred_element_type=f32)
+        slope_ref[...] = slope[:, :states]
+        read_ref[...] = (read * slope[:, states:]).astype(bf16)
+
+
+def inner_terms(cots, ins, decays, steps, pre, entry):
+    tokens, channels = cots.shape
+    heads = decays.shape[0]
+    states = entry.shape[1]
+    grid = 4
+    span = channels // grid
+    whole = lambda i: (0, 0)
+    return pl.pallas_call(
+        inner_body,
+        grid=(grid,),
+        in_specs=[
+            pl.BlockSpec((tokens, span), lambda i: (0, i)),
+            pl.BlockSpec((tokens, span), lambda i: (0, i)),
+            pl.BlockSpec((heads, tokens), whole),
+            pl.BlockSpec((heads, tokens), whole),
+            pl.BlockSpec((tokens, 2 * states), whole),
+            pl.BlockSpec((span, states), lambda i: (i, 0)),
+        ],
+        out_specs=[
+            pl.BlockSpec((tokens, span), lambda i: (0, i)),
+            pl.BlockSpec((tokens, states), whole),
+            pl.BlockSpec((tokens, states), whole),
+            pl.BlockSpec((tokens, states), whole),
+        ],
+        out_shape=[
+            jax.ShapeDtypeStruct((tokens, channels), bf16),
+            jax.ShapeDtypeStruct((tokens, states), f32),
+            jax.ShapeDtypeStruct((tokens, states), f32),
+            jax.ShapeDtypeStruct((tokens, states), bf16),
+        ],
+        scratch_shapes=[
+            pltpu.VMEM((tokens, 128), f32),
+            pltpu.VMEM((heads, tokens), f32),
+            pltpu.VMEM((4, heads, tokens), bf16),
+            pltpu.VMEM((tokens, tokens), f32),
+            pltpu.VMEM((tokens, states), f32),
+        ],
+        compiler_params=budget(16),
+        cost_estimate=pl.CostEstimate(
+            flops=4 * 10**9, transcendentals=2 * 10**6, bytes_accessed=6 * 10**6
+        ),
+        name="inner_terms",
+    )(cots, ins, decays, steps, pre, entry)
+
+
+def turn_body(in_ref, out_ref, hot_ref):
+    n_c, n_x, _, part, _ = out_ref.shape
+    span = in_ref.shape[1]
+    n_z, own = 8, part // 16
+
+    @pl.when(pl.program_id(0) == 0)
+    def _():
+        row = lax.broadcasted_iota(jnp.int32, (span, 1), 0)
+        i, row = lax.rem(row, own), lax.div(row, own)
+        z, row = lax.rem(row, n_z), lax.div(row, n_z)
+        y, row = lax.rem(row, 2), lax.div(row, 2)
+        x, c = lax.rem(row, n_x), lax.div(row, n_x)
+        source = (((y * n_x + x) * n_z + z) * n_c + c) * own + i
+        lane = lax.broadcasted_iota(jnp.int32, (span, span), 1)
+        hot_ref[...] = jnp.where(lane == source, 1.0, 0.0).astype(bf16)
+
+    turned = lax.dot_general(
+        hot_ref[...], in_ref[...], (((1,), (1,)), ((), ())), preferred_element_type=f32
+    ).astype(bf16)
+    for c in range(n_c):
+        for x in range(n_x):
+            at = (c * n_x + x) * part
+            out_ref[c, x, 0] = turned[at : at + part]
+
+
+def turn(rows_in, n_x, n_c):
+    tokens, width = rows_in.shape
+    grid = 4
+    span = width // grid
+    part = span // (n_x * n_c)
+    return pl.pallas_call(
+        turn_body,
+        grid=(grid,),
+        in_specs=[pl.BlockSpec((tokens, span), lambda i: (0, i))],
+        out_specs=pl.BlockSpec((n_c, n_x, 1, part, tokens), lambda i: (0, 0, i, 0, 0)),
+        out_shape=jax.ShapeDtypeStruct((n_c, n_x, grid, part, tokens), bf16),
+        scratch_shapes=[pltpu.VMEM((span, span), bf16)],
+        compiler_params=budget(12),
+        cost_estimate=pl.CostEstimate(
+            flops=10**9, transcendentals=0, bytes_accessed=3 * 10**6
+        ),
+        name="turn",
+    )(rows_in).reshape(width, tokens)
 
 
 def finish_body(win_ref, beyond_ref, inner_ref, slope_ref, read_ref, turned_ref, peak_ref, grad_ref, prod_ref):
@@ -170,6 +359,7 @@
             jax.ShapeDtypeStruct((tokens, 2 * states), bf16),
             jax.ShapeDtypeStruct((2, width // 2 + 8, 2 * states), bf16),
         ],
+        compiler_params=budget(16),
         name="finish",
     )(weighted_in, beyond, inner, slope, grad_read, turned, peak)
 
@@ -188,6 +378,7 @@
             jax.ShapeDtypeStruct((rows - 8, cols), bf16),
             jax.ShapeDtypeStruct((8, cols), f32),
         ],
+        compiler_params=budget(8),
         name="add_pair",
     )(got)
 
@@ -213,6 +404,7 @@
         split_body,
         out_shape=jax.ShapeDtypeStruct((pieces, 8, cols), bf16),
         scratch_shapes=[pltpu.VMEM((rows + 8, cols), f32)],
+        compiler_params=budget(6),
         name="add_split",
     )(got, peak)
 
@@ -242,6 +434,7 @@
             pl.BlockSpec(memory_space=pltpu.VMEM),
         ],
         out_shape=jax.ShapeDtypeStruct((own, cols), f32),
+        compiler_params=budget(4),
         name="close",
     )(place, got)
 
@@ -263,59 +456,31 @@
     rows_in = layer_input.reshape(tokens, width)
     flat_cot = scan_cotangent.reshape(tokens, channels)
     flat_pre = state_inputs.reshape(tokens, 2 * states)
-    sent, cumulative = summarize(
-        rows_in, flat_cot, log_decay.reshape(heads, tokens), flat_pre, n_seq, states
-    )
+    decays = log_decay.reshape(heads, tokens)
+    sent = summarize(rows_in, flat_cot, decays, flat_pre, n_seq, states)
     got = exchange(sent, SEQ)
     bound = head_size - ((y * n_x + x) * slice_rows) % head_size
-    slices, seq_peaks = scan_states(got, bound.astype(jnp.int32).reshape(1), slice_rows)
+    place = jnp.stack([y, z * n_c + c, bound]).astype(jnp.int32)
+    slices, seq_peaks = scan_states(got, place, slice_rows)
     beyond = exchange(slices, SEQ).reshape(channels, states)
 
-    inputs = scan_input.reshape(tokens, heads, head_size)
-    cotangents = scan_cotangent.reshape(tokens, heads, head_size)
-    steps = step_size.reshape(heads, tokens)
-    preact = flat_pre.astype(f32)
-    activated = jax.nn.silu(preact).astype(bf16)
-    writes = activated[:, :states]
-    reads = activated[:, states:]
-    weighted_cot = (cotangents * jnp.exp(cumulative).T[:, :, None]).astype(bf16)
-    later = lax.broadcasted_iota(jnp.int32, (tokens, tokens), 0) >= lax.broadcasted_iota(
-        jnp.int32, (tokens, tokens), 1
+    weighted_in, inner_write, slope, grad_read = inner_terms(
+        flat_cot,
+        scan_input.reshape(tokens, channels),
+        decays,
+        step_size.reshape(heads, tokens),
+        flat_pre,
+        entry_state.reshape(channels, states),
     )
-    scores = jnp.einsum("shp,thp->hst", cotangents, inputs, preferred_element_type=f32)
-    spread = jnp.where(later[None], cumulative[:, :, None] - cumulative[:, None, :], 0.0)
-    decay = jnp.where(later[None], jnp.exp(spread), 0.0)
-    mixing = (scores * decay * steps[:, None, :]).astype(bf16)
-    inner_write = jnp.einsum("hst,sn->tn", mixing, reads, preferred_element_type=f32)
-    inner_read = jnp.einsum("hst,tn->sn", mixing, writes, preferred_element_type=f32)
-    weighted_in = (
-        inputs * (steps * jnp.exp(cumulative[:, -1:] - cumulative)).T[:, :, None]
-    ).astype(bf16)
-    carried_read = jnp.dot(
-        weighted_cot.reshape(tokens, channels),
-        entry_state.reshape(channels, states),
-        preferred_element_type=f32,
-    )
-    slope = silu_slope(preact)
-    grad_read = ((inner_read + carried_read) * slope[:, states:]).astype(bf16)
-    turned = rows_in.reshape(tokens, n_y, n_x, n_z, n_c, own_rows)
-    turned = turned.transpose(4, 2, 1, 3, 5, 0).reshape(width, tokens)
-
+    turned = turn(rows_in, n_x, n_c)
     state_input_grad, product = finish(
-        weighted_in.reshape(tokens, channels),
-        beyond,
-        inner_write,
-        slope[:, :states],
-        grad_read,
-        turned,
-        seq_peaks,
+        weighted_in, beyond, inner_write, slope, grad_read, turned, seq_peaks
     )
     half, peaks = add_pair(exchange(product, "dp_1"))
     quarter = exchange(half.reshape(n_x, width // (n_x * n_c), 2 * states), "seq_1")
     pieces = add_split(quarter, peaks, n_y * n_z)
     arrived = exchange(pieces, ("seq_0", "dp_0"))
-    where = jnp.stack([y, z * n_c + c]).astype(jnp.int32)
-    return state_input_grad[None], close(arrived, where, own_rows)
+    return state_input_grad[None], close(arrived, place, own_rows)
 
 
 def solution(mesh):

time: 140 us -> 113 us (0.81)
  blocking collectives: 24.4 us -> 45.8 us
  local copies, waits for them, and re-layouts: 21 us -> 1.6 us
  starting transfers between devices: 32.8 us -> 16 us
  matrix products: 11 us -> 0 us
  other arithmetic: 5.95 us -> 0.08 us
  waiting for transfers between devices: 24 us -> 27.6 us
  Pallas kernels: 17.9 us -> 19.5 us
    all_to_all x2 -> x3, blocking collectives: 24.4 us -> 45.8 us  [exchange(): return lax.all_to_all(x, axes, 0, 0, tiled=True)]
    all_to_all x3 -> x2, starting transfers between devices: 32.8 us -> 16 us  [exchange(): return lax.all_to_all(x, axes, 0, 0, tiled=True)]
    dot_general x4 -> x0, matrix products: 11 us -> none  [the longest x1 5.82 us: on_device(): jnp.einsum('shp,thp->hst', cotangents, inputs, preferred_element_type=f32)]
    pallas_call x0 -> x2, Pallas kernels: none -> 9.19 us  [the longest x1 6.56 us: inner_terms(): pl.pallas_call(inner_body, grid=(grid,), in_specs=[pl.BlockSpec((tokens,...]
    mul x2 -> x0, local copies, waits for them, and re-layouts: 3.85 us -> none  [on_device(): inputs * (steps * jnp.exp(cumulative[:, -1:] - cumulative)).T[:, :, None]]
    reshape x1 -> x0, local copies, waits for them, and re-layouts: 3.66 us -> none  [on_device(): turned = turned.transpose(4, 2, 1, 3, 5, 0).reshape(width, tokens)]
    another operation x1 -> x0, local copies, waits for them, and re-layouts: 3.61 us -> none  [on_device(): turned = rows_in.reshape(tokens, n_y, n_x, n_z, n_c, own_rows)]
    all_to_all x3 -> x2, waiting for transfers between devices: 24 us -> 27.6 us  [exchange(): return lax.all_to_all(x, axes, 0, 0, tiled=True)]
  transfers between devices with their start and end apart: 3 -> 2, of which waited for: 2 -> 2; matrix products, arithmetic and copies ran while one was open for 27% -> 0% of each run, Pallas kernels for 0% -> 8%
where the time goes in v3:
time: 113 us; the launch traced here: 111 us
  blocking collectives  45.8 us (41%)
  waiting for transfers between devices  27.6 us (24%)
  Pallas kernels  19.5 us (17%)
  starting transfers between devices  16 us (14%)
  local copies, waits for them, and re-layouts  1.6 us (1%)
    all_to_all x3, blocking collectives, exchange(): return lax.all_to_all(x, axes, 0, 0, tiled=True)  45.8 us
    all_to_all x2, waiting for transfers between devices, exchange(): return lax.all_to_all(x, axes, 0, 0, tiled=True)  27.6 us
    all_to_all x2, starting transfers between devices, exchange(): return lax.all_to_all(x, axes, 0, 0, tiled=True)  16 us
    pallas_call x1, Pallas kernels, inner_terms(): pl.pallas_call(inner_body, grid=(grid,), in_specs=[pl.BlockSpec((tokens,...  6.56 us
    pallas_call x1, Pallas kernels, summarize(): pl.pallas_call(summary_body, grid=(grid,), in_specs=[pl.BlockSpec((tokens...  5.53 us
    pallas_call x1, Pallas kernels, turn(): pl.pallas_call(turn_body, grid=(grid,), in_specs=[pl.BlockSpec((tokens, s...  2.63 us
  transfers between devices with their start and end apart: 2, of which 2 were waited for; matrix products, arithmetic and copies ran while one was open for 0% of the time, Pallas kernels for 8%

profile of v3, /device:TPU:1, one launch (start us, length us, event | category | flops | bytes accessed | tf_op | source)
XLA Modules:
  0.0 111.4 jit_solution(17171037750170779579)
XLA Ops:
  0.6 5.5 %summarize.1 = bf16[32,88,128]{2,1,0:T(8,128)(2,1)} custom-call(bf16[256,2560]{1,0:T(8,128)(2,1)} %bitcast.15, bf16[256,2560]{1,0:T(8,128)(2,1)} %bitcast.17, f32[40,256]{1,0:T(8,128)} %bitcast.23, bf16[256,256]{1,0:T(8,128)(2,1)} %bitcast.21), custom_call_target="tpu_custom_call" | custom-call | tf_op jit(solution)/shard_map/summarize/pallas_call | solution.py:121
  6.2 10.5 %all-to-all-start = ((bf16[32,88,128]{2,1,0:T(8,128)(2,1)}), bf16[32,88,128]{2,1,0:T(8,128)(2,1)S(1)}, u32[]{:S(2)}, u32[]{:S(2)}) async-start(bf16[32,88,128]{2,1,0:T(8,128)(2,1)} %summarize.1), calls=%async_computation | async-start | bytes 1441792 | tf_op jit(solution)/shard_map/all_to_all | solution.py:23
  16.7 0.0 copy-start
  16.7 0.1 pad_add_fusion.place_ref
  16.8 19.9 %all-to-all-done.got_ref = bf16[32,88,128]{2,1,0:T(8,128)(2,1)S(1)} async-done(((bf16[32,88,128]{2,1,0:T(8,128)(2,1)}), bf16[32,88,128]{2,1,0:T(8,128)(2,1)S(1)}, u32[]{:S(2)}, u32[]{:S(2)}) %all-to-all-start) | async-done | bytes 720928 | tf_op jit(solution)/shard_map/all_to_all | solution.py:23
  36.6 1.6 %scan_states.1 = (bf16[32,80,128]{2,1,0:T(8,128)(2,1)}, f32[1,128]{1,0:T(1,128)S(1)}) custom-call(s32[3]{0:T(128)S(1)} %pad_add_fusion.place_ref, bf16[32,88,128]{2,1,0:T(8,128)(2,1)S(1)} %all-to-all-done.got_ref), custom_call_target="tpu_custom_call" | custom-call | tf_op jit(solution)/shard_map/scan_states/pallas_call | solution.py:43
  38.2 5.5 %all-to-all-start.1 = ((bf16[32,80,128]{2,1,0:T(8,128)(2,1)}), bf16[32,80,128]{2,1,0:T(8,128)(2,1)S(1)}, u32[]{:S(2)}, u32[]{:S(2)}) async-start(bf16[32,80,128]{2,1,0:T(8,128)(2,1)} %get-tuple-element.13), calls=%async_computation.1 | async-start | bytes 1310720 | tf_op jit(solution)/shard_map/all_to_all | solution.py:23
  43.8 0.0 copy-done
  43.8 0.0 copy-start.1
  43.8 0.0 copy-start.2
  43.8 0.0 copy-start.5
  43.8 0.0 copy-start.6
  43.8 0.0 copy-start.7
  43.9 0.0 copy-start.8
  43.9 2.6 %turn.1 = bf16[2,4,4,80,256]{4,3,2,1,0:T(8,128)(2,1)S(1)} custom-call(bf16[256,2560]{1,0:T(8,128)(2,1)S(1)} %bitcast.16), custom_call_target="tpu_custom_call" | custom-call | flops 1000000000 | bytes 3000000 | tf_op jit(solution)/shard_map/turn/pallas_call | solution.py:323
  46.5 0.0 copy-done.1
  46.5 0.0 copy-done.2
  46.5 0.0 copy-done.5
  46.5 0.0 copy-done.6
  46.5 0.0 copy-done.7
  46.6 0.0 copy-done.8
  46.6 6.6 %inner_terms.1 = (bf16[256,2560]{1,0:T(8,128)(2,1)S(1)}, f32[256,128]{1,0:T(8,128)S(1)}, f32[256,128]{1,0:T(8,128)S(1)}, bf16[256,128]{1,0:T(8,128)(2,1)S(1)}) custom-call(bf16[256,2560]{1,0:T(8,128)(2,1)S(1)} %bitcast.18, bf16[256,2560]{1,0:T(8,128)(2,1)S(1)} %bitcast.25, f32[40,256]{1,0:T(8,128)S(1)} %bitcast.24, f32[40,256]{1,0:T(8,128)S(1)} %bitcast.27, ...), custom_call_target="tpu_custom_call" | custom-call | flops 4000000000 | bytes 6000000 | tf_op jit(solution)/shard_map/inner_terms/pallas_call | solution.py:255
  53.1 0.0 copy-start.3
  53.2 0.6 copy-done.3
  53.8 7.7 %all-to-all-done.1 = bf16[32,80,128]{2,1,0:T(8,128)(2,1)S(1)} async-done(((bf16[32,80,128]{2,1,0:T(8,128)(2,1)}), bf16[32,80,128]{2,1,0:T(8,128)(2,1)S(1)}, u32[]{:S(2)}, u32[]{:S(2)}) %all-to-all-start.1) | async-done | bytes 655392 | tf_op jit(solution)/shard_map/all_to_all | solution.py:23
  61.5 0.0 copy-start.4
  61.5 0.9 copy-done.4
  62.4 1.6 %finish.1 = (bf16[256,256]{1,0:T(8,128)(2,1)}, bf16[2,1288,256]{2,1,0:T(8,128)(2,1)S(1)}) custom-call(bf16[256,2560]{1,0:T(8,128)(2,1)S(1)} %get-tuple-element.12.win_ref, bf16[2560,128]{1,0:T(8,128)(2,1)S(1)} %bitcast.14, f32[256,128]{1,0:T(8,128)S(1)} %get-tuple-element.14.inner_ref, f32[256,128]{1,0:T(8,128)S(1)} %copy-done.4, ...), custom_call_target="tpu_custom_call" | custom-call | tf_op jit(solution)/shard_map/finish/pallas_call | solution.py:356
  64.0 8.0 %all_to_all.25.got_ref = bf16[2,1288,256]{2,1,0:T(8,128)(2,1)S(1)} all-to-all(bf16[2,1288,256]{2,1,0:T(8,128)(2,1)S(1)} %get-tuple-element.19), channel_id=1, replica_groups=mesh['seq_0'=8,'seq_1'=4,'dp_0'=8,'dp_1'=2] {'dp_1'}, dimensions={0} | all-to-all | bytes 2637824 | tf_op jit(solution)/shard_map/all_to_all | solution.py:23
  72.0 0.2 add_pair.1
  72.1 13.3 %all_to_all.26.got_ref = bf16[4,320,256]{2,1,0:T(8,128)(2,1)S(1)} all-to-all(bf16[4,320,256]{2,1,0:T(8,128)(2,1)S(1)} %bitcast.20), channel_id=1, replica_groups=mesh['seq_0'=8,'seq_1'=4,'dp_0'=8,'dp_1'=2] {'seq_1'}, dimensions={0} | all-to-all | bytes 1310720 | tf_op jit(solution)/shard_map/all_to_all | solution.py:23
  85.5 0.2 add_split.1
  85.7 24.5 %all_to_all.27.got_ref = bf16[64,8,256]{2,1,0:T(8,128)(2,1)S(1)} all-to-all(bf16[64,8,256]{2,1,0:T(8,128)(2,1)S(1)} %add_split.1), channel_id=1, replica_groups=mesh['seq_0'=8,'seq_1'=4,'dp_0'=8,'dp_1'=2] {'seq_0','dp_0'}, dimensions={0} | all-to-all | bytes 524288 | tf_op jit(solution)/shard_map/all_to_all | solution.py:23
  110.1 1.2 %close.1 = f32[5,256]{1,0:T(8,128)} custom-call(s32[3]{0:T(128)S(1)} %pad_add_fusion.place_ref, bf16[64,8,256]{2,1,0:T(8,128)(2,1)S(1)} %all_to_all.27.got_ref), custom_call_target="tpu_custom_call" | custom-call | tf_op jit(solution)/shard_map/close/pallas_call | solution.py:430
Async XLA Ops:
  6.2 30.5 %all-to-all-start = ((bf16[32,88,128]{2,1,0:T(8,128)(2,1)}), bf16[32,88,128]{2,1,0:T(8,128)(2,1)S(1)}, u32[]{:S(2)}, u32[]{:S(2)}) async-start(bf16[32,88,128]{2,1,0:T(8,128)(2,1)} %summarize.1), calls=%async_computation | async-start | bytes 1441792 | tf_op jit(solution)/shard_map/all_to_all | solution.py:23
  16.7 27.1 %copy-start = (bf16[1,256,2560]{2,1,0:T(8,128)(2,1)S(1)}, bf16[1,256,2560]{2,1,0:T(8,128)(2,1)}, u32[]{:S(2)}) copy-start(bf16[1,256,2560]{2,1,0:T(8,128)(2,1)} %param.7) | copy-start | bytes 3932164
  38.2 23.3 %all-to-all-start.1 = ((bf16[32,80,128]{2,1,0:T(8,128)(2,1)}), bf16[32,80,128]{2,1,0:T(8,128)(2,1)S(1)}, u32[]{:S(2)}, u32[]{:S(2)}) async-start(bf16[32,80,128]{2,1,0:T(8,128)(2,1)} %get-tuple-element.13), calls=%async_computation.1 | async-start | bytes 1310720 | tf_op jit(solution)/shard_map/all_to_all | solution.py:23
  43.8 2.7 %copy-start.1 = (bf16[1,256,2560]{2,1,0:T(8,128)(2,1)S(1)}, bf16[1,256,2560]{2,1,0:T(8,128)(2,1)}, u32[]{:S(2)}) copy-start(bf16[1,256,2560]{2,1,0:T(8,128)(2,1)} %param.9) | copy-start | bytes 3932164
  43.8 2.7 %copy-start.2 = (bf16[1,256,256]{2,1,0:T(8,128)(2,1)S(1)}, bf16[1,256,256]{2,1,0:T(8,128)(2,1)}, u32[]{:S(2)}) copy-start(bf16[1,256,256]{2,1,0:T(8,128)(2,1)} %param.12) | copy-start | bytes 393220
  43.8 2.7 %copy-start.5 = (f32[1,40,256]{2,1,0:T(8,128)S(1)}, f32[1,40,256]{2,1,0:T(8,128)}, u32[]{:S(2)}) copy-start(f32[1,40,256]{2,1,0:T(8,128)} %param.11) | copy-start | bytes 122884
  43.8 2.7 %copy-start.6 = (bf16[1,256,2560]{2,1,0:T(8,128)(2,1)S(1)}, bf16[1,256,2560]{2,1,0:T(8,128)(2,1)}, u32[]{:S(2)}) copy-start(bf16[1,256,2560]{2,1,0:T(8,128)(2,1)} %param.8) | copy-start | bytes 3932164
  43.8 2.7 %copy-start.7 = (bf16[1,1,2560,128]{3,2,1,0:T(8,128)(2,1)S(1)}, bf16[1,1,2560,128]{3,2,1,0:T(8,128)(2,1)}, u32[]{:S(2)}) copy-start(bf16[1,1,2560,128]{3,2,1,0:T(8,128)(2,1)} %param.13) | copy-start | bytes 1966084
  43.9 2.7 %copy-start.8 = (f32[1,40,256]{2,1,0:T(8,128)S(1)}, f32[1,40,256]{2,1,0:T(8,128)}, u32[]{:S(2)}) copy-start(f32[1,40,256]{2,1,0:T(8,128)} %param.10) | copy-start | bytes 122884
  53.1 0.7 copy-start.3
  61.5 0.9 copy-start.4

commit v4 on v3

--- a/solution.py
+++ b/solution.py
@@ -13,6 +13,11 @@
 epsilon = 1e-06
 f32 = jnp.float32
 bf16 = jnp.bfloat16
+
+
+def silu_slope(value):
+    sigma = 1.0 / (1.0 + jnp.exp(-value))
+    return sigma * (1.0 + value * (1.0 - sigma))
 
 
 def budget(mib):
@@ -51,7 +56,7 @@
             pl.BlockSpec(memory_space=pltpu.VMEM),
         ],
         out_shape=[
-            jax.ShapeDtypeStruct((blocks, rows, states), bf16),
+            pltpu.VMEM((blocks, rows, states), bf16),
             jax.ShapeDtypeStruct((1, states), f32),
         ],
         compiler_params=budget(8),
@@ -59,10 +64,11 @@
     )(place, got)
 
 
-def summary_body(in_ref, cot_ref, decay_ref, pre_ref, sent_ref, reads_ref, spread_ref):
+def summary_body(place_ref, in_ref, cot_ref, decay_ref, pre_ref, sent_ref, reads_ref, spread_ref):
     step = pl.program_id(0)
     heads, tokens = decay_ref.shape
-    chunks, rows_all, states = sent_ref.shape
+    total, rows_all, states = sent_ref.shape
+    chunks = total // pl.num_programs(0)
     span = cot_ref.shape[1]
     rows = span // chunks
     head_size = span * pl.num_programs(0) // heads
@@ -98,7 +104,7 @@
     last = scale[tokens - 1 :, :]
     row = lax.broadcasted_iota(jnp.int32, (rows_all - rows, states), 0)
     for d in range(chunks):
-        sent_ref[d, :rows, :] = later[d * rows : (d + 1) * rows]
+        sent_ref[step * chunks + d, :rows, :] = later[d * rows : (d + 1) * rows]
         first = jnp.broadcast_to(last[:, d * rows : d * rows + 1], (8, states))
         second = jnp.broadcast_to(last[:, (d + 1) * rows - 1 : (d + 1) * rows], (8, states))
         first_high = first.astype(bf16).astype(f32)
@@ -108,34 +114,35 @@
         extra = jnp.where(row == 2, second_high, extra)
         extra = jnp.where(row == 3, second - second_high, extra)
         extra = jnp.where(row >= 4, turned[:, :states], extra)
-        sent_ref[d, rows:, :] = extra.astype(bf16)
-
-
-def summarize(rows_in, cots, decays, pre, n_seq, head_states):
+        sent_ref[step * chunks + d, rows:, :] = extra.astype(bf16)
+
+
+def summarize(place, rows_in, cots, decays, pre, n_seq, head_states):
     tokens, channels = cots.shape
     heads = decays.shape[0]
     states = head_states
-    grid = 4
+    grid = 2
     span = channels // grid
     rows = channels // n_seq
     return pl.pallas_call(
         summary_body,
         grid=(grid,),
         in_specs=[
+            pl.BlockSpec(memory_space=pltpu.SMEM),
             pl.BlockSpec((tokens, span), lambda i: (0, i)),
             pl.BlockSpec((tokens, span), lambda i: (0, i)),
             pl.BlockSpec((heads, tokens), lambda i: (0, 0)),
             pl.BlockSpec((tokens, 2 * states), lambda i: (0, 0)),
         ],
-        out_specs=pl.BlockSpec((n_seq // grid, rows + 8, states), lambda i: (i, 0, 0)),
-        out_shape=jax.ShapeDtypeStruct((n_seq, rows + 8, states), bf16),
+        out_specs=pl.BlockSpec(memory_space=pltpu.VMEM),
+        out_shape=pltpu.VMEM((n_seq, rows + 8, states), bf16),
         scratch_shapes=[
             pltpu.VMEM((tokens, states), bf16),
             pltpu.VMEM((2, heads, tokens), bf16),
         ],
         compiler_params=budget(60),
         name="summarize",
-    )(rows_in, cots, decays, pre)
+    )(place, rows_in, cots, decays, pre)
 
 
 def inner_body(
@@ -145,10 +152,7 @@
     step_ref,
     pre_ref,
     entry_ref,
-    win_ref,
-    inner_ref,
-    slope_ref,
-    read_ref,
+    out_ref,
     column_ref,
     row_ref,
     spread_ref,
@@ -203,7 +207,8 @@
             spread_ref[2 * k + 1], hot, both, preferred_element_type=f32
         )
 
-    win_ref[...] = (in_ref[...].astype(f32) * expanded(1)).astype(bf16)
+    at = pl.multiple_of(step * span, 128)
+    out_ref[:, pl.ds(at, span)] = (in_ref[...].astype(f32) * expanded(1)).astype(bf16)
     weighted_cot = (cot_ref[...].astype(f32) * expanded(0)).astype(bf16)
     carry_ref[...] += jnp.dot(weighted_cot, entry_ref[...], preferred_element_type=f32)
 
@@ -233,16 +238,17 @@
     @pl.when(step == pl.num_programs(0) - 1)
     def _():
         value = pre_ref[...].astype(f32)
-        sigma = 1.0 / (1.0 + jnp.exp(-value))
         active = (value / (1.0 + jnp.exp(-value))).astype(bf16)
-        slope = sigma * (1.0 + value * (1.0 - sigma))
         mixed = mix_ref[...].astype(bf16)
-        inner_ref[...] = lax.dot_general(
-            mixed, active[:, states:], both, preferred_element_type=f32
-        )
+        inner = lax.dot_general(mixed, active[:, states:], both, preferred_element_type=f32)
+        high = inner.astype(bf16)
+        channels = out_ref.shape[1] - 3 * states
+        out_ref[:, channels : channels + states] = high
+        low_part = (inner - high.astype(f32)).astype(bf16)
+        out_ref[:, channels + states : channels + 2 * states] = low_part
         read = carry_ref[...] + jnp.dot(mixed, active[:, :states], preferred_element_type=f32)
-        slope_ref[...] = slope[:, :states]
-        read_ref[...] = (read * slope[:, states:]).astype(bf16)
+        read = read * silu_slope(value[:, states:])
+        out_ref[:, channels + 2 * states :] = read.astype(bf16)
 
 
 def inner_terms(cots, ins, decays, steps, pre, entry):
@@ -263,18 +269,8 @@
             pl.BlockSpec((tokens, 2 * states), whole),
             pl.BlockSpec((span, states), lambda i: (i, 0)),
         ],
-        out_specs=[
-            pl.BlockSpec((tokens, span), lambda i: (0, i)),
-            pl.BlockSpec((tokens, states), whole),
-            pl.BlockSpec((tokens, states), whole),
-            pl.BlockSpec((tokens, states), whole),
-        ],
-        out_shape=[
-            jax.ShapeDtypeStruct((tokens, channels), bf16),
-            jax.ShapeDtypeStruct((tokens, states), f32),
-            jax.ShapeDtypeStruct((tokens, states), f32),
-            jax.ShapeDtypeStruct((tokens, states), bf16),
-        ],
+        out_specs=pl.BlockSpec(memory_space=pltpu.VMEM),
+        out_shape=pltpu.VMEM((tokens, channels + 3 * states), bf16),
         scratch_shapes=[
             pltpu.VMEM((tokens, 128), f32),
             pltpu.VMEM((heads, tokens), f32),
@@ -325,7 +321,7 @@
         grid=(grid,),
         in_specs=[pl.BlockSpec((tokens, span), lambda i: (0, i))],
         out_specs=pl.BlockSpec((n_c, n_x, 1, part, tokens), lambda i: (0, 0, i, 0, 0)),
-        out_shape=jax.ShapeDtypeStruct((n_c, n_x, grid, part, tokens), bf16),
+        out_shape=pltpu.VMEM((n_c, n_x, grid, part, tokens), bf16),
         scratch_shapes=[pltpu.VMEM((span, span), bf16)],
         compiler_params=budget(12),
         cost_estimate=pl.CostEstimate(
@@ -335,12 +331,18 @@
     )(rows_in).reshape(width, tokens)
 
 
-def finish_body(win_ref, beyond_ref, inner_ref, slope_ref, read_ref, turned_ref, peak_ref, grad_ref, prod_ref):
+def finish_body(
+    terms_ref, beyond_ref, pre_ref, turned_ref, peak_ref, grad_ref, prod_ref
+):
     states = beyond_ref.shape[1]
     half = turned_ref.shape[0] // 2
-    carried = jnp.dot(win_ref[...], beyond_ref[...], preferred_element_type=f32)
-    grad_ref[:, :states] = ((inner_ref[...] + carried) * slope_ref[...]).astype(bf16)
-    grad_ref[:, states:] = read_ref[...]
+    channels = beyond_ref.shape[0]
+    carried = jnp.dot(terms_ref[:, :channels], beyond_ref[...], preferred_element_type=f32)
+    inner = terms_ref[:, channels : channels + states].astype(f32)
+    inner += terms_ref[:, channels + states : channels + 2 * states].astype(f32)
+    grad = (inner + carried) * silu_slope(pre_ref[:, :states].astype(f32))
+    grad_ref[:, :states] = grad.astype(bf16)
+    grad_ref[:, states:] = terms_ref[:, channels + 2 * states :]
     for c in range(2):
         prod_ref[c, :half, :] = jnp.dot(
             turned_ref[c * half : (c + 1) * half, :], grad_ref[...], preferred_element_type=f32
@@ -349,8 +351,8 @@
         prod_ref[c, half:, states:] = jnp.zeros((8, states), bf16)
 
 
-def finish(weighted_in, beyond, inner, slope, grad_read, turned, peak):
-    tokens = weighted_in.shape[0]
+def finish(terms, beyond, pre, turned, peak):
+    tokens = terms.shape[0]
     width = turned.shape[0]
     states = beyond.shape[1]
     return pl.pallas_call(
@@ -361,7 +363,7 @@
         ],
         compiler_params=budget(16),
         name="finish",
-    )(weighted_in, beyond, inner, slope, grad_read, turned, peak)
+    )(terms, beyond, pre, turned, peak)
 
 
 def pair_body(got_ref, sum_ref, peak_ref):
@@ -453,18 +455,18 @@
     own_rows = width // (n_seq * n_z * n_c)
     y, x, z, c = (lax.axis_index(a) for a in SEQ_DP)
 
+    bound = head_size - ((y * n_x + x) * slice_rows) % head_size
+    place = jnp.stack([y, z * n_c + c, bound]).astype(jnp.int32)
     rows_in = layer_input.reshape(tokens, width)
     flat_cot = scan_cotangent.reshape(tokens, channels)
     flat_pre = state_inputs.reshape(tokens, 2 * states)
     decays = log_decay.reshape(heads, tokens)
-    sent = summarize(rows_in, flat_cot, decays, flat_pre, n_seq, states)
+    sent = summarize(place, rows_in, flat_cot, decays, flat_pre, n_seq, states)
     got = exchange(sent, SEQ)
-    bound = head_size - ((y * n_x + x) * slice_rows) % head_size
-    place = jnp.stack([y, z * n_c + c, bound]).astype(jnp.int32)
     slices, seq_peaks = scan_states(got, place, slice_rows)
     beyond = exchange(slices, SEQ).reshape(channels, states)
 
-    weighted_in, inner_write, slope, grad_read = inner_terms(
+    terms = inner_terms(
         flat_cot,
         scan_input.reshape(tokens, channels),
         decays,
@@ -473,9 +475,7 @@
         entry_state.reshape(channels, states),
     )
     turned = turn(rows_in, n_x, n_c)
-    state_input_grad, product = finish(
-        weighted_in, beyond, inner_write, slope, grad_read, turned, seq_peaks
-    )
+    state_input_grad, product = finish(terms, beyond, flat_pre, turned, seq_peaks)
     half, peaks = add_pair(exchange(product, "dp_1"))
     quarter = exchange(half.reshape(n_x, width // (n_x * n_c), 2 * states), "seq_1")
     pieces = add_split(quarter, peaks, n_y * n_z)

time: 113 us -> 111 us (0.982)
  blocking collectives: 45.8 us -> 76.1 us
  waiting for transfers between devices: 27.6 us -> 8.56 us
  starting transfers between devices: 16 us -> 5.53 us
  Pallas kernels: 19.5 us -> 17.2 us
    all_to_all x3 -> x4, blocking collectives: 45.8 us -> 76.1 us  [exchange(): return lax.all_to_all(x, axes, 0, 0, tiled=True)]
    all_to_all x2 -> x1, waiting for transfers between devices: 27.6 us -> 8.56 us  [exchange(): return lax.all_to_all(x, axes, 0, 0, tiled=True)]
    all_to_all x2 -> x1, starting transfers between devices: 16 us -> 5.53 us  [exchange(): return lax.all_to_all(x, axes, 0, 0, tiled=True)]
    pallas_call x1, Pallas kernels: 5.53 us -> 3.45 us  [summarize(): pl.pallas_call(summary_body, grid=(grid,), in_specs=[pl.BlockSpec(memory_...]
  transfers between devices with their start and end apart: 2 -> 1, of which waited for: 2 -> 1; matrix products, arithmetic and copies ran while one was open for 0% -> 0% of each run, Pallas kernels for 8% -> 8%
where the time goes in v4:
time: 111 us; the launch traced here: 110 us
  blocking collectives  76.1 us (69%)
  Pallas kernels  17.2 us (15%)
  waiting for transfers between devices  8.56 us (8%)
  starting transfers between devices  5.53 us (5%)
    all_to_all x4, blocking collectives, exchange(): return lax.all_to_all(x, axes, 0, 0, tiled=True)  76.1 us
    all_to_all x1, waiting for transfers between devices, exchange(): return lax.all_to_all(x, axes, 0, 0, tiled=True)  8.56 us
    pallas_call x1, Pallas kernels, inner_terms(): pl.pallas_call(inner_body, grid=(grid,), in_specs=[pl.BlockSpec((tokens,...  6.41 us
    all_to_all x1, starting transfers between devices, exchange(): return lax.all_to_all(x, axes, 0, 0, tiled=True)  5.53 us
    pallas_call x1, Pallas kernels, summarize(): pl.pallas_call(summary_body, grid=(grid,), in_specs=[pl.BlockSpec(memory_...  3.45 us
    pallas_call x1, Pallas kernels, turn(): pl.pallas_call(turn_body, grid=(grid,), in_specs=[pl.BlockSpec((tokens, s...  2.62 us
  transfers between devices with their start and end apart: 1, of which 1 were waited for; matrix products, arithmetic and copies ran while one was open for 0% of the time, Pallas kernels for 8%

profile of v4, /device:TPU:1, one launch (start us, length us, event | category | flops | bytes accessed | tf_op | source)
XLA Modules:
  0.0 109.8 jit_solution(2698710428099372452)
XLA Ops:
  0.6 0.6 pad_add_fusion.place_ref
  1.3 3.5 %summarize.1 = bf16[32,88,128]{2,1,0:T(8,128)(2,1)S(1)} custom-call(s32[3]{0:T(128)} %pad_add_fusion.place_ref, bf16[256,2560]{1,0:T(8,128)(2,1)} %bitcast.15, bf16[256,2560]{1,0:T(8,128)(2,1)} %bitcast.17, f32[40,256]{1,0:T(8,128)} %bitcast.24, bf16[256,256]{1,0:T(8,128)(2,1)} %bitcast.21), custom_call_target="tpu_custom_call" | custom-call | tf_op jit(solution)/shard_map/summarize/pallas_call | solution.py:127
  4.7 0.0 copy-start.5
  4.7 30.3 %all_to_all.25.got_ref = bf16[32,88,128]{2,1,0:T(8,128)(2,1)S(1)} all-to-all(bf16[32,88,128]{2,1,0:T(8,128)(2,1)S(1)} %summarize.1), channel_id=1, replica_groups=mesh['seq_0'=8,'seq_1'=4,'dp_0'=8,'dp_1'=2] {'seq_0','seq_1'}, dimensions={0} | all-to-all | bytes 1441792 | tf_op jit(solution)/shard_map/all_to_all | solution.py:28
  35.0 0.0 copy-done.5
  35.0 0.0 copy-start
  35.0 1.6 %scan_states.1 = (bf16[32,80,128]{2,1,0:T(8,128)(2,1)}, f32[1,128]{1,0:T(1,128)S(1)}) custom-call(s32[3]{0:T(128)S(1)} %copy-done.5, bf16[32,88,128]{2,1,0:T(8,128)(2,1)S(1)} %all_to_all.25.got_ref), custom_call_target="tpu_custom_call" | custom-call | tf_op jit(solution)/shard_map/scan_states/pallas_call | solution.py:48
  36.6 5.5 %all-to-all-start.1 = ((bf16[32,80,128]{2,1,0:T(8,128)(2,1)}), bf16[32,80,128]{2,1,0:T(8,128)(2,1)S(1)}, u32[]{:S(2)}, u32[]{:S(2)}) async-start(bf16[32,80,128]{2,1,0:T(8,128)(2,1)} %get-tuple-element.8), calls=%async_computation.1 | async-start | bytes 1310720 | tf_op jit(solution)/shard_map/all_to_all | solution.py:28
  42.2 0.0 copy-done
  42.2 0.0 copy-start.1
  42.2 0.0 copy-start.2
  42.2 0.0 copy-start.4
  42.2 0.0 copy-start.6
  42.2 0.0 copy-start.7
  42.2 0.0 copy-start.8
  42.2 2.6 %turn.1 = bf16[2,4,4,80,256]{4,3,2,1,0:T(8,128)(2,1)S(1)} custom-call(bf16[256,2560]{1,0:T(8,128)(2,1)S(1)} %bitcast.16), custom_call_target="tpu_custom_call" | custom-call | flops 1000000000 | bytes 3000000 | tf_op jit(solution)/shard_map/turn/pallas_call | solution.py:319
  44.9 0.0 copy-done.1
  44.9 0.0 copy-done.2
  44.9 0.0 copy-done.4
  44.9 0.0 copy-done.6
  44.9 0.0 copy-done.7
  44.9 0.0 copy-done.8
  44.9 6.4 %inner_terms.1.terms_ref = bf16[256,2944]{1,0:T(8,128)(2,1)S(1)} custom-call(bf16[256,2560]{1,0:T(8,128)(2,1)S(1)} %bitcast.18, bf16[256,2560]{1,0:T(8,128)(2,1)S(1)} %bitcast.26, f32[40,256]{1,0:T(8,128)S(1)} %bitcast.25, f32[40,256]{1,0:T(8,128)S(1)} %bitcast.28, bf16[256,256]{1,0:T(8,128)(2,1)S(1)} %bitcast.22, bf16[2560,128]{1,0:T(8,128)(2,1)S(1)} %bitcast.27), custom_call_target="tpu_custom_call" | custom-call | flops 4000000000 | bytes 6000000 | tf_op jit(solution)/shard_map/inner_terms/pallas_call | solution.py:261
  51.4 8.6 %all-to-all-done.1 = bf16[32,80,128]{2,1,0:T(8,128)(2,1)S(1)} async-done(((bf16[32,80,128]{2,1,0:T(8,128)(2,1)}), bf16[32,80,128]{2,1,0:T(8,128)(2,1)S(1)}, u32[]{:S(2)}, u32[]{:S(2)}) %all-to-all-start.1) | async-done | bytes 655392 | tf_op jit(solution)/shard_map/all_to_all | solution.py:28
  59.9 0.0 copy-start.3
  59.9 0.9 copy-done.3
  60.8 1.6 %finish.1 = (bf16[256,256]{1,0:T(8,128)(2,1)}, bf16[2,1288,256]{2,1,0:T(8,128)(2,1)S(1)}) custom-call(bf16[256,2944]{1,0:T(8,128)(2,1)S(1)} %inner_terms.1.terms_ref, bf16[2560,128]{1,0:T(8,128)(2,1)S(1)} %bitcast.14, bf16[256,256]{1,0:T(8,128)(2,1)S(1)} %bitcast.23, bf16[2560,256]{1,0:T(8,128)(2,1)S(1)} %bitcast.19, f32[1,128]{1,0:T(1,128)S(1)} %get-tuple-element.9.peak_ref), custom_call_target="tpu_custom_call" | custom-call | tf_op jit(solution)/shard_map/finish/pallas_call | solution.py:358
  62.4 8.0 %all_to_all.26.got_ref = bf16[2,1288,256]{2,1,0:T(8,128)(2,1)S(1)} all-to-all(bf16[2,1288,256]{2,1,0:T(8,128)(2,1)S(1)} %get-tuple-element.11), channel_id=1, replica_groups=mesh['seq_0'=8,'seq_1'=4,'dp_0'=8,'dp_1'=2] {'dp_1'}, dimensions={0} | all-to-all | bytes 2637824 | tf_op jit(solution)/shard_map/all_to_all | solution.py:28
  70.4 0.2 add_pair.1
  70.5 13.4 %all_to_all.27.got_ref = bf16[4,320,256]{2,1,0:T(8,128)(2,1)S(1)} all-to-all(bf16[4,320,256]{2,1,0:T(8,128)(2,1)S(1)} %bitcast.20), channel_id=1, replica_groups=mesh['seq_0'=8,'seq_1'=4,'dp_0'=8,'dp_1'=2] {'seq_1'}, dimensions={0} | all-to-all | bytes 1310720 | tf_op jit(solution)/shard_map/all_to_all | solution.py:28
  83.9 0.2 add_split.1
  84.1 24.5 %all_to_all.28.got_ref = bf16[64,8,256]{2,1,0:T(8,128)(2,1)S(1)} all-to-all(bf16[64,8,256]{2,1,0:T(8,128)(2,1)S(1)} %add_split.1), channel_id=1, replica_groups=mesh['seq_0'=8,'seq_1'=4,'dp_0'=8,'dp_1'=2] {'seq_0','dp_0'}, dimensions={0} | all-to-all | bytes 524288 | tf_op jit(solution)/shard_map/all_to_all | solution.py:28
  108.5 1.2 %close.1 = f32[5,256]{1,0:T(8,128)} custom-call(s32[3]{0:T(128)S(1)} %copy-done.5, bf16[64,8,256]{2,1,0:T(8,128)(2,1)S(1)} %all_to_all.28.got_ref), custom_call_target="tpu_custom_call" | custom-call | tf_op jit(solution)/shard_map/close/pallas_call | solution.py:432
Async XLA Ops:
  4.7 30.3 %copy-start.5 = (s32[3]{0:T(128)S(1)}, s32[3]{0:T(128)}, u32[]{:S(2)}) copy-start(s32[3]{0:T(128)} %pad_add_fusion.place_ref) | copy-start | bytes 40
  35.0 7.2 %copy-start = (bf16[1,256,2560]{2,1,0:T(8,128)(2,1)S(1)}, bf16[1,256,2560]{2,1,0:T(8,128)(2,1)}, u32[]{:S(2)}) copy-start(bf16[1,256,2560]{2,1,0:T(8,128)(2,1)} %param.7) | copy-start | bytes 3932164
  36.6 23.3 %all-to-all-start.1 = ((bf16[32,80,128]{2,1,0:T(8,128)(2,1)}), bf16[32,80,128]{2,1,0:T(8,128)(2,1)S(1)}, u32[]{:S(2)}, u32[]{:S(2)}) async-start(bf16[32,80,128]{2,1,0:T(8,128)(2,1)} %get-tuple-element.8), calls=%async_computation.1 | async-start | bytes 1310720 | tf_op jit(solution)/shard_map/all_to_all | solution.py:28
  42.2 2.7 %copy-start.1 = (bf16[1,256,2560]{2,1,0:T(8,128)(2,1)S(1)}, bf16[1,256,2560]{2,1,0:T(8,128)(2,1)}, u32[]{:S(2)}) copy-start(bf16[1,256,2560]{2,1,0:T(8,128)(2,1)} %param.9) | copy-start | bytes 3932164
  42.2 2.7 %copy-start.2 = (bf16[1,256,256]{2,1,0:T(8,128)(2,1)S(1)}, bf16[1,256,256]{2,1,0:T(8,128)(2,1)}, u32[]{:S(2)}) copy-start(bf16[1,256,256]{2,1,0:T(8,128)(2,1)} %param.12) | copy-start | bytes 393220
  42.2 2.7 %copy-start.4 = (f32[1,40,256]{2,1,0:T(8,128)S(1)}, f32[1,40,256]{2,1,0:T(8,128)}, u32[]{:S(2)}) copy-start(f32[1,40,256]{2,1,0:T(8,128)} %param.11) | copy-start | bytes 122884
  42.2 2.7 %copy-start.6 = (bf16[1,256,2560]{2,1,0:T(8,128)(2,1)S(1)}, bf16[1,256,2560]{2,1,0:T(8,128)(2,1)}, u32[]{:S(2)}) copy-start(bf16[1,256,2560]{2,1,0:T(8,128)(2,1)} %param.8) | copy-start | bytes 3932164
  42.2 2.7 %copy-start.7 = (bf16[1,1,2560,128]{3,2,1,0:T(8,128)(2,1)S(1)}, bf16[1,1,2560,128]{3,2,1,0:T(8,128)(2,1)}, u32[]{:S(2)}) copy-start(bf16[1,1,2560,128]{3,2,1,0:T(8,128)(2,1)} %param.13) | copy-start | bytes 1966084
  42.2 2.7 %copy-start.8 = (f32[1,40,256]{2,1,0:T(8,128)S(1)}, f32[1,40,256]{2,1,0:T(8,128)}, u32[]{:S(2)}) copy-start(f32[1,40,256]{2,1,0:T(8,128)} %param.10) | copy-start | bytes 122884
  59.9 0.9 copy-start.3

commit v5 on v4

--- a/solution.py
+++ b/solution.py
@@ -1,3 +1,5 @@
+import functools
+
 import jax
 import jax.numpy as jnp
 from jax import lax
@@ -28,10 +30,16 @@
     return lax.all_to_all(x, axes, 0, 0, tiled=True)
 
 
-def scan_body(place_ref, got_ref, out_ref, peak_ref):
+def swapped(x):
+    return lax.ppermute(x, "dp_1", [(0, 1), (1, 0)])
+
+
+def scan_body(head_size, got_ref, out_ref, peak_ref):
     blocks, _, states = got_ref.shape
     rows = out_ref.shape[1]
-    first = lax.broadcasted_iota(jnp.int32, (rows, states), 0) < place_ref[2]
+    slot = lax.axis_index("seq_0") * lax.axis_size("seq_1") + lax.axis_index("seq_1")
+    bound = head_size - lax.rem(slot * rows, head_size)
+    first = lax.broadcasted_iota(jnp.int32, (rows, states), 0) < bound
     state = jnp.zeros((rows, states), f32)
     peak = jnp.zeros((1, states), f32)
     for k in reversed(range(blocks)):
@@ -43,28 +51,20 @@
     peak_ref[...] = peak
 
 
-def scan_states(got, place, rows):
+def scan_states(got, rows, head_size):
     blocks, _, states = got.shape
     return pl.pallas_call(
-        scan_body,
-        in_specs=[
-            pl.BlockSpec(memory_space=pltpu.SMEM),
-            pl.BlockSpec(memory_space=pltpu.VMEM),
-        ],
-        out_specs=[
-            pl.BlockSpec(memory_space=pltpu.VMEM),
-            pl.BlockSpec(memory_space=pltpu.VMEM),
-        ],
+        functools.partial(scan_body, head_size),
         out_shape=[
             pltpu.VMEM((blocks, rows, states), bf16),
             jax.ShapeDtypeStruct((1, states), f32),
         ],
         compiler_params=budget(8),
         name="scan_states",
-    )(place, got)
-
-
-def summary_body(place_ref, in_ref, cot_ref, decay_ref, pre_ref, sent_ref, reads_ref, spread_ref):
+    )(got)
+
+
+def summary_body(in_ref, cot_ref, decay_ref, pre_ref, sent_ref, reads_ref, spread_ref):
     step = pl.program_id(0)
     heads, tokens = decay_ref.shape
     total, rows_all, states = sent_ref.shape
@@ -117,7 +117,7 @@
         sent_ref[step * chunks + d, rows:, :] = extra.astype(bf16)
 
 
-def summarize(place, rows_in, cots, decays, pre, n_seq, head_states):
+def summarize(rows_in, cots, decays, pre, n_seq, head_states):
     tokens, channels = cots.shape
     heads = decays.shape[0]
     states = head_states
@@ -128,7 +128,6 @@
         summary_body,
         grid=(grid,),
         in_specs=[
-            pl.BlockSpec(memory_space=pltpu.SMEM),
             pl.BlockSpec((tokens, span), lambda i: (0, i)),
             pl.BlockSpec((tokens, span), lambda i: (0, i)),
             pl.BlockSpec((heads, tokens), lambda i: (0, 0)),
@@ -142,7 +141,7 @@
         ],
         compiler_params=budget(60),
         name="summarize",
-    )(place, rows_in, cots, decays, pre)
+    )(rows_in, cots, decays, pre)
 
 
 def inner_body(
@@ -241,14 +240,16 @@
         active = (value / (1.0 + jnp.exp(-value))).astype(bf16)
         mixed = mix_ref[...].astype(bf16)
         inner = lax.dot_general(mixed, active[:, states:], both, preferred_element_type=f32)
-        high = inner.astype(bf16)
-        channels = out_ref.shape[1] - 3 * states
-        out_ref[:, channels : channels + states] = high
-        low_part = (inner - high.astype(f32)).astype(bf16)
-        out_ref[:, channels + states : channels + 2 * states] = low_part
         read = carry_ref[...] + jnp.dot(mixed, active[:, :states], preferred_element_type=f32)
-        read = read * silu_slope(value[:, states:])
-        out_ref[:, channels + 2 * states :] = read.astype(bf16)
+        slope = silu_slope(value)
+        parts = []
+        for part in (inner, slope[:, :states]):
+            high = part.astype(bf16)
+            parts += [high, (part - high.astype(f32)).astype(bf16)]
+        parts.append((read * slope[:, states:]).astype(bf16))
+        at = out_ref.shape[1] - len(parts) * states
+        for k, part in enumerate(parts):
+            out_ref[:, at + k * states : at + (k + 1) * states] = part
 
 
 def inner_terms(cots, ins, decays, steps, pre, entry):
@@ -270,7 +271,7 @@
             pl.BlockSpec((span, states), lambda i: (i, 0)),
         ],
         out_specs=pl.BlockSpec(memory_space=pltpu.VMEM),
-        out_shape=pltpu.VMEM((tokens, channels + 3 * states), bf16),
+        out_shape=pltpu.VMEM((tokens, channels + 5 * states), bf16),
         scratch_shapes=[
             pltpu.VMEM((tokens, 128), f32),
             pltpu.VMEM((heads, tokens), f32),
@@ -286,29 +287,33 @@
     )(cots, ins, decays, steps, pre, entry)
 
 
-def turn_body(in_ref, out_ref, hot_ref):
-    n_c, n_x, _, part, _ = out_ref.shape
+def turn_body(in_ref, own_ref, other_ref, hot_ref, turned_ref):
+    n_x, _, part, _ = own_ref.shape
     span = in_ref.shape[1]
-    n_z, own = 8, part // 16
+    n_z, n_c = lax.axis_size("dp_0"), lax.axis_size("dp_1")
+    n_y = span // (n_x * part)
+    own = part // (n_y * n_z)
 
     @pl.when(pl.program_id(0) == 0)
     def _():
         row = lax.broadcasted_iota(jnp.int32, (span, 1), 0)
         i, row = lax.rem(row, own), lax.div(row, own)
         z, row = lax.rem(row, n_z), lax.div(row, n_z)
-        y, row = lax.rem(row, 2), lax.div(row, 2)
+        y, row = lax.rem(row, n_y), lax.div(row, n_y)
         x, c = lax.rem(row, n_x), lax.div(row, n_x)
         source = (((y * n_x + x) * n_z + z) * n_c + c) * own + i
         lane = lax.broadcasted_iota(jnp.int32, (span, span), 1)
         hot_ref[...] = jnp.where(lane == source, 1.0, 0.0).astype(bf16)
 
-    turned = lax.dot_general(
+    turned_ref[...] = lax.dot_general(
         hot_ref[...], in_ref[...], (((1,), (1,)), ((), ())), preferred_element_type=f32
     ).astype(bf16)
-    for c in range(n_c):
-        for x in range(n_x):
-            at = (c * n_x + x) * part
-            out_ref[c, x, 0] = turned[at : at + part]
+    mine = lax.axis_index("dp_1")
+    for x in range(n_x):
+        at = pl.multiple_of((mine * n_x + x) * part, 16)
+        own_ref[x, 0] = turned_ref[pl.ds(at, part), :]
+        at = pl.multiple_of(((1 - mine) * n_x + x) * part, 16)
+        other_ref[x, 0] = turned_ref[pl.ds(at, part), :]
 
 
 def turn(rows_in, n_x, n_c):
@@ -316,73 +321,88 @@
     grid = 4
     span = width // grid
     part = span // (n_x * n_c)
-    return pl.pallas_call(
+    block = pl.BlockSpec((n_x, 1, part, tokens), lambda i: (0, i, 0, 0))
+    shape = (n_x, grid, part, tokens)
+    own, other = pl.pallas_call(
         turn_body,
         grid=(grid,),
         in_specs=[pl.BlockSpec((tokens, span), lambda i: (0, i))],
-        out_specs=pl.BlockSpec((n_c, n_x, 1, part, tokens), lambda i: (0, 0, i, 0, 0)),
-        out_shape=pltpu.VMEM((n_c, n_x, grid, part, tokens), bf16),
-        scratch_shapes=[pltpu.VMEM((span, span), bf16)],
+        out_specs=[block, block],
+        out_shape=[pltpu.VMEM(shape, bf16), pltpu.VMEM(shape, bf16)],
+        scratch_shapes=[pltpu.VMEM((span, span), bf16), pltpu.VMEM((span, tokens), bf16)],
         compiler_params=budget(12),
         cost_estimate=pl.CostEstimate(
             flops=10**9, transcendentals=0, bytes_accessed=3 * 10**6
         ),
         name="turn",
-    )(rows_in).reshape(width, tokens)
-
-
-def finish_body(
-    terms_ref, beyond_ref, pre_ref, turned_ref, peak_ref, grad_ref, prod_ref
-):
-    states = beyond_ref.shape[1]
-    half = turned_ref.shape[0] // 2
-    channels = beyond_ref.shape[0]
+    )(rows_in)
+    return own.reshape(width // n_c, tokens), other.reshape(width // n_c, tokens)
+
+
+def finish_body(terms_ref, beyond_ref, peak_ref, grad_ref, send_ref):
+    channels, states = beyond_ref.shape
+    tokens = terms_ref.shape[0]
     carried = jnp.dot(terms_ref[:, :channels], beyond_ref[...], preferred_element_type=f32)
-    inner = terms_ref[:, channels : channels + states].astype(f32)
-    inner += terms_ref[:, channels + states : channels + 2 * states].astype(f32)
-    grad = (inner + carried) * silu_slope(pre_ref[:, :states].astype(f32))
-    grad_ref[:, :states] = grad.astype(bf16)
-    grad_ref[:, states:] = terms_ref[:, channels + 2 * states :]
-    for c in range(2):
-        prod_ref[c, :half, :] = jnp.dot(
-            turned_ref[c * half : (c + 1) * half, :], grad_ref[...], preferred_element_type=f32
-        ).astype(bf16)
-        prod_ref[c, half:, :states] = jnp.broadcast_to(peak_ref[...], (8, states)).astype(bf16)
-        prod_ref[c, half:, states:] = jnp.zeros((8, states), bf16)
-
-
-def finish(terms, beyond, pre, turned, peak):
+
+    def part(k):
+        return terms_ref[:, channels + k * states : channels + (k + 1) * states]
+
+    def whole(k):
+        return part(k).astype(f32) + part(k + 1).astype(f32)
+
+    send_ref[:tokens, :states] = ((whole(0) + carried) * whole(2)).astype(bf16)
+    send_ref[:tokens, states:] = part(4)
+    send_ref[tokens:, :states] = jnp.broadcast_to(peak_ref[...], (8, states)).astype(bf16)
+    send_ref[tokens:, states:] = jnp.zeros((8, states), bf16)
+    grad_ref[...] = send_ref[:tokens, :]
+
+
+def finish(terms, beyond, peak):
     tokens = terms.shape[0]
-    width = turned.shape[0]
     states = beyond.shape[1]
     return pl.pallas_call(
         finish_body,
         out_shape=[
             jax.ShapeDtypeStruct((tokens, 2 * states), bf16),
-            jax.ShapeDtypeStruct((2, width // 2 + 8, 2 * states), bf16),
+            jax.ShapeDtypeStruct((tokens + 8, 2 * states), bf16),
         ],
         compiler_params=budget(16),
         name="finish",
-    )(terms, beyond, pre, turned, peak)
-
-
-def pair_body(got_ref, sum_ref, peak_ref):
-    half = sum_ref.shape[0]
-    sum_ref[...] = (got_ref[0, :half].astype(f32) + got_ref[1, :half].astype(f32)).astype(bf16)
-    peak_ref[...] = jnp.maximum(got_ref[0, half:].astype(f32), got_ref[1, half:].astype(f32))
-
-
-def add_pair(got):
-    _, rows, cols = got.shape
-    return pl.pallas_call(
-        pair_body,
+    )(terms, beyond, peak)
+
+
+def product_body(own_ref, mine_ref, other_ref, got_ref, half_ref, peak_ref, held_ref, sem):
+    tokens = own_ref.shape[1]
+    copy = pltpu.make_async_copy(other_ref, held_ref, sem)
+    copy.start()
+    total = jnp.dot(own_ref[...], mine_ref[:tokens, :], preferred_element_type=f32)
+    copy.wait()
+    total += jnp.dot(held_ref[...], got_ref[:tokens, :], preferred_element_type=f32)
+    half_ref[...] = total.astype(bf16)
+    peak_ref[...] = jnp.maximum(
+        mine_ref[tokens:, :].astype(f32), got_ref[tokens:, :].astype(f32)
+    )
+
+
+def multiply(own, mine, other, got):
+    rows = own.shape[0]
+    cols = mine.shape[1]
+    return pl.pallas_call(
+        product_body,
         out_shape=[
-            jax.ShapeDtypeStruct((rows - 8, cols), bf16),
+            jax.ShapeDtypeStruct((rows, cols), bf16),
             jax.ShapeDtypeStruct((8, cols), f32),
         ],
-        compiler_params=budget(8),
-        name="add_pair",
-    )(got)
+        in_specs=[
+            pl.BlockSpec(memory_space=pltpu.VMEM),
+            pl.BlockSpec(memory_space=pltpu.VMEM),
+            pl.BlockSpec(memory_space=pl.ANY),
+            pl.BlockSpec(memory_space=pltpu.VMEM),
+        ],
+        scratch_shapes=[pltpu.VMEM(other.shape, bf16), pltpu.SemaphoreType.DMA],
+        compiler_params=budget(16),
+        name="multiply",
+    )(own, mine, other, got)
 
 
 def split_body(got_ref, peak_ref, out_ref, sum_ref):
@@ -411,34 +431,34 @@
     )(got, peak)
 
 
-def close_body(place_ref, got_ref, out_ref):
+def close_body(got_ref, out_ref):
     count, rows, cols = got_ref.shape
     own = out_ref.shape[0]
     total = got_ref[0].astype(f32)
     for k in range(1, count):
         total += got_ref[k].astype(f32)
     peak = jnp.zeros((rows, cols), f32)
-    for z in range(8):
-        peak = jnp.maximum(peak, got_ref[place_ref[0] * 8 + z].astype(f32))
+    n_z = lax.axis_size("dp_0")
+    at = lax.axis_index("seq_0") * n_z
+    pair = lax.axis_size("dp_1")
+    spot = (lax.axis_index("dp_0") * pair + lax.axis_index("dp_1")) * own
+    for z in range(n_z):
+        peak = jnp.maximum(peak, got_ref[at + z].astype(f32))
     lane = lax.broadcasted_iota(jnp.int32, (rows, cols), 1)
     row = lax.broadcasted_iota(jnp.int32, (rows, cols), 0)
     line = jnp.broadcast_to(peak[own : own + 1, :], (rows, cols))
-    column = jnp.sum(jnp.where(lane == place_ref[1] * own + row, line, 0.0), axis=1, keepdims=True)
+    column = jnp.sum(jnp.where(lane == spot + row, line, 0.0), axis=1, keepdims=True)
     out_ref[...] = (total * (1.0 / (column + epsilon)))[:own]
 
 
-def close(got, place, own):
+def close(got, own):
     cols = got.shape[2]
     return pl.pallas_call(
         close_body,
-        in_specs=[
-            pl.BlockSpec(memory_space=pltpu.SMEM),
-            pl.BlockSpec(memory_space=pltpu.VMEM),
-        ],
         out_shape=jax.ShapeDtypeStruct((own, cols), f32),
         compiler_params=budget(4),
         name="close",
-    )(place, got)
+    )(got)
 
 
 def on_device(
@@ -453,17 +473,14 @@
     n_seq = n_y * n_x
     slice_rows = channels // n_seq
     own_rows = width // (n_seq * n_z * n_c)
-    y, x, z, c = (lax.axis_index(a) for a in SEQ_DP)
-
-    bound = head_size - ((y * n_x + x) * slice_rows) % head_size
-    place = jnp.stack([y, z * n_c + c, bound]).astype(jnp.int32)
+
     rows_in = layer_input.reshape(tokens, width)
     flat_cot = scan_cotangent.reshape(tokens, channels)
     flat_pre = state_inputs.reshape(tokens, 2 * states)
     decays = log_decay.reshape(heads, tokens)
-    sent = summarize(place, rows_in, flat_cot, decays, flat_pre, n_seq, states)
+    sent = summarize(rows_in, flat_cot, decays, flat_pre, n_seq, states)
     got = exchange(sent, SEQ)
-    slices, seq_peaks = scan_states(got, place, slice_rows)
+    slices, seq_peaks = scan_states(got, slice_rows, head_size)
     beyond = exchange(slices, SEQ).reshape(channels, states)
 
     terms = inner_terms(
@@ -474,13 +491,14 @@
         flat_pre,
         entry_state.reshape(channels, states),
     )
-    turned = turn(rows_in, n_x, n_c)
-    state_input_grad, product = finish(terms, beyond, flat_pre, turned, seq_peaks)
-    half, peaks = add_pair(exchange(product, "dp_1"))
+    kept, given = turn(rows_in, n_x, n_c)
+    taken = swapped(given)
+    state_input_grad, sums = finish(terms, beyond, seq_peaks)
+    half, peaks = multiply(kept, sums, taken, swapped(sums))
     quarter = exchange(half.reshape(n_x, width // (n_x * n_c), 2 * states), "seq_1")
     pieces = add_split(quarter, peaks, n_y * n_z)
     arrived = exchange(pieces, ("seq_0", "dp_0"))
-    return state_input_grad[None], close(arrived, place, own_rows)
+    return state_input_grad[None], close(arrived, own_rows)
 
 
 def solution(mesh):

time: 111 us -> 108 us (0.973)
  starting transfers between devices: 5.53 us -> 15 us
  blocking collectives: 76.1 us -> 68.1 us
  waiting for transfers between devices: 8.56 us -> 4.46 us
    ppermute x0 -> x2, starting transfers between devices: none -> 9.46 us  [swapped(): return lax.ppermute(x, 'dp_1', [(0, 1), (1, 0)])]
    all_to_all x4 -> x3, blocking collectives: 76.1 us -> 68.1 us  [exchange(): return lax.all_to_all(x, axes, 0, 0, tiled=True)]
    all_to_all x1, waiting for transfers between devices: 8.56 us -> 3.5 us  [exchange(): return lax.all_to_all(x, axes, 0, 0, tiled=True)]
  transfers between devices with their start and end apart: 1 -> 3, of which waited for: 1 -> 2; matrix products, arithmetic and copies ran while one was open for 0% -> 0% of each run, Pallas kernels for 8% -> 11%
where the time goes in v5:
time: 108 us; the launch traced here: 107 us
  blocking collectives  68.1 us (63%)
  Pallas kernels  18.3 us (17%)
  starting transfers between devices  15 us (14%)
  waiting for transfers between devices  4.46 us (4%)
    all_to_all x3, blocking collectives, exchange(): return lax.all_to_all(x, axes, 0, 0, tiled=True)  68.1 us
    ppermute x2, starting transfers between devices, swapped(): return lax.ppermute(x, 'dp_1', [(0, 1), (1, 0)])  9.46 us
    pallas_call x1, Pallas kernels, inner_terms(): pl.pallas_call(inner_body, grid=(grid,), in_specs=[pl.BlockSpec((tokens,...  6.42 us
    all_to_all x1, starting transfers between devices, exchange(): return lax.all_to_all(x, axes, 0, 0, tiled=True)  5.52 us
    pallas_call x1, Pallas kernels, turn(): pl.pallas_call(turn_body, grid=(grid,), in_specs=[pl.BlockSpec((tokens, s...  3.72 us
    all_to_all x1, waiting for transfers between devices, exchange(): return lax.all_to_all(x, axes, 0, 0, tiled=True)  3.5 us
    pallas_call x1, Pallas kernels, summarize(): pl.pallas_call(summary_body, grid=(grid,), in_specs=[pl.BlockSpec((tokens...  3.46 us
  transfers between devices with their start and end apart: 3, of which 2 were waited for; matrix products, arithmetic and copies ran while one was open for 0% of the time, Pallas kernels for 11%

profile of v5, /device:TPU:1, one launch (start us, length us, event | category | flops | bytes accessed | tf_op | source)
XLA Modules:
  0.0 106.7 jit_solution(15961125050973623678)
XLA Ops:
  0.6 3.5 %summarize.1 = bf16[32,88,128]{2,1,0:T(8,128)(2,1)S(1)} custom-call(bf16[256,2560]{1,0:T(8,128)(2,1)} %bitcast.13, bf16[256,2560]{1,0:T(8,128)(2,1)} %bitcast.15, f32[40,256]{1,0:T(8,128)} %bitcast.21, bf16[256,256]{1,0:T(8,128)(2,1)} %bitcast.19), custom_call_target="tpu_custom_call" | custom-call | tf_op jit(solution)/shard_map/summarize/pallas_call | solution.py:127
  4.1 30.3 %all_to_all.20.got_ref = bf16[32,88,128]{2,1,0:T(8,128)(2,1)S(1)} all-to-all(bf16[32,88,128]{2,1,0:T(8,128)(2,1)S(1)} %summarize.1), channel_id=1, replica_groups=mesh['seq_0'=8,'seq_1'=4,'dp_0'=8,'dp_1'=2] {'seq_0','seq_1'}, dimensions={0} | all-to-all | bytes 1441792 | tf_op jit(solution)/shard_map/all_to_all | solution.py:30
  34.4 0.0 copy-start
  34.4 1.1 %scan_states.1 = (bf16[32,80,128]{2,1,0:T(8,128)(2,1)}, f32[1,128]{1,0:T(1,128)S(1)}) custom-call(bf16[32,88,128]{2,1,0:T(8,128)(2,1)S(1)} %all_to_all.20.got_ref), custom_call_target="tpu_custom_call" | custom-call | tf_op jit(solution)/shard_map/scan_states/pallas_call | solution.py:56
  35.5 5.5 %all-to-all-start.1 = ((bf16[32,80,128]{2,1,0:T(8,128)(2,1)}), bf16[32,80,128]{2,1,0:T(8,128)(2,1)S(1)}, u32[]{:S(2)}, u32[]{:S(2)}) async-start(bf16[32,80,128]{2,1,0:T(8,128)(2,1)} %get-tuple-element.10), calls=%async_computation.1 | async-start | bytes 1310720 | tf_op jit(solution)/shard_map/all_to_all | solution.py:30
  41.0 0.0 copy-done
  41.0 0.0 copy-start.1
  41.0 0.0 copy-start.2
  41.0 0.0 copy-start.3
  41.0 0.0 copy-start.4
  41.0 0.0 copy-start.5
  41.1 0.0 copy-start.6
  41.1 3.7 %turn.1 = (bf16[4,4,80,256]{3,2,1,0:T(8,128)(2,1)S(1)}, bf16[4,4,80,256]{3,2,1,0:T(8,128)(2,1)}) custom-call(bf16[256,2560]{1,0:T(8,128)(2,1)S(1)} %bitcast.14), custom_call_target="tpu_custom_call" | custom-call | flops 1000000000 | bytes 3000000 | tf_op jit(solution)/shard_map/turn/pallas_call | solution.py:326
  44.8 4.0 %collective-permute-start = (bf16[1280,256]{1,0:T(8,128)(2,1)}, bf16[1280,256]{1,0:T(8,128)(2,1)}, u32[]{:S(2)}, u32[]{:S(2)}) collective-permute-start(bf16[1280,256]{1,0:T(8,128)(2,1)} %bitcast.10), channel_id=1, source_target_pairs={{0,1},{1,0},{2,3},{3,2},{4,5},{5,4},{6,7},{7,6},{8,9},{9,8},{10,11... | collective-permute-start | bytes 1966088 | tf_op jit(solution)/shard_map/ppermute | solution.py:34
  48.7 0.0 copy-done.1
  48.8 0.0 copy-done.2
  48.8 0.0 copy-done.3
  48.8 0.0 copy-done.4
  48.8 0.0 copy-done.5
  48.8 0.0 copy-done.6
  48.8 6.4 %inner_terms.1.terms_ref = bf16[256,3200]{1,0:T(8,128)(2,1)S(1)} custom-call(bf16[256,2560]{1,0:T(8,128)(2,1)S(1)} %bitcast.16, bf16[256,2560]{1,0:T(8,128)(2,1)S(1)} %bitcast.23, f32[40,256]{1,0:T(8,128)S(1)} %bitcast.22, f32[40,256]{1,0:T(8,128)S(1)} %bitcast.25, bf16[256,256]{1,0:T(8,128)(2,1)S(1)} %bitcast.20, bf16[2560,128]{1,0:T(8,128)(2,1)S(1)} %bitcast.24), custom_call_target="tpu_custom_call" | custom-call | flops 4000000000 | bytes 6000000 | tf_op jit(solution)/shard_map/inner_terms/pallas_call | solution.py:262
  55.2 3.5 %all-to-all-done.1 = bf16[32,80,128]{2,1,0:T(8,128)(2,1)S(1)} async-done(((bf16[32,80,128]{2,1,0:T(8,128)(2,1)}), bf16[32,80,128]{2,1,0:T(8,128)(2,1)S(1)}, u32[]{:S(2)}, u32[]{:S(2)}) %all-to-all-start.1) | async-done | bytes 655392 | tf_op jit(solution)/shard_map/all_to_all | solution.py:30
  58.7 1.2 %finish.1 = (bf16[256,256]{1,0:T(8,128)(2,1)}, bf16[264,256]{1,0:T(8,128)(2,1)S(1)}) custom-call(bf16[256,3200]{1,0:T(8,128)(2,1)S(1)} %inner_terms.1.terms_ref, bf16[2560,128]{1,0:T(8,128)(2,1)S(1)} %bitcast.12, f32[1,128]{1,0:T(1,128)S(1)} %get-tuple-element.11.peak_ref), custom_call_target="tpu_custom_call" | custom-call | tf_op jit(solution)/shard_map/finish/pallas_call | solution.py:363
  59.9 5.5 %collective-permute-start.1 = (bf16[264,256]{1,0:T(8,128)(2,1)S(1)}, bf16[264,256]{1,0:T(8,128)(2,1)S(1)}, u32[]{:S(2)}, u32[]{:S(2)}) collective-permute-start(bf16[264,256]{1,0:T(8,128)(2,1)S(1)} %get-tuple-element.14.mine_ref), channel_id=1, source_target_pairs={{0,1},{1,0},{2,3},{3,2},{4,5},{5,4},{6,7},{7,6},{8,9},{9,8},{10,11... | collective-permute-start | bytes 405512 | tf_op jit(solution)/shard_map/ppermute | solution.py:34
  65.4 0.0 collective-permute-done.other_ref
  65.4 1.0 collective-permute-done.1.got_ref
  66.4 1.6 %multiply.1 = (bf16[1280,256]{1,0:T(8,128)(2,1)S(1)}, f32[8,256]{1,0:T(8,128)S(1)}) custom-call(bf16[1280,256]{1,0:T(8,128)(2,1)S(1)} %bitcast.17, bf16[264,256]{1,0:T(8,128)(2,1)S(1)} %get-tuple-element.14.mine_ref, bf16[1280,256]{1,0:T(8,128)(2,1)} %collective-permute-done.other_ref, bf16[264,256]{1,0:T(8,128)(2,1)S(1)} %collective-permute-done.1.got_ref), custom_call_target="tpu_custom_call" | custom-call | tf_op jit(solution)/shard_map/multiply/pallas_call | solution.py:390
  68.0 13.4 %all_to_all.21.got_ref = bf16[4,320,256]{2,1,0:T(8,128)(2,1)S(1)} all-to-all(bf16[4,320,256]{2,1,0:T(8,128)(2,1)S(1)} %bitcast.18), channel_id=1, replica_groups=mesh['seq_0'=8,'seq_1'=4,'dp_0'=8,'dp_1'=2] {'seq_1'}, dimensions={0} | all-to-all | bytes 1310720 | tf_op jit(solution)/shard_map/all_to_all | solution.py:30
  81.4 0.2 add_split.1
  81.6 24.5 %all_to_all.22.got_ref = bf16[64,8,256]{2,1,0:T(8,128)(2,1)S(1)} all-to-all(bf16[64,8,256]{2,1,0:T(8,128)(2,1)S(1)} %add_split.1), channel_id=1, replica_groups=mesh['seq_0'=8,'seq_1'=4,'dp_0'=8,'dp_1'=2] {'seq_0','dp_0'}, dimensions={0} | all-to-all | bytes 524288 | tf_op jit(solution)/shard_map/all_to_all | solution.py:30
  106.0 0.7 close.1
Async XLA Ops:
  34.4 6.6 %copy-start = (bf16[1,256,2560]{2,1,0:T(8,128)(2,1)S(1)}, bf16[1,256,2560]{2,1,0:T(8,128)(2,1)}, u32[]{:S(2)}) copy-start(bf16[1,256,2560]{2,1,0:T(8,128)(2,1)} %param.7) | copy-start | bytes 3932164
  35.5 23.3 %all-to-all-start.1 = ((bf16[32,80,128]{2,1,0:T(8,128)(2,1)}), bf16[32,80,128]{2,1,0:T(8,128)(2,1)S(1)}, u32[]{:S(2)}, u32[]{:S(2)}) async-start(bf16[32,80,128]{2,1,0:T(8,128)(2,1)} %get-tuple-element.10), calls=%async_computation.1 | async-start | bytes 1310720 | tf_op jit(solution)/shard_map/all_to_all | solution.py:30
  41.0 7.8 %copy-start.1 = (bf16[1,256,2560]{2,1,0:T(8,128)(2,1)S(1)}, bf16[1,256,2560]{2,1,0:T(8,128)(2,1)}, u32[]{:S(2)}) copy-start(bf16[1,256,2560]{2,1,0:T(8,128)(2,1)} %param.9) | copy-start | bytes 3932164
  41.0 7.8 %copy-start.2 = (bf16[1,256,256]{2,1,0:T(8,128)(2,1)S(1)}, bf16[1,256,256]{2,1,0:T(8,128)(2,1)}, u32[]{:S(2)}) copy-start(bf16[1,256,256]{2,1,0:T(8,128)(2,1)} %param.12) | copy-start | bytes 393220
  41.0 7.8 %copy-start.3 = (f32[1,40,256]{2,1,0:T(8,128)S(1)}, f32[1,40,256]{2,1,0:T(8,128)}, u32[]{:S(2)}) copy-start(f32[1,40,256]{2,1,0:T(8,128)} %param.11) | copy-start | bytes 122884
  41.0 7.7 %copy-start.4 = (bf16[1,256,2560]{2,1,0:T(8,128)(2,1)S(1)}, bf16[1,256,2560]{2,1,0:T(8,128)(2,1)}, u32[]{:S(2)}) copy-start(bf16[1,256,2560]{2,1,0:T(8,128)(2,1)} %param.8) | copy-start | bytes 3932164
  41.0 7.7 %copy-start.5 = (bf16[1,1,2560,128]{3,2,1,0:T(8,128)(2,1)S(1)}, bf16[1,1,2560,128]{3,2,1,0:T(8,128)(2,1)}, u32[]{:S(2)}) copy-start(bf16[1,1,2560,128]{3,2,1,0:T(8,128)(2,1)} %param.13) | copy-start | bytes 1966084
  41.1 7.7 %copy-start.6 = (f32[1,40,256]{2,1,0:T(8,128)S(1)}, f32[1,40,256]{2,1,0:T(8,128)}, u32[]{:S(2)}) copy-start(f32[1,40,256]{2,1,0:T(8,128)} %param.10) | copy-start | bytes 122884
  44.8 20.6 %collective-permute-start = (bf16[1280,256]{1,0:T(8,128)(2,1)}, bf16[1280,256]{1,0:T(8,128)(2,1)}, u32[]{:S(2)}, u32[]{:S(2)}) collective-permute-start(bf16[1280,256]{1,0:T(8,128)(2,1)} %bitcast.10), channel_id=1, source_target_pairs={{0,1},{1,0},{2,3},{3,2},{4,5},{5,4},{6,7},{7,6},{8,9},{9,8},{10,11... | collective-permute-start | bytes 1966088 | tf_op jit(solution)/shard_map/ppermute | solution.py:34
  59.9 6.5 %collective-permute-start.1 = (bf16[264,256]{1,0:T(8,128)(2,1)S(1)}, bf16[264,256]{1,0:T(8,128)(2,1)S(1)}, u32[]{:S(2)}, u32[]{:S(2)}) collective-permute-start(bf16[264,256]{1,0:T(8,128)(2,1)S(1)} %get-tuple-element.14.mine_ref), channel_id=1, source_target_pairs={{0,1},{1,0},{2,3},{3,2},{4,5},{5,4},{6,7},{7,6},{8,9},{9,8},{10,11... | collective-permute-start | bytes 405512 | tf_op jit(solution)/shard_map/ppermute | solution.py:34

commit v6 on v5

--- a/solution.py
+++ b/solution.py
@@ -371,35 +371,42 @@
     )(terms, beyond, peak)
 
 
-def product_body(own_ref, mine_ref, other_ref, got_ref, half_ref, peak_ref, held_ref, sem):
-    tokens = own_ref.shape[1]
-    copy = pltpu.make_async_copy(other_ref, held_ref, sem)
-    copy.start()
-    total = jnp.dot(own_ref[...], mine_ref[:tokens, :], preferred_element_type=f32)
-    copy.wait()
-    total += jnp.dot(held_ref[...], got_ref[:tokens, :], preferred_element_type=f32)
-    half_ref[...] = total.astype(bf16)
+def own_body(left_ref, right_ref, out_ref):
+    tokens = left_ref.shape[1]
+    out_ref[...] = jnp.dot(left_ref[...], right_ref[:tokens, :], preferred_element_type=f32)
+
+
+def own_product(left, right):
+    rows = left.shape[0]
+    cols = right.shape[1]
+    return pl.pallas_call(
+        own_body,
+        out_shape=pltpu.VMEM((rows, cols), f32),
+        compiler_params=budget(16),
+        cost_estimate=pl.CostEstimate(
+            flops=3 * 10**8, transcendentals=0, bytes_accessed=2 * 10**6
+        ),
+        name="own_product",
+    )(left, right)
+
+
+def product_body(own_ref, mine_ref, other_ref, got_ref, half_ref, peak_ref):
+    tokens = other_ref.shape[1]
+    total = jnp.dot(other_ref[...], got_ref[:tokens, :], preferred_element_type=f32)
+    half_ref[...] = (own_ref[...] + total).astype(bf16)
     peak_ref[...] = jnp.maximum(
         mine_ref[tokens:, :].astype(f32), got_ref[tokens:, :].astype(f32)
     )
 
 
 def multiply(own, mine, other, got):
-    rows = own.shape[0]
-    cols = mine.shape[1]
+    rows, cols = own.shape
     return pl.pallas_call(
         product_body,
         out_shape=[
             jax.ShapeDtypeStruct((rows, cols), bf16),
             jax.ShapeDtypeStruct((8, cols), f32),
         ],
-        in_specs=[
-            pl.BlockSpec(memory_space=pltpu.VMEM),
-            pl.BlockSpec(memory_space=pltpu.VMEM),
-            pl.BlockSpec(memory_space=pl.ANY),
-            pl.BlockSpec(memory_space=pltpu.VMEM),
-        ],
-        scratch_shapes=[pltpu.VMEM(other.shape, bf16), pltpu.SemaphoreType.DMA],
         compiler_params=budget(16),
         name="multiply",
     )(own, mine, other, got)
@@ -494,7 +501,7 @@
     kept, given = turn(rows_in, n_x, n_c)
     taken = swapped(given)
     state_input_grad, sums = finish(terms, beyond, seq_peaks)
-    half, peaks = multiply(kept, sums, taken, swapped(sums))
+    half, peaks = multiply(own_product(kept, sums), sums, taken, swapped(sums))
     quarter = exchange(half.reshape(n_x, width // (n_x * n_c), 2 * states), "seq_1")
     pieces = add_split(quarter, peaks, n_y * n_z)
     arrived = exchange(pieces, ("seq_0", "dp_0"))

time: 108 us -> 108 us (level)
  no operation moved by 1% of the time
where the time goes in v6:
time: 108 us; the launch traced here: 107 us
  blocking collectives  68.1 us (63%)
  Pallas kernels  18.5 us (17%)
  starting transfers between devices  15 us (14%)
  waiting for transfers between devices  4.13 us (4%)
    all_to_all x3, blocking collectives, exchange(): return lax.all_to_all(x, axes, 0, 0, tiled=True)  68.1 us
    ppermute x2, starting transfers between devices, swapped(): return lax.ppermute(x, 'dp_1', [(0, 1), (1, 0)])  9.46 us
    pallas_call x1, Pallas kernels, inner_terms(): pl.pallas_call(inner_body, grid=(grid,), in_specs=[pl.BlockSpec((tokens,...  6.42 us
    all_to_all x1, starting transfers between devices, exchange(): return lax.all_to_all(x, axes, 0, 0, tiled=True)  5.52 us
    pallas_call x1, Pallas kernels, turn(): pl.pallas_call(turn_body, grid=(grid,), in_specs=[pl.BlockSpec((tokens, s...  3.72 us
    all_to_all x1, waiting for transfers between devices, exchange(): return lax.all_to_all(x, axes, 0, 0, tiled=True)  3.5 us
    pallas_call x1, Pallas kernels, summarize(): pl.pallas_call(summary_body, grid=(grid,), in_specs=[pl.BlockSpec((tokens...  3.46 us
  transfers between devices with their start and end apart: 3, of which 2 were waited for; matrix products, arithmetic and copies ran while one was open for 0% of the time, Pallas kernels for 11%

profile of v6, /device:TPU:1, one launch (start us, length us, event | category | flops | bytes accessed | tf_op | source)
XLA Modules:
  0.0 106.5 jit_solution(12547540986540025176)
XLA Ops:
  0.6 3.5 %summarize.1 = bf16[32,88,128]{2,1,0:T(8,128)(2,1)S(1)} custom-call(bf16[256,2560]{1,0:T(8,128)(2,1)} %bitcast.13, bf16[256,2560]{1,0:T(8,128)(2,1)} %bitcast.15, f32[40,256]{1,0:T(8,128)} %bitcast.21, bf16[256,256]{1,0:T(8,128)(2,1)} %bitcast.19), custom_call_target="tpu_custom_call" | custom-call | tf_op jit(solution)/shard_map/summarize/pallas_call | solution.py:127
  4.1 30.3 %all_to_all.20.got_ref = bf16[32,88,128]{2,1,0:T(8,128)(2,1)S(1)} all-to-all(bf16[32,88,128]{2,1,0:T(8,128)(2,1)S(1)} %summarize.1), channel_id=1, replica_groups=mesh['seq_0'=8,'seq_1'=4,'dp_0'=8,'dp_1'=2] {'seq_0','seq_1'}, dimensions={0} | all-to-all | bytes 1441792 | tf_op jit(solution)/shard_map/all_to_all | solution.py:30
  34.4 0.0 copy-start
  34.4 1.1 %scan_states.1 = (bf16[32,80,128]{2,1,0:T(8,128)(2,1)}, f32[1,128]{1,0:T(1,128)S(1)}) custom-call(bf16[32,88,128]{2,1,0:T(8,128)(2,1)S(1)} %all_to_all.20.got_ref), custom_call_target="tpu_custom_call" | custom-call | tf_op jit(solution)/shard_map/scan_states/pallas_call | solution.py:56
  35.5 5.5 %all-to-all-start.1 = ((bf16[32,80,128]{2,1,0:T(8,128)(2,1)}), bf16[32,80,128]{2,1,0:T(8,128)(2,1)S(1)}, u32[]{:S(2)}, u32[]{:S(2)}) async-start(bf16[32,80,128]{2,1,0:T(8,128)(2,1)} %get-tuple-element.10), calls=%async_computation.1 | async-start | bytes 1310720 | tf_op jit(solution)/shard_map/all_to_all | solution.py:30
  41.0 0.0 copy-done
  41.0 0.0 copy-start.1
  41.0 0.0 copy-start.2
  41.0 0.0 copy-start.3
  41.0 0.0 copy-start.4
  41.0 0.0 copy-start.5
  41.1 0.0 copy-start.6
  41.1 3.7 %turn.1 = (bf16[4,4,80,256]{3,2,1,0:T(8,128)(2,1)S(1)}, bf16[4,4,80,256]{3,2,1,0:T(8,128)(2,1)}) custom-call(bf16[256,2560]{1,0:T(8,128)(2,1)S(1)} %bitcast.14), custom_call_target="tpu_custom_call" | custom-call | flops 1000000000 | bytes 3000000 | tf_op jit(solution)/shard_map/turn/pallas_call | solution.py:326
  44.8 4.0 %collective-permute-start = (bf16[1280,256]{1,0:T(8,128)(2,1)}, bf16[1280,256]{1,0:T(8,128)(2,1)}, u32[]{:S(2)}, u32[]{:S(2)}) collective-permute-start(bf16[1280,256]{1,0:T(8,128)(2,1)} %bitcast.10), channel_id=1, source_target_pairs={{0,1},{1,0},{2,3},{3,2},{4,5},{5,4},{6,7},{7,6},{8,9},{9,8},{10,11... | collective-permute-start | bytes 1966088 | tf_op jit(solution)/shard_map/ppermute | solution.py:34
  48.7 0.0 copy-done.1
  48.8 0.0 copy-done.2
  48.8 0.0 copy-done.3
  48.8 0.0 copy-done.4
  48.8 0.0 copy-done.5
  48.8 0.0 copy-done.6
  48.8 6.4 %inner_terms.1.terms_ref = bf16[256,3200]{1,0:T(8,128)(2,1)S(1)} custom-call(bf16[256,2560]{1,0:T(8,128)(2,1)S(1)} %bitcast.16, bf16[256,2560]{1,0:T(8,128)(2,1)S(1)} %bitcast.23, f32[40,256]{1,0:T(8,128)S(1)} %bitcast.22, f32[40,256]{1,0:T(8,128)S(1)} %bitcast.25, bf16[256,256]{1,0:T(8,128)(2,1)S(1)} %bitcast.20, bf16[2560,128]{1,0:T(8,128)(2,1)S(1)} %bitcast.24), custom_call_target="tpu_custom_call" | custom-call | flops 4000000000 | bytes 6000000 | tf_op jit(solution)/shard_map/inner_terms/pallas_call | solution.py:262
  55.2 3.5 %all-to-all-done.1 = bf16[32,80,128]{2,1,0:T(8,128)(2,1)S(1)} async-done(((bf16[32,80,128]{2,1,0:T(8,128)(2,1)}), bf16[32,80,128]{2,1,0:T(8,128)(2,1)S(1)}, u32[]{:S(2)}, u32[]{:S(2)}) %all-to-all-start.1) | async-done | bytes 655392 | tf_op jit(solution)/shard_map/all_to_all | solution.py:30
  58.7 1.2 %finish.1 = (bf16[256,256]{1,0:T(8,128)(2,1)}, bf16[264,256]{1,0:T(8,128)(2,1)S(1)}) custom-call(bf16[256,3200]{1,0:T(8,128)(2,1)S(1)} %inner_terms.1.terms_ref, bf16[2560,128]{1,0:T(8,128)(2,1)S(1)} %bitcast.12, f32[1,128]{1,0:T(1,128)S(1)} %get-tuple-element.11.peak_ref), custom_call_target="tpu_custom_call" | custom-call | tf_op jit(solution)/shard_map/finish/pallas_call | solution.py:363
  59.9 5.5 %collective-permute-start.1 = (bf16[264,256]{1,0:T(8,128)(2,1)S(1)}, bf16[264,256]{1,0:T(8,128)(2,1)S(1)}, u32[]{:S(2)}, u32[]{:S(2)}) collective-permute-start(bf16[264,256]{1,0:T(8,128)(2,1)S(1)} %get-tuple-element.14.right_ref.mine_ref), channel_id=1, source_target_pairs={{0,1},{1,0},{2,3},{3,2},{4,5},{5,4},{6,7},{7,6},{8,9},{9,8},{10,11... | collective-permute-start | bytes 405512 | tf_op jit(solution)/shard_map/ppermute | solution.py:34
  65.4 0.3 own_product.1.own_ref
  65.8 0.0 collective-permute-done.other_ref
  65.8 0.6 collective-permute-done.1.got_ref
  66.4 1.4 %multiply.1 = (bf16[1280,256]{1,0:T(8,128)(2,1)S(1)}, f32[8,256]{1,0:T(8,128)S(1)}) custom-call(f32[1280,256]{1,0:T(8,128)S(1)} %own_product.1.own_ref, bf16[264,256]{1,0:T(8,128)(2,1)S(1)} %get-tuple-element.14.right_ref.mine_ref, bf16[1280,256]{1,0:T(8,128)(2,1)} %collective-permute-done.other_ref, bf16[264,256]{1,0:T(8,128)(2,1)S(1)} %collective-permute-done.1.got_ref), custom_call_target="tpu_custom_call" | custom-call | tf_op jit(solution)/shard_map/multiply/pallas_call | solution.py:404
  67.8 13.4 %all_to_all.21.got_ref = bf16[4,320,256]{2,1,0:T(8,128)(2,1)S(1)} all-to-all(bf16[4,320,256]{2,1,0:T(8,128)(2,1)S(1)} %bitcast.18), channel_id=1, replica_groups=mesh['seq_0'=8,'seq_1'=4,'dp_0'=8,'dp_1'=2] {'seq_1'}, dimensions={0} | all-to-all | bytes 1310720 | tf_op jit(solution)/shard_map/all_to_all | solution.py:30
  81.2 0.2 add_split.1
  81.4 24.5 %all_to_all.22.got_ref = bf16[64,8,256]{2,1,0:T(8,128)(2,1)S(1)} all-to-all(bf16[64,8,256]{2,1,0:T(8,128)(2,1)S(1)} %add_split.1), channel_id=1, replica_groups=mesh['seq_0'=8,'seq_1'=4,'dp_0'=8,'dp_1'=2] {'seq_0','dp_0'}, dimensions={0} | all-to-all | bytes 524288 | tf_op jit(solution)/shard_map/all_to_all | solution.py:30
  105.8 0.7 close.1
Async XLA Ops:
  34.4 6.6 %copy-start = (bf16[1,256,2560]{2,1,0:T(8,128)(2,1)S(1)}, bf16[1,256,2560]{2,1,0:T(8,128)(2,1)}, u32[]{:S(2)}) copy-start(bf16[1,256,2560]{2,1,0:T(8,128)(2,1)} %param.7) | copy-start | bytes 3932164
  35.5 23.3 %all-to-all-start.1 = ((bf16[32,80,128]{2,1,0:T(8,128)(2,1)}), bf16[32,80,128]{2,1,0:T(8,128)(2,1)S(1)}, u32[]{:S(2)}, u32[]{:S(2)}) async-start(bf16[32,80,128]{2,1,0:T(8,128)(2,1)} %get-tuple-element.10), calls=%async_computation.1 | async-start | bytes 1310720 | tf_op jit(solution)/shard_map/all_to_all | solution.py:30
  41.0 7.8 %copy-start.1 = (bf16[1,256,2560]{2,1,0:T(8,128)(2,1)S(1)}, bf16[1,256,2560]{2,1,0:T(8,128)(2,1)}, u32[]{:S(2)}) copy-start(bf16[1,256,2560]{2,1,0:T(8,128)(2,1)} %param.9) | copy-start | bytes 3932164
  41.0 7.8 %copy-start.2 = (bf16[1,256,256]{2,1,0:T(8,128)(2,1)S(1)}, bf16[1,256,256]{2,1,0:T(8,128)(2,1)}, u32[]{:S(2)}) copy-start(bf16[1,256,256]{2,1,0:T(8,128)(2,1)} %param.12) | copy-start | bytes 393220
  41.0 7.8 %copy-start.3 = (f32[1,40,256]{2,1,0:T(8,128)S(1)}, f32[1,40,256]{2,1,0:T(8,128)}, u32[]{:S(2)}) copy-start(f32[1,40,256]{2,1,0:T(8,128)} %param.11) | copy-start | bytes 122884
  41.0 7.7 %copy-start.4 = (bf16[1,256,2560]{2,1,0:T(8,128)(2,1)S(1)}, bf16[1,256,2560]{2,1,0:T(8,128)(2,1)}, u32[]{:S(2)}) copy-start(bf16[1,256,2560]{2,1,0:T(8,128)(2,1)} %param.8) | copy-start | bytes 3932164
  41.0 7.7 %copy-start.5 = (bf16[1,1,2560,128]{3,2,1,0:T(8,128)(2,1)S(1)}, bf16[1,1,2560,128]{3,2,1,0:T(8,128)(2,1)}, u32[]{:S(2)}) copy-start(bf16[1,1,2560,128]{3,2,1,0:T(8,128)(2,1)} %param.13) | copy-start | bytes 1966084
  41.1 7.7 %copy-start.6 = (f32[1,40,256]{2,1,0:T(8,128)S(1)}, f32[1,40,256]{2,1,0:T(8,128)}, u32[]{:S(2)}) copy-start(f32[1,40,256]{2,1,0:T(8,128)} %param.10) | copy-start | bytes 122884
  44.8 21.0 %collective-permute-start = (bf16[1280,256]{1,0:T(8,128)(2,1)}, bf16[1280,256]{1,0:T(8,128)(2,1)}, u32[]{:S(2)}, u32[]{:S(2)}) collective-permute-start(bf16[1280,256]{1,0:T(8,128)(2,1)} %bitcast.10), channel_id=1, source_target_pairs={{0,1},{1,0},{2,3},{3,2},{4,5},{5,4},{6,7},{7,6},{8,9},{9,8},{10,11... | collective-permute-start | bytes 1966088 | tf_op jit(solution)/shard_map/ppermute | solution.py:34
  59.9 6.5 %collective-permute-start.1 = (bf16[264,256]{1,0:T(8,128)(2,1)S(1)}, bf16[264,256]{1,0:T(8,128)(2,1)S(1)}, u32[]{:S(2)}, u32[]{:S(2)}) collective-permute-start(bf16[264,256]{1,0:T(8,128)(2,1)S(1)} %get-tuple-element.14.right_ref.mine_ref), channel_id=1, source_target_pairs={{0,1},{1,0},{2,3},{3,2},{4,5},{5,4},{6,7},{7,6},{8,9},{9,8},{10,11... | collective-permute-start | bytes 405512 | tf_op jit(solution)/shard_map/ppermute | solution.py:34

commit v7 on v6

--- a/solution.py
+++ b/solution.py
@@ -72,6 +72,7 @@
     span = cot_ref.shape[1]
     rows = span // chunks
     head_size = span * pl.num_programs(0) // heads
+    half = spread_ref.shape[0] // 2
 
     @pl.when(step == 0)
     def _():
@@ -85,17 +86,18 @@
         )
         grown = jnp.exp(cum)
         high = grown.astype(bf16)
-        spread_ref[0] = high
-        spread_ref[1] = (grown - high.astype(f32)).astype(bf16)
+        spread_ref[...] = jnp.zeros_like(spread_ref)
+        spread_ref[:heads] = high
+        spread_ref[half : half + heads] = (grown - high.astype(f32)).astype(bf16)
         value = pre_ref[:, states:].astype(f32)
         reads_ref[...] = (value / (1.0 + jnp.exp(-value))).astype(bf16)
 
-    owner = lax.broadcasted_iota(jnp.int32, (heads, span), 0) * head_size - step * span
-    lane = lax.broadcasted_iota(jnp.int32, (heads, span), 1)
+    head = lax.broadcasted_iota(jnp.int32, (2 * half, span), 0)
+    owner = jnp.where(head < half, head, head - half) * head_size - step * span
+    lane = lax.broadcasted_iota(jnp.int32, (2 * half, span), 1)
     hot = jnp.where((lane >= owner) & (lane < owner + head_size), 1.0, 0.0).astype(bf16)
     both = (((0,), (0,)), ((), ()))
-    scale = lax.dot_general(spread_ref[0], hot, both, preferred_element_type=f32)
-    scale += lax.dot_general(spread_ref[1], hot, both, preferred_element_type=f32)
+    scale = lax.dot_general(spread_ref[...], hot, both, preferred_element_type=f32)
     weighted = (cot_ref[...].astype(f32) * scale).astype(bf16)
     later = lax.dot_general(weighted, reads_ref[...], both, preferred_element_type=f32)
     later = later.astype(bf16)
@@ -137,7 +139,7 @@
         out_shape=pltpu.VMEM((n_seq, rows + 8, states), bf16),
         scratch_shapes=[
             pltpu.VMEM((tokens, states), bf16),
-            pltpu.VMEM((2, heads, tokens), bf16),
+            pltpu.VMEM((2 * (-(-heads // 16) * 16), tokens), bf16),
         ],
         compiler_params=budget(60),
         name="summarize",
@@ -371,23 +373,32 @@
     )(terms, beyond, peak)
 
 
-def own_body(left_ref, right_ref, out_ref):
+def own_body(left_ref, right_ref, taken_ref, out_ref, held_ref, sem):
     tokens = left_ref.shape[1]
+    copy = pltpu.make_async_copy(taken_ref, held_ref, sem)
+    copy.start()
     out_ref[...] = jnp.dot(left_ref[...], right_ref[:tokens, :], preferred_element_type=f32)
-
-
-def own_product(left, right):
+    copy.wait()
+
+
+def own_product(left, right, taken):
     rows = left.shape[0]
     cols = right.shape[1]
     return pl.pallas_call(
         own_body,
-        out_shape=pltpu.VMEM((rows, cols), f32),
+        in_specs=[
+            pl.BlockSpec(memory_space=pltpu.VMEM),
+            pl.BlockSpec(memory_space=pltpu.VMEM),
+            pl.BlockSpec(memory_space=pltpu.HBM),
+        ],
+        out_shape=[pltpu.VMEM((rows, cols), f32), pltpu.VMEM(taken.shape, bf16)],
+        scratch_shapes=[pltpu.SemaphoreType.DMA],
         compiler_params=budget(16),
         cost_estimate=pl.CostEstimate(
             flops=3 * 10**8, transcendentals=0, bytes_accessed=2 * 10**6
         ),
         name="own_product",
-    )(left, right)
+    )(left, right, taken)
 
 
 def product_body(own_ref, mine_ref, other_ref, got_ref, half_ref, peak_ref):
@@ -501,7 +512,8 @@
     kept, given = turn(rows_in, n_x, n_c)
     taken = swapped(given)
     state_input_grad, sums = finish(terms, beyond, seq_peaks)
-    half, peaks = multiply(own_product(kept, sums), sums, taken, swapped(sums))
+    own, held = own_product(kept, sums, taken)
+    half, peaks = multiply(own, sums, held, swapped(sums))
     quarter = exchange(half.reshape(n_x, width // (n_x * n_c), 2 * states), "seq_1")
     pieces = add_split(quarter, peaks, n_y * n_z)
     arrived = exchange(pieces, ("seq_0", "dp_0"))

time: 108 us -> 107 us (level)
    pallas_call x1, Pallas kernels: 1.41 us -> 0.33 us  [multiply(): pl.pallas_call(product_body, out_shape=[jax.ShapeDtypeStruct((rows, cols)...]
  transfers between devices with their start and end apart: 3 -> 3, of which waited for: 2 -> 1; matrix products, arithmetic and copies ran while one was open for 0% -> 0% of each run, Pallas kernels for 11% -> 12%
where the time goes in v7:
time: 107 us; the launch traced here: 105 us
  blocking collectives  68.2 us (64%)
  Pallas kernels  17.8 us (17%)
  starting transfers between devices  15 us (14%)
  waiting for transfers between devices  3.48 us (3%)
    all_to_all x3, blocking collectives, exchange(): return lax.all_to_all(x, axes, 0, 0, tiled=True)  68.2 us
    ppermute x2, starting transfers between devices, swapped(): return lax.ppermute(x, 'dp_1', [(0, 1), (1, 0)])  9.45 us
    pallas_call x1, Pallas kernels, inner_terms(): pl.pallas_call(inner_body, grid=(grid,), in_specs=[pl.BlockSpec((tokens,...  6.42 us
    all_to_all x1, starting transfers between devices, exchange(): return lax.all_to_all(x, axes, 0, 0, tiled=True)  5.53 us
    pallas_call x1, Pallas kernels, turn(): pl.pallas_call(turn_body, grid=(grid,), in_specs=[pl.BlockSpec((tokens, s...  3.75 us
    all_to_all x1, waiting for transfers between devices, exchange(): return lax.all_to_all(x, axes, 0, 0, tiled=True)  3.48 us
    pallas_call x1, Pallas kernels, summarize(): pl.pallas_call(summary_body, grid=(grid,), in_specs=[pl.BlockSpec((tokens...  3.09 us
  transfers between devices with their start and end apart: 3, of which 1 were waited for; matrix products, arithmetic and copies ran while one was open for 0% of the time, Pallas kernels for 12%

profile of v7, /device:TPU:1, one launch (start us, length us, event | category | flops | bytes accessed | tf_op | source)
XLA Modules:
  0.0 105.3 jit_solution(5847540040621562165)
XLA Ops:
  0.6 3.1 %summarize.1 = bf16[32,88,128]{2,1,0:T(8,128)(2,1)S(1)} custom-call(bf16[256,2560]{1,0:T(8,128)(2,1)} %bitcast.13, bf16[256,2560]{1,0:T(8,128)(2,1)} %bitcast.15, f32[40,256]{1,0:T(8,128)} %bitcast.21, bf16[256,256]{1,0:T(8,128)(2,1)} %bitcast.19), custom_call_target="tpu_custom_call" | custom-call | tf_op jit(solution)/shard_map/summarize/pallas_call | solution.py:129
  3.7 30.3 %all_to_all.20.got_ref = bf16[32,88,128]{2,1,0:T(8,128)(2,1)S(1)} all-to-all(bf16[32,88,128]{2,1,0:T(8,128)(2,1)S(1)} %summarize.1), channel_id=1, replica_groups=mesh['seq_0'=8,'seq_1'=4,'dp_0'=8,'dp_1'=2] {'seq_0','seq_1'}, dimensions={0} | all-to-all | bytes 1441792 | tf_op jit(solution)/shard_map/all_to_all | solution.py:30
  34.0 0.0 copy-start
  34.0 1.1 %scan_states.1 = (bf16[32,80,128]{2,1,0:T(8,128)(2,1)}, f32[1,128]{1,0:T(1,128)S(1)}) custom-call(bf16[32,88,128]{2,1,0:T(8,128)(2,1)S(1)} %all_to_all.20.got_ref), custom_call_target="tpu_custom_call" | custom-call | tf_op jit(solution)/shard_map/scan_states/pallas_call | solution.py:56
  35.1 5.5 %all-to-all-start.1 = ((bf16[32,80,128]{2,1,0:T(8,128)(2,1)}), bf16[32,80,128]{2,1,0:T(8,128)(2,1)S(1)}, u32[]{:S(2)}, u32[]{:S(2)}) async-start(bf16[32,80,128]{2,1,0:T(8,128)(2,1)} %get-tuple-element.12), calls=%async_computation.1 | async-start | bytes 1310720 | tf_op jit(solution)/shard_map/all_to_all | solution.py:30
  40.6 0.0 copy-done
  40.6 0.0 copy-start.1
  40.6 0.0 copy-start.2
  40.7 0.0 copy-start.3
  40.7 0.0 copy-start.4
  40.7 0.0 copy-start.5
  40.7 0.0 copy-start.6
  40.7 3.7 %turn.1 = (bf16[4,4,80,256]{3,2,1,0:T(8,128)(2,1)S(1)}, bf16[4,4,80,256]{3,2,1,0:T(8,128)(2,1)}) custom-call(bf16[256,2560]{1,0:T(8,128)(2,1)S(1)} %bitcast.14), custom_call_target="tpu_custom_call" | custom-call | flops 1000000000 | bytes 3000000 | tf_op jit(solution)/shard_map/turn/pallas_call | solution.py:328
  44.4 3.9 %collective-permute-start = (bf16[1280,256]{1,0:T(8,128)(2,1)}, bf16[1280,256]{1,0:T(8,128)(2,1)}, u32[]{:S(2)}, u32[]{:S(2)}) collective-permute-start(bf16[1280,256]{1,0:T(8,128)(2,1)} %bitcast.10), channel_id=1, source_target_pairs={{0,1},{1,0},{2,3},{3,2},{4,5},{5,4},{6,7},{7,6},{8,9},{9,8},{10,11... | collective-permute-start | bytes 1966088 | tf_op jit(solution)/shard_map/ppermute | solution.py:34
  48.4 0.0 copy-done.1
  48.4 0.0 copy-done.2
  48.4 0.0 copy-done.3
  48.4 0.0 copy-done.4
  48.4 0.0 copy-done.5
  48.4 0.0 copy-done.6
  48.5 6.4 %inner_terms.1.terms_ref = bf16[256,3200]{1,0:T(8,128)(2,1)S(1)} custom-call(bf16[256,2560]{1,0:T(8,128)(2,1)S(1)} %bitcast.16, bf16[256,2560]{1,0:T(8,128)(2,1)S(1)} %bitcast.23, f32[40,256]{1,0:T(8,128)S(1)} %bitcast.22, f32[40,256]{1,0:T(8,128)S(1)} %bitcast.25, bf16[256,256]{1,0:T(8,128)(2,1)S(1)} %bitcast.20, bf16[2560,128]{1,0:T(8,128)(2,1)S(1)} %bitcast.24), custom_call_target="tpu_custom_call" | custom-call | flops 4000000000 | bytes 6000000 | tf_op jit(solution)/shard_map/inner_terms/pallas_call | solution.py:264
  54.9 3.5 %all-to-all-done.1 = bf16[32,80,128]{2,1,0:T(8,128)(2,1)S(1)} async-done(((bf16[32,80,128]{2,1,0:T(8,128)(2,1)}), bf16[32,80,128]{2,1,0:T(8,128)(2,1)S(1)}, u32[]{:S(2)}, u32[]{:S(2)}) %all-to-all-start.1) | async-done | bytes 655392 | tf_op jit(solution)/shard_map/all_to_all | solution.py:30
  58.4 1.2 %finish.1 = (bf16[256,256]{1,0:T(8,128)(2,1)}, bf16[264,256]{1,0:T(8,128)(2,1)S(1)}) custom-call(bf16[256,3200]{1,0:T(8,128)(2,1)S(1)} %inner_terms.1.terms_ref, bf16[2560,128]{1,0:T(8,128)(2,1)S(1)} %bitcast.12, f32[1,128]{1,0:T(1,128)S(1)} %get-tuple-element.13.peak_ref), custom_call_target="tpu_custom_call" | custom-call | tf_op jit(solution)/shard_map/finish/pallas_call | solution.py:365
  59.5 5.5 %collective-permute-start.1 = (bf16[264,256]{1,0:T(8,128)(2,1)S(1)}, bf16[264,256]{1,0:T(8,128)(2,1)S(1)}, u32[]{:S(2)}, u32[]{:S(2)}) collective-permute-start(bf16[264,256]{1,0:T(8,128)(2,1)S(1)} %get-tuple-element.16.right_ref.mine_ref), channel_id=1, source_target_pairs={{0,1},{1,0},{2,3},{3,2},{4,5},{5,4},{6,7},{7,6},{8,9},{9,8},{10,11... | collective-permute-start | bytes 405512 | tf_op jit(solution)/shard_map/ppermute | solution.py:34
  65.1 0.0 collective-permute-done.taken_ref
  65.1 1.1 %own_product.1 = (f32[1280,256]{1,0:T(8,128)S(1)}, bf16[1280,256]{1,0:T(8,128)(2,1)S(1)}) custom-call(bf16[1280,256]{1,0:T(8,128)(2,1)S(1)} %bitcast.17, bf16[264,256]{1,0:T(8,128)(2,1)S(1)} %get-tuple-element.16.right_ref.mine_ref, bf16[1280,256]{1,0:T(8,128)(2,1)} %collective-permute-done.taken_ref), custom_call_target="tpu_custom_call" | custom-call | flops 300000000 | bytes 2000000 | tf_op jit(solution)/shard_map/own_product/pallas_call | solution.py:387
  66.2 0.0 collective-permute-done.1.got_ref
  66.2 0.3 multiply.1
  66.5 13.9 %all_to_all.21.got_ref = bf16[4,320,256]{2,1,0:T(8,128)(2,1)S(1)} all-to-all(bf16[4,320,256]{2,1,0:T(8,128)(2,1)S(1)} %bitcast.18), channel_id=1, replica_groups=mesh['seq_0'=8,'seq_1'=4,'dp_0'=8,'dp_1'=2] {'seq_1'}, dimensions={0} | all-to-all | bytes 1310720 | tf_op jit(solution)/shard_map/all_to_all | solution.py:30
  80.4 0.2 add_split.1
  80.6 24.1 %all_to_all.22.got_ref = bf16[64,8,256]{2,1,0:T(8,128)(2,1)S(1)} all-to-all(bf16[64,8,256]{2,1,0:T(8,128)(2,1)S(1)} %add_split.1), channel_id=1, replica_groups=mesh['seq_0'=8,'seq_1'=4,'dp_0'=8,'dp_1'=2] {'seq_0','dp_0'}, dimensions={0} | all-to-all | bytes 524288 | tf_op jit(solution)/shard_map/all_to_all | solution.py:30
  104.6 0.7 close.1
Async XLA Ops:
  34.0 6.6 %copy-start = (bf16[1,256,2560]{2,1,0:T(8,128)(2,1)S(1)}, bf16[1,256,2560]{2,1,0:T(8,128)(2,1)}, u32[]{:S(2)}) copy-start(bf16[1,256,2560]{2,1,0:T(8,128)(2,1)} %param.7) | copy-start | bytes 3932164
  35.1 23.3 %all-to-all-start.1 = ((bf16[32,80,128]{2,1,0:T(8,128)(2,1)}), bf16[32,80,128]{2,1,0:T(8,128)(2,1)S(1)}, u32[]{:S(2)}, u32[]{:S(2)}) async-start(bf16[32,80,128]{2,1,0:T(8,128)(2,1)} %get-tuple-element.12), calls=%async_computation.1 | async-start | bytes 1310720 | tf_op jit(solution)/shard_map/all_to_all | solution.py:30
  40.6 7.8 %copy-start.1 = (bf16[1,256,2560]{2,1,0:T(8,128)(2,1)S(1)}, bf16[1,256,2560]{2,1,0:T(8,128)(2,1)}, u32[]{:S(2)}) copy-start(bf16[1,256,2560]{2,1,0:T(8,128)(2,1)} %param.9) | copy-start | bytes 3932164
  40.6 7.8 %copy-start.2 = (bf16[1,256,256]{2,1,0:T(8,128)(2,1)S(1)}, bf16[1,256,256]{2,1,0:T(8,128)(2,1)}, u32[]{:S(2)}) copy-start(bf16[1,256,256]{2,1,0:T(8,128)(2,1)} %param.12) | copy-start | bytes 393220
  40.7 7.8 %copy-start.3 = (f32[1,40,256]{2,1,0:T(8,128)S(1)}, f32[1,40,256]{2,1,0:T(8,128)}, u32[]{:S(2)}) copy-start(f32[1,40,256]{2,1,0:T(8,128)} %param.11) | copy-start | bytes 122884
  40.7 7.8 %copy-start.4 = (bf16[1,256,2560]{2,1,0:T(8,128)(2,1)S(1)}, bf16[1,256,2560]{2,1,0:T(8,128)(2,1)}, u32[]{:S(2)}) copy-start(bf16[1,256,2560]{2,1,0:T(8,128)(2,1)} %param.8) | copy-start | bytes 3932164
  40.7 7.8 %copy-start.5 = (bf16[1,1,2560,128]{3,2,1,0:T(8,128)(2,1)S(1)}, bf16[1,1,2560,128]{3,2,1,0:T(8,128)(2,1)}, u32[]{:S(2)}) copy-start(bf16[1,1,2560,128]{3,2,1,0:T(8,128)(2,1)} %param.13) | copy-start | bytes 1966084
  40.7 7.8 %copy-start.6 = (f32[1,40,256]{2,1,0:T(8,128)S(1)}, f32[1,40,256]{2,1,0:T(8,128)}, u32[]{:S(2)}) copy-start(f32[1,40,256]{2,1,0:T(8,128)} %param.10) | copy-start | bytes 122884
  44.4 20.6 %collective-permute-start = (bf16[1280,256]{1,0:T(8,128)(2,1)}, bf16[1280,256]{1,0:T(8,128)(2,1)}, u32[]{:S(2)}, u32[]{:S(2)}) collective-permute-start(bf16[1280,256]{1,0:T(8,128)(2,1)} %bitcast.10), channel_id=1, source_target_pairs={{0,1},{1,0},{2,3},{3,2},{4,5},{5,4},{6,7},{7,6},{8,9},{9,8},{10,11... | collective-permute-start | bytes 1966088 | tf_op jit(solution)/shard_map/ppermute | solution.py:34
  59.5 6.6 %collective-permute-start.1 = (bf16[264,256]{1,0:T(8,128)(2,1)S(1)}, bf16[264,256]{1,0:T(8,128)(2,1)S(1)}, u32[]{:S(2)}, u32[]{:S(2)}) collective-permute-start(bf16[264,256]{1,0:T(8,128)(2,1)S(1)} %get-tuple-element.16.right_ref.mine_ref), channel_id=1, source_target_pairs={{0,1},{1,0},{2,3},{3,2},{4,5},{5,4},{6,7},{7,6},{8,9},{9,8},{10,11... | collective-permute-start | bytes 405512 | tf_op jit(solution)/shard_map/ppermute | solution.py:34

commit v8 on v7

--- a/solution.py
+++ b/solution.py
@@ -154,6 +154,7 @@
     pre_ref,
     entry_ref,
     out_ref,
+    read_ref,
     column_ref,
     row_ref,
     spread_ref,
@@ -248,7 +249,7 @@
         for part in (inner, slope[:, :states]):
             high = part.astype(bf16)
             parts += [high, (part - high.astype(f32)).astype(bf16)]
-        parts.append((read * slope[:, states:]).astype(bf16))
+        read_ref[...] = (read * slope[:, states:]).astype(bf16)
         at = out_ref.shape[1] - len(parts) * states
         for k, part in enumerate(parts):
             out_ref[:, at + k * states : at + (k + 1) * states] = part
@@ -272,8 +273,11 @@
             pl.BlockSpec((tokens, 2 * states), whole),
             pl.BlockSpec((span, states), lambda i: (i, 0)),
         ],
-        out_specs=pl.BlockSpec(memory_space=pltpu.VMEM),
-        out_shape=pltpu.VMEM((tokens, channels + 5 * states), bf16),
+        out_specs=[pl.BlockSpec(memory_space=pltpu.VMEM), pl.BlockSpec((tokens, states), whole)],
+        out_shape=[
+            pltpu.VMEM((tokens, channels + 4 * states), bf16),
+            jax.ShapeDtypeStruct((tokens, states), bf16),
+        ],
         scratch_shapes=[
             pltpu.VMEM((tokens, 128), f32),
             pltpu.VMEM((heads, tokens), f32),
@@ -341,7 +345,7 @@
     return own.reshape(width // n_c, tokens), other.reshape(width // n_c, tokens)
 
 
-def finish_body(terms_ref, beyond_ref, peak_ref, grad_ref, send_ref):
+def finish_body(terms_ref, beyond_ref, peak_ref, send_ref):
     channels, states = beyond_ref.shape
     tokens = terms_ref.shape[0]
     carried = jnp.dot(terms_ref[:, :channels], beyond_ref[...], preferred_element_type=f32)
@@ -352,11 +356,8 @@
     def whole(k):
         return part(k).astype(f32) + part(k + 1).astype(f32)
 
-    send_ref[:tokens, :states] = ((whole(0) + carried) * whole(2)).astype(bf16)
-    send_ref[:tokens, states:] = part(4)
-    send_ref[tokens:, :states] = jnp.broadcast_to(peak_ref[...], (8, states)).astype(bf16)
-    send_ref[tokens:, states:] = jnp.zeros((8, states), bf16)
-    grad_ref[...] = send_ref[:tokens, :]
+    send_ref[:tokens, :] = ((whole(0) + carried) * whole(2)).astype(bf16)
+    send_ref[tokens:, :] = jnp.broadcast_to(peak_ref[...], (8, states)).astype(bf16)
 
 
 def finish(terms, beyond, peak):
@@ -364,24 +365,84 @@
     states = beyond.shape[1]
     return pl.pallas_call(
         finish_body,
-        out_shape=[
-            jax.ShapeDtypeStruct((tokens, 2 * states), bf16),
-            jax.ShapeDtypeStruct((tokens + 8, 2 * states), bf16),
-        ],
+        out_shape=jax.ShapeDtypeStruct((tokens + 8, states), bf16),
         compiler_params=budget(16),
         name="finish",
     )(terms, beyond, peak)
 
 
-def own_body(left_ref, right_ref, taken_ref, out_ref, held_ref, sem):
+def early_body(left_ref, mine_ref, other_ref, got_ref, keep_ref, send_ref, total_ref):
+    rows = keep_ref.shape[1]
+    total_ref[...] = jnp.dot(
+        left_ref[...], mine_ref[...], preferred_element_type=f32
+    ) + jnp.dot(other_ref[...], got_ref[...], preferred_element_type=f32)
+    x = lax.axis_index("seq_1")
+    odd, high = lax.rem(x, 2), lax.div(x, 2)
+    for j in range(2):
+        side = odd + j - 2 * odd * j
+        at = pl.multiple_of((2 * high + side) * rows, 8)
+        keep_ref[j] = total_ref[pl.ds(at, rows), :]
+        at = pl.multiple_of((2 * (1 - high) + side) * rows, 8)
+        send_ref[j] = total_ref[pl.ds(at, rows), :].astype(bf16)
+
+
+def early_product(left, mine, other, got, n_x):
+    rows, cols = left.shape[0], mine.shape[1]
+    shape = (2, rows // n_x, cols)
+    return pl.pallas_call(
+        early_body,
+        out_shape=[jax.ShapeDtypeStruct(shape, f32), jax.ShapeDtypeStruct(shape, bf16)],
+        scratch_shapes=[pltpu.VMEM((rows, cols), f32)],
+        compiler_params=budget(16),
+        cost_estimate=pl.CostEstimate(
+            flops=3 * 10**8, transcendentals=0, bytes_accessed=2 * 10**6
+        ),
+        name="early_product",
+    )(left, mine, other, got)
+
+
+def first_body(keep_ref, got_ref, rest_ref, send_ref):
+    rest_ref[...] = keep_ref[0] + got_ref[0].astype(f32)
+    send_ref[...] = (keep_ref[1] + got_ref[1].astype(f32)).astype(bf16)
+
+
+def add_first(keep, got):
+    return pl.pallas_call(
+        first_body,
+        out_shape=[
+            jax.ShapeDtypeStruct(keep.shape[1:], f32),
+            jax.ShapeDtypeStruct(keep.shape[1:], bf16),
+        ],
+        compiler_params=budget(8),
+        name="add_first",
+    )(keep, got)
+
+
+def second_body(rest_ref, got_ref, out_ref):
+    out_ref[...] = rest_ref[...] + got_ref[...].astype(f32)
+
+
+def add_second(rest, got):
+    return pl.pallas_call(
+        second_body,
+        out_shape=jax.ShapeDtypeStruct(rest.shape, f32),
+        compiler_params=budget(8),
+        name="add_second",
+    )(rest, got)
+
+
+def own_body(left_ref, right_ref, taken_ref, read_ref, out_ref, held_ref, grad_ref, sem):
     tokens = left_ref.shape[1]
     copy = pltpu.make_async_copy(taken_ref, held_ref, sem)
     copy.start()
     out_ref[...] = jnp.dot(left_ref[...], right_ref[:tokens, :], preferred_element_type=f32)
+    states = read_ref.shape[1]
+    grad_ref[:, :states] = right_ref[:tokens, :]
+    grad_ref[:, states:] = read_ref[...]
     copy.wait()
 
 
-def own_product(left, right, taken):
+def own_product(left, right, taken, read):
     rows = left.shape[0]
     cols = right.shape[1]
     return pl.pallas_call(
@@ -390,15 +451,20 @@
             pl.BlockSpec(memory_space=pltpu.VMEM),
             pl.BlockSpec(memory_space=pltpu.VMEM),
             pl.BlockSpec(memory_space=pltpu.HBM),
-        ],
-        out_shape=[pltpu.VMEM((rows, cols), f32), pltpu.VMEM(taken.shape, bf16)],
+            pl.BlockSpec(memory_space=pltpu.VMEM),
+        ],
+        out_shape=[
+            pltpu.VMEM((rows, cols), f32),
+            pltpu.VMEM(taken.shape, bf16),
+            jax.ShapeDtypeStruct((left.shape[1], 2 * cols), bf16),
+        ],
         scratch_shapes=[pltpu.SemaphoreType.DMA],
         compiler_params=budget(16),
         cost_estimate=pl.CostEstimate(
             flops=3 * 10**8, transcendentals=0, bytes_accessed=2 * 10**6
         ),
         name="own_product",
-    )(left, right, taken)
+    )(left, right, taken, read)
 
 
 def product_body(own_ref, mine_ref, other_ref, got_ref, half_ref, peak_ref):
@@ -423,30 +489,32 @@
     )(own, mine, other, got)
 
 
-def split_body(got_ref, peak_ref, out_ref, sum_ref):
-    count, rows, cols = got_ref.shape
-    pieces = out_ref.shape[0]
+def split_body(got_ref, read_ref, peak_ref, out_ref, sum_ref):
+    count, rows, states = got_ref.shape
+    pieces, _, cols = out_ref.shape
     own = rows // pieces
     total = got_ref[0].astype(f32)
     for k in range(1, count):
         total += got_ref[k].astype(f32)
-    sum_ref[:rows] = total
+    sum_ref[:rows, :states] = total
+    sum_ref[:rows, states:] = read_ref[...]
     sum_ref[rows:] = jnp.zeros((8, cols), f32)
     row = lax.broadcasted_iota(jnp.int32, (8, cols), 0)
-    peak = peak_ref[...]
+    peak = jnp.concatenate([peak_ref[...], jnp.zeros_like(peak_ref)], axis=1)
     for q in range(pieces):
         out_ref[q] = jnp.where(row < own, sum_ref[own * q : own * q + 8, :], peak).astype(bf16)
 
 
-def add_split(got, peak, pieces):
-    _, rows, cols = got.shape
+def add_split(got, read, peak, pieces):
+    _, rows, states = got.shape
+    cols = 2 * states
     return pl.pallas_call(
         split_body,
         out_shape=jax.ShapeDtypeStruct((pieces, 8, cols), bf16),
         scratch_shapes=[pltpu.VMEM((rows + 8, cols), f32)],
         compiler_params=budget(6),
         name="add_split",
-    )(got, peak)
+    )(got, read, peak)
 
 
 def close_body(got_ref, out_ref):
@@ -500,8 +568,9 @@
     got = exchange(sent, SEQ)
     slices, seq_peaks = scan_states(got, slice_rows, head_size)
     beyond = exchange(slices, SEQ).reshape(channels, states)
-
-    terms = inner_terms(
+    kept, given = turn(rows_in, n_x, n_c)
+    taken = swapped(given)
+    terms, grad_read = inner_terms(
         flat_cot,
         scan_input.reshape(tokens, channels),
         decays,
@@ -509,13 +578,16 @@
         flat_pre,
         entry_state.reshape(channels, states),
     )
-    kept, given = turn(rows_in, n_x, n_c)
-    taken = swapped(given)
-    state_input_grad, sums = finish(terms, beyond, seq_peaks)
-    own, held = own_product(kept, sums, taken)
+    keep, send = early_product(kept, grad_read, taken, swapped(grad_read), n_x)
+    got = lax.ppermute(send, "seq_1", [(i, (i + 2) % 4) for i in range(4)])
+    rest, send = add_first(keep, got)
+    got = lax.ppermute(send, "seq_1", [(0, 1), (1, 0), (2, 3), (3, 2)])
+    read = add_second(rest, got)
+    sums = finish(terms, beyond, seq_peaks)
+    own, held, state_input_grad = own_product(kept, sums, taken, grad_read)
     half, peaks = multiply(own, sums, held, swapped(sums))
-    quarter = exchange(half.reshape(n_x, width // (n_x * n_c), 2 * states), "seq_1")
-    pieces = add_split(quarter, peaks, n_y * n_z)
+    quarter = exchange(half.reshape(n_x, width // (n_x * n_c), states), "seq_1")
+    pieces = add_split(quarter, read, peaks, n_y * n_z)
     arrived = exchange(pieces, ("seq_0", "dp_0"))
     return state_input_grad[None], close(arrived, own_rows)
 
@@ -531,6 +603,7 @@
         P(DP, SEQ, None),
         P(DP, SEQ, None, None),
     )
+
     return jax.shard_map(
         on_device,
         mesh=torus,

time: 107 us -> 112 us (1.047)
  the two profiles are of different devices: /device:TPU:1 before, /device:TPU:4 now
where the time goes in v8:
time: 112 us; the launch traced here: 111 us
  blocking collectives  58.2 us (52%)
  starting transfers between devices  23.7 us (21%)
  Pallas kernels  20.8 us (19%)
  waiting for transfers between devices  7.62 us (7%)
    all_to_all x2, blocking collectives, exchange(): return lax.all_to_all(x, axes, 0, 0, tiled=True)  58.2 us
    all_to_all x2, starting transfers between devices, exchange(): return lax.all_to_all(x, axes, 0, 0, tiled=True)  11.5 us
    pallas_call x1, Pallas kernels, inner_terms(): pl.pallas_call(inner_body, grid=(grid,), in_specs=[pl.BlockSpec((tokens,...  7.06 us
    ppermute x3, starting transfers between devices, swapped(): return lax.ppermute(x, 'dp_1', [(0, 1), (1, 0)])  6.22 us
    ppermute x1, waiting for transfers between devices, on_device(): got = lax.ppermute(send, 'seq_1', [(0, 1), (1, 0), (2, 3), (3, 2)])  4.3 us
    pallas_call x1, Pallas kernels, turn(): pl.pallas_call(turn_body, grid=(grid,), in_specs=[pl.BlockSpec((tokens, s...  3.73 us
    all_to_all x2, waiting for transfers between devices, exchange(): return lax.all_to_all(x, axes, 0, 0, tiled=True)  3.31 us
    pallas_call x1, Pallas kernels, summarize(): pl.pallas_call(summary_body, grid=(grid,), in_specs=[pl.BlockSpec((tokens...  3.09 us
  transfers between devices with their start and end apart: 7, of which 2 were waited for; matrix products, arithmetic and copies ran while one was open for 0% of the time, Pallas kernels for 14%

profile of v8, /device:TPU:4, one launch (start us, length us, event | category | flops | bytes accessed | tf_op | source)
XLA Modules:
  0.0 111.3 jit_solution(9451132702891361058)
XLA Ops:
  0.6 3.1 %summarize.1 = bf16[32,88,128]{2,1,0:T(8,128)(2,1)S(1)} custom-call(bf16[256,2560]{1,0:T(8,128)(2,1)} %bitcast.15, bf16[256,2560]{1,0:T(8,128)(2,1)} %bitcast.17, f32[40,256]{1,0:T(8,128)} %bitcast.21, bf16[256,256]{1,0:T(8,128)(2,1)} %bitcast.19), custom_call_target="tpu_custom_call" | custom-call | tf_op jit(solution)/shard_map/summarize/pallas_call | solution.py:129
  3.7 31.1 %all_to_all.20.got_ref = bf16[32,88,128]{2,1,0:T(8,128)(2,1)S(1)} all-to-all(bf16[32,88,128]{2,1,0:T(8,128)(2,1)S(1)} %summarize.1), channel_id=1, replica_groups=mesh['seq_0'=8,'seq_1'=4,'dp_0'=8,'dp_1'=2] {'seq_0','seq_1'}, dimensions={0} | all-to-all | bytes 1441792 | tf_op jit(solution)/shard_map/all_to_all | solution.py:30
  34.8 0.0 copy-start
  34.8 1.1 scan_states.1
  35.9 5.6 %all-to-all-start.1 = ((bf16[32,80,128]{2,1,0:T(8,128)(2,1)}), bf16[32,80,128]{2,1,0:T(8,128)(2,1)S(1)}, u32[]{:S(2)}, u32[]{:S(2)}) async-start(bf16[32,80,128]{2,1,0:T(8,128)(2,1)} %get-tuple-element.19), calls=%async_computation.1 | async-start | bytes 1310720 | tf_op jit(solution)/shard_map/all_to_all | solution.py:30
  41.4 0.0 copy-done
  41.4 0.0 copy-start.1
  41.5 0.0 copy-start.2
  41.5 0.0 copy-start.3
  41.5 0.0 copy-start.4
  41.5 0.0 copy-start.5
  41.5 0.0 copy-start.6
  41.5 3.7 %turn.1 = (bf16[4,4,80,256]{3,2,1,0:T(8,128)(2,1)S(1)}, bf16[4,4,80,256]{3,2,1,0:T(8,128)(2,1)}) custom-call(bf16[256,2560]{1,0:T(8,128)(2,1)S(1)} %bitcast.16), custom_call_target="tpu_custom_call" | custom-call | flops 1000000000 | bytes 3000000 | tf_op jit(solution)/shard_map/turn/pallas_call | solution.py:332
  45.2 1.9 %collective-permute-start = (bf16[1280,256]{1,0:T(8,128)(2,1)}, bf16[1280,256]{1,0:T(8,128)(2,1)S(1)}, u32[]{:S(2)}, u32[]{:S(2)}) collective-permute-start(bf16[1280,256]{1,0:T(8,128)(2,1)} %bitcast.9), channel_id=1, source_target_pairs={{0,1},{1,0},{2,3},{3,2},{4,5},{5,4},{6,7},{7,6},{8,9},{9,8},{10,11... | collective-permute-start | bytes 1966088 | tf_op jit(solution)/shard_map/ppermute | solution.py:34
  47.2 0.0 copy-done.1
  47.2 0.0 copy-done.2
  47.2 0.0 copy-done.3
  47.2 0.0 copy-done.4
  47.2 0.0 copy-done.5
  47.2 0.0 copy-done.6
  47.2 7.1 %inner_terms.1 = (bf16[256,3072]{1,0:T(8,128)(2,1)S(1)}, bf16[256,128]{1,0:T(8,128)(2,1)}) custom-call(bf16[256,2560]{1,0:T(8,128)(2,1)S(1)} %bitcast.18, bf16[256,2560]{1,0:T(8,128)(2,1)S(1)} %bitcast.23, f32[40,256]{1,0:T(8,128)S(1)} %bitcast.22, f32[40,256]{1,0:T(8,128)S(1)} %bitcast.25, bf16[256,256]{1,0:T(8,128)(2,1)S(1)} %bitcast.20, ...), custom_call_target="tpu_custom_call" | custom-call | flops 4000000000 | bytes 6000000 | tf_op jit(solution)/shard_map/inner_terms/pallas_call | solution.py:265
  54.3 2.4 %collective-permute-start.2 = (bf16[256,128]{1,0:T(8,128)(2,1)}, bf16[256,128]{1,0:T(8,128)(2,1)}, u32[]{:S(2)}, u32[]{:S(2)}) collective-permute-start(bf16[256,128]{1,0:T(8,128)(2,1)} %get-tuple-element.22.read_ref.mine_ref), channel_id=1, source_target_pairs={{0,1},{1,0},{2,3},{3,2},{4,5},{5,4},{6,7},{7,6},{8,9},{9,8},{10,11... | collective-permute-start | bytes 196616 | tf_op jit(solution)/shard_map/ppermute | solution.py:34
  56.7 3.3 %all-to-all-done.1 = bf16[32,80,128]{2,1,0:T(8,128)(2,1)S(1)} async-done(((bf16[32,80,128]{2,1,0:T(8,128)(2,1)}), bf16[32,80,128]{2,1,0:T(8,128)(2,1)S(1)}, u32[]{:S(2)}, u32[]{:S(2)}) %all-to-all-start.1) | async-done | bytes 655392 | tf_op jit(solution)/shard_map/all_to_all | solution.py:30
  60.0 0.5 finish.1.right_ref.mine_ref
  60.5 1.9 %collective-permute-start.1 = (bf16[264,128]{1,0:T(8,128)(2,1)S(1)}, bf16[264,128]{1,0:T(8,128)(2,1)S(1)}, u32[]{:S(2)}, u32[]{:S(2)}) collective-permute-start(bf16[264,128]{1,0:T(8,128)(2,1)S(1)} %finish.1.right_ref.mine_ref), channel_id=1, source_target_pairs={{0,1},{1,0},{2,3},{3,2},{4,5},{5,4},{6,7},{7,6},{8,9},{9,8},{10,11... | collective-permute-start | bytes 202760 | tf_op jit(solution)/shard_map/ppermute | solution.py:34
  62.4 0.0 collective-permute-done.2.got_ref
  62.4 0.0 collective-permute-done.taken_ref.other_ref
  62.4 1.4 %early_product.1 = (f32[2,320,128]{2,1,0:T(8,128)S(1)}, bf16[2,320,128]{2,1,0:T(8,128)(2,1)S(1)}) custom-call(bf16[1280,256]{1,0:T(8,128)(2,1)S(1)} %bitcast.12, bf16[256,128]{1,0:T(8,128)(2,1)} %get-tuple-element.22.read_ref.mine_ref, bf16[1280,256]{1,0:T(8,128)(2,1)S(1)} %collective-permute-done.taken_ref.other_ref, ...), custom_call_target="tpu_custom_call" | custom-call | flops 300000000 | bytes 2000000 | tf_op jit(solution)/shard_map/early_product/pallas_call | solution.py:392
  63.9 2.9 %collective-permute-start.3 = (bf16[2,320,128]{2,1,0:T(8,128)(2,1)S(1)}, bf16[2,320,128]{2,1,0:T(8,128)(2,1)S(1)}, u32[]{:S(2)}, u32[]{:S(2)}) collective-permute-start(bf16[2,320,128]{2,1,0:T(8,128)(2,1)S(1)} %get-tuple-element.28), channel_id=1, source_target_pairs={{0,32},{16,48},{32,0},{48,16},{1,33},{17,49},{33,1},{49,17},{2,34}... | collective-permute-start | bytes 491528 | tf_op jit(solution)/shard_map/ppermute | solution.py:582
  66.8 2.0 %own_product.1 = (f32[1280,128]{1,0:T(8,128)S(1)}, bf16[1280,256]{1,0:T(8,128)(2,1)S(1)}, bf16[256,256]{1,0:T(8,128)(2,1)}) custom-call(bf16[1280,256]{1,0:T(8,128)(2,1)S(1)} %bitcast.13, bf16[264,128]{1,0:T(8,128)(2,1)S(1)} %finish.1.right_ref.mine_ref, bf16[1280,256]{1,0:T(8,128)(2,1)S(1)} %collective-permute-done.taken_ref.other_ref, ...), custom_call_target="tpu_custom_call" | custom-call | flops 300000000 | bytes 2000000 | tf_op jit(solution)/shard_map/own_product/pallas_call | solution.py:448
  68.8 0.0 collective-permute-done.1.got_ref
  68.8 1.1 multiply.1
  69.9 5.9 %all-to-all-start.2 = ((bf16[4,320,128]{2,1,0:T(8,128)(2,1)}), bf16[4,320,128]{2,1,0:T(8,128)(2,1)S(1)}, u32[]{:S(2)}, u32[]{:S(2)}) async-start(bf16[4,320,128]{2,1,0:T(8,128)(2,1)} %bitcast.11), calls=%async_computation.2 | async-start | bytes 655360 | tf_op jit(solution)/shard_map/all_to_all | solution.py:30
  75.8 0.0 collective-permute-done.3.got_ref
  75.9 3.1 %collective-permute-start.4 = (bf16[320,128]{1,0:T(8,128)(2,1)S(1)}, bf16[320,128]{1,0:T(8,128)(2,1)S(1)}, u32[]{:S(2)}, u32[]{:S(2)}) collective-permute-start(bf16[320,128]{1,0:T(8,128)(2,1)S(1)} %get-tuple-element.30), channel_id=1, source_target_pairs={{0,16},{16,0},{32,48},{48,32},{1,17},{17,1},{33,49},{49,33},{2,18}... | collective-permute-start | bytes 245768 | tf_op jit(solution)/shard_map/ppermute | solution.py:584
  79.0 4.3 %collective-permute-done.4.got_ref = bf16[320,128]{1,0:T(8,128)(2,1)S(1)} collective-permute-done((bf16[320,128]{1,0:T(8,128)(2,1)S(1)}, bf16[320,128]{1,0:T(8,128)(2,1)S(1)}, u32[]{:S(2)}, u32[]{:S(2)}) %collective-permute-start.4) | collective-permute-done | bytes 81952 | tf_op jit(solution)/shard_map/ppermute | solution.py:584
  83.3 0.0 all-to-all-done.2.got_ref
  83.3 0.1 add_split.1
  83.4 27.2 %all_to_all.21.got_ref = bf16[64,8,256]{2,1,0:T(8,128)(2,1)S(1)} all-to-all(bf16[64,8,256]{2,1,0:T(8,128)(2,1)S(1)} %add_split.1), channel_id=1, replica_groups=mesh['seq_0'=8,'seq_1'=4,'dp_0'=8,'dp_1'=2] {'seq_0','dp_0'}, dimensions={0} | all-to-all | bytes 524288 | tf_op jit(solution)/shard_map/all_to_all | solution.py:30
  110.6 0.7 close.1
  (2 shorter events, 0.0 us)
Async XLA Ops:
  34.8 6.6 %copy-start = (bf16[1,256,2560]{2,1,0:T(8,128)(2,1)S(1)}, bf16[1,256,2560]{2,1,0:T(8,128)(2,1)}, u32[]{:S(2)}) copy-start(bf16[1,256,2560]{2,1,0:T(8,128)(2,1)} %param.7) | copy-start | bytes 3932164
  35.9 24.1 %all-to-all-start.1 = ((bf16[32,80,128]{2,1,0:T(8,128)(2,1)}), bf16[32,80,128]{2,1,0:T(8,128)(2,1)S(1)}, u32[]{:S(2)}, u32[]{:S(2)}) async-start(bf16[32,80,128]{2,1,0:T(8,128)(2,1)} %get-tuple-element.19), calls=%async_computation.1 | async-start | bytes 1310720 | tf_op jit(solution)/shard_map/all_to_all | solution.py:30
  41.4 5.7 %copy-start.1 = (bf16[1,256,2560]{2,1,0:T(8,128)(2,1)S(1)}, bf16[1,256,2560]{2,1,0:T(8,128)(2,1)}, u32[]{:S(2)}) copy-start(bf16[1,256,2560]{2,1,0:T(8,128)(2,1)} %param.9) | copy-start | bytes 3932164
  41.5 5.7 %copy-start.2 = (bf16[1,256,256]{2,1,0:T(8,128)(2,1)S(1)}, bf16[1,256,256]{2,1,0:T(8,128)(2,1)}, u32[]{:S(2)}) copy-start(bf16[1,256,256]{2,1,0:T(8,128)(2,1)} %param.12) | copy-start | bytes 393220
  41.5 5.7 %copy-start.3 = (f32[1,40,256]{2,1,0:T(8,128)S(1)}, f32[1,40,256]{2,1,0:T(8,128)}, u32[]{:S(2)}) copy-start(f32[1,40,256]{2,1,0:T(8,128)} %param.11) | copy-start | bytes 122884
  41.5 5.7 %copy-start.4 = (bf16[1,256,2560]{2,1,0:T(8,128)(2,1)S(1)}, bf16[1,256,2560]{2,1,0:T(8,128)(2,1)}, u32[]{:S(2)}) copy-start(bf16[1,256,2560]{2,1,0:T(8,128)(2,1)} %param.8) | copy-start | bytes 3932164
  41.5 5.7 %copy-start.5 = (bf16[1,1,2560,128]{3,2,1,0:T(8,128)(2,1)S(1)}, bf16[1,1,2560,128]{3,2,1,0:T(8,128)(2,1)}, u32[]{:S(2)}) copy-start(bf16[1,1,2560,128]{3,2,1,0:T(8,128)(2,1)} %param.13) | copy-start | bytes 1966084
  41.5 5.7 %copy-start.6 = (f32[1,40,256]{2,1,0:T(8,128)S(1)}, f32[1,40,256]{2,1,0:T(8,128)}, u32[]{:S(2)}) copy-start(f32[1,40,256]{2,1,0:T(8,128)} %param.10) | copy-start | bytes 122884
  45.2 17.2 %collective-permute-start = (bf16[1280,256]{1,0:T(8,128)(2,1)}, bf16[1280,256]{1,0:T(8,128)(2,1)S(1)}, u32[]{:S(2)}, u32[]{:S(2)}) collective-permute-start(bf16[1280,256]{1,0:T(8,128)(2,1)} %bitcast.9), channel_id=1, source_target_pairs={{0,1},{1,0},{2,3},{3,2},{4,5},{5,4},{6,7},{7,6},{8,9},{9,8},{10,11... | collective-permute-start | bytes 1966088 | tf_op jit(solution)/shard_map/ppermute | solution.py:34
  54.3 8.1 %collective-permute-start.2 = (bf16[256,128]{1,0:T(8,128)(2,1)}, bf16[256,128]{1,0:T(8,128)(2,1)}, u32[]{:S(2)}, u32[]{:S(2)}) collective-permute-start(bf16[256,128]{1,0:T(8,128)(2,1)} %get-tuple-element.22.read_ref.mine_ref), channel_id=1, source_target_pairs={{0,1},{1,0},{2,3},{3,2},{4,5},{5,4},{6,7},{7,6},{8,9},{9,8},{10,11... | collective-permute-start | bytes 196616 | tf_op jit(solution)/shard_map/ppermute | solution.py:34
  60.5 8.3 %collective-permute-start.1 = (bf16[264,128]{1,0:T(8,128)(2,1)S(1)}, bf16[264,128]{1,0:T(8,128)(2,1)S(1)}, u32[]{:S(2)}, u32[]{:S(2)}) collective-permute-start(bf16[264,128]{1,0:T(8,128)(2,1)S(1)} %finish.1.right_ref.mine_ref), channel_id=1, source_target_pairs={{0,1},{1,0},{2,3},{3,2},{4,5},{5,4},{6,7},{7,6},{8,9},{9,8},{10,11... | collective-permute-start | bytes 202760 | tf_op jit(solution)/shard_map/ppermute | solution.py:34
  63.9 12.0 %collective-permute-start.3 = (bf16[2,320,128]{2,1,0:T(8,128)(2,1)S(1)}, bf16[2,320,128]{2,1,0:T(8,128)(2,1)S(1)}, u32[]{:S(2)}, u32[]{:S(2)}) collective-permute-start(bf16[2,320,128]{2,1,0:T(8,128)(2,1)S(1)} %get-tuple-element.28), channel_id=1, source_target_pairs={{0,32},{16,48},{32,0},{48,16},{1,33},{17,49},{33,1},{49,17},{2,34}... | collective-permute-start | bytes 491528 | tf_op jit(solution)/shard_map/ppermute | solution.py:582
  69.9 13.4 %all-to-all-start.2 = ((bf16[4,320,128]{2,1,0:T(8,128)(2,1)}), bf16[4,320,128]{2,1,0:T(8,128)(2,1)S(1)}, u32[]{:S(2)}, u32[]{:S(2)}) async-start(bf16[4,320,128]{2,1,0:T(8,128)(2,1)} %bitcast.11), calls=%async_computation.2 | async-start | bytes 655360 | tf_op jit(solution)/shard_map/all_to_all | solution.py:30
  75.9 7.4 %collective-permute-start.4 = (bf16[320,128]{1,0:T(8,128)(2,1)S(1)}, bf16[320,128]{1,0:T(8,128)(2,1)S(1)}, u32[]{:S(2)}, u32[]{:S(2)}) collective-permute-start(bf16[320,128]{1,0:T(8,128)(2,1)S(1)} %get-tuple-element.30), channel_id=1, source_target_pairs={{0,16},{16,0},{32,48},{48,32},{1,17},{17,1},{33,49},{49,33},{2,18}... | collective-permute-start | bytes 245768 | tf_op jit(solution)/shard_map/ppermute | solution.py:584

commit v9 on v7

--- a/solution.py
+++ b/solution.py
@@ -341,7 +341,7 @@
     return own.reshape(width // n_c, tokens), other.reshape(width // n_c, tokens)
 
 
-def finish_body(terms_ref, beyond_ref, peak_ref, grad_ref, send_ref):
+def finish_body(terms_ref, beyond_ref, peak_ref, send_ref):
     channels, states = beyond_ref.shape
     tokens = terms_ref.shape[0]
     carried = jnp.dot(terms_ref[:, :channels], beyond_ref[...], preferred_element_type=f32)
@@ -356,7 +356,6 @@
     send_ref[:tokens, states:] = part(4)
     send_ref[tokens:, :states] = jnp.broadcast_to(peak_ref[...], (8, states)).astype(bf16)
     send_ref[tokens:, states:] = jnp.zeros((8, states), bf16)
-    grad_ref[...] = send_ref[:tokens, :]
 
 
 def finish(terms, beyond, peak):
@@ -364,20 +363,18 @@
     states = beyond.shape[1]
     return pl.pallas_call(
         finish_body,
-        out_shape=[
-            jax.ShapeDtypeStruct((tokens, 2 * states), bf16),
-            jax.ShapeDtypeStruct((tokens + 8, 2 * states), bf16),
-        ],
+        out_shape=jax.ShapeDtypeStruct((tokens + 8, 2 * states), bf16),
         compiler_params=budget(16),
         name="finish",
     )(terms, beyond, peak)
 
 
-def own_body(left_ref, right_ref, taken_ref, out_ref, held_ref, sem):
+def own_body(left_ref, right_ref, taken_ref, out_ref, held_ref, grad_ref, sem):
     tokens = left_ref.shape[1]
     copy = pltpu.make_async_copy(taken_ref, held_ref, sem)
     copy.start()
     out_ref[...] = jnp.dot(left_ref[...], right_ref[:tokens, :], preferred_element_type=f32)
+    grad_ref[...] = right_ref[:tokens, :]
     copy.wait()
 
 
@@ -391,7 +388,11 @@
             pl.BlockSpec(memory_space=pltpu.VMEM),
             pl.BlockSpec(memory_space=pltpu.HBM),
         ],
-        out_shape=[pltpu.VMEM((rows, cols), f32), pltpu.VMEM(taken.shape, bf16)],
+        out_shape=[
+            pltpu.VMEM((rows, cols), f32),
+            pltpu.VMEM(taken.shape, bf16),
+            jax.ShapeDtypeStruct((left.shape[1], cols), bf16),
+        ],
         scratch_shapes=[pltpu.SemaphoreType.DMA],
         compiler_params=budget(16),
         cost_estimate=pl.CostEstimate(
@@ -511,8 +512,8 @@
     )
     kept, given = turn(rows_in, n_x, n_c)
     taken = swapped(given)
-    state_input_grad, sums = finish(terms, beyond, seq_peaks)
-    own, held = own_product(kept, sums, taken)
+    sums = finish(terms, beyond, seq_peaks)
+    own, held, state_input_grad = own_product(kept, sums, taken)
     half, peaks = multiply(own, sums, held, swapped(sums))
     quarter = exchange(half.reshape(n_x, width // (n_x * n_c), 2 * states), "seq_1")
     pieces = add_split(quarter, peaks, n_y * n_z)

time: 107 us -> 107 us (level)
  no operation moved by 1% of the time
where the time goes in v9:
time: 107 us; the launch traced here: 105 us
  blocking collectives  68.2 us (64%)
  Pallas kernels  17.9 us (17%)
  starting transfers between devices  15 us (14%)
  waiting for transfers between devices  3.5 us (3%)
    all_to_all x3, blocking collectives, exchange(): return lax.all_to_all(x, axes, 0, 0, tiled=True)  68.2 us
    ppermute x2, starting transfers between devices, swapped(): return lax.ppermute(x, 'dp_1', [(0, 1), (1, 0)])  9.46 us
    pallas_call x1, Pallas kernels, inner_terms(): pl.pallas_call(inner_body, grid=(grid,), in_specs=[pl.BlockSpec((tokens,...  6.42 us
    all_to_all x1, starting transfers between devices, exchange(): return lax.all_to_all(x, axes, 0, 0, tiled=True)  5.53 us
    pallas_call x1, Pallas kernels, turn(): pl.pallas_call(turn_body, grid=(grid,), in_specs=[pl.BlockSpec((tokens, s...  3.73 us
    all_to_all x1, waiting for transfers between devices, exchange(): return lax.all_to_all(x, axes, 0, 0, tiled=True)  3.5 us
    pallas_call x1, Pallas kernels, summarize(): pl.pallas_call(summary_body, grid=(grid,), in_specs=[pl.BlockSpec((tokens...  3.09 us
  transfers between devices with their start and end apart: 3, of which 1 were waited for; matrix products, arithmetic and copies ran while one was open for 0% of the time, Pallas kernels for 12%

profile of v9, /device:TPU:1, one launch (start us, length us, event | category | flops | bytes accessed | tf_op | source)
XLA Modules:
  0.0 105.4 jit_solution(8737176141923520699)
XLA Ops:
  0.6 3.1 %summarize.1 = bf16[32,88,128]{2,1,0:T(8,128)(2,1)S(1)} custom-call(bf16[256,2560]{1,0:T(8,128)(2,1)} %bitcast.13, bf16[256,2560]{1,0:T(8,128)(2,1)} %bitcast.15, f32[40,256]{1,0:T(8,128)} %bitcast.21, bf16[256,256]{1,0:T(8,128)(2,1)} %bitcast.19), custom_call_target="tpu_custom_call" | custom-call | tf_op jit(solution)/shard_map/summarize/pallas_call | solution.py:129
  3.7 30.3 %all_to_all.20.got_ref = bf16[32,88,128]{2,1,0:T(8,128)(2,1)S(1)} all-to-all(bf16[32,88,128]{2,1,0:T(8,128)(2,1)S(1)} %summarize.1), channel_id=1, replica_groups=mesh['seq_0'=8,'seq_1'=4,'dp_0'=8,'dp_1'=2] {'seq_0','seq_1'}, dimensions={0} | all-to-all | bytes 1441792 | tf_op jit(solution)/shard_map/all_to_all | solution.py:30
  34.0 0.0 copy-start
  34.0 1.1 %scan_states.1 = (bf16[32,80,128]{2,1,0:T(8,128)(2,1)}, f32[1,128]{1,0:T(1,128)S(1)}) custom-call(bf16[32,88,128]{2,1,0:T(8,128)(2,1)S(1)} %all_to_all.20.got_ref), custom_call_target="tpu_custom_call" | custom-call | tf_op jit(solution)/shard_map/scan_states/pallas_call | solution.py:56
  35.1 5.5 %all-to-all-start.1 = ((bf16[32,80,128]{2,1,0:T(8,128)(2,1)}), bf16[32,80,128]{2,1,0:T(8,128)(2,1)S(1)}, u32[]{:S(2)}, u32[]{:S(2)}) async-start(bf16[32,80,128]{2,1,0:T(8,128)(2,1)} %get-tuple-element.12), calls=%async_computation.1 | async-start | bytes 1310720 | tf_op jit(solution)/shard_map/all_to_all | solution.py:30
  40.6 0.0 copy-done
  40.6 0.0 copy-start.1
  40.6 0.0 copy-start.2
  40.7 0.0 copy-start.3
  40.7 0.0 copy-start.4
  40.7 0.0 copy-start.5
  40.7 0.0 copy-start.6
  40.7 3.7 %turn.1 = (bf16[4,4,80,256]{3,2,1,0:T(8,128)(2,1)S(1)}, bf16[4,4,80,256]{3,2,1,0:T(8,128)(2,1)}) custom-call(bf16[256,2560]{1,0:T(8,128)(2,1)S(1)} %bitcast.14), custom_call_target="tpu_custom_call" | custom-call | flops 1000000000 | bytes 3000000 | tf_op jit(solution)/shard_map/turn/pallas_call | solution.py:328
  44.4 3.9 %collective-permute-start = (bf16[1280,256]{1,0:T(8,128)(2,1)}, bf16[1280,256]{1,0:T(8,128)(2,1)}, u32[]{:S(2)}, u32[]{:S(2)}) collective-permute-start(bf16[1280,256]{1,0:T(8,128)(2,1)} %bitcast.9), channel_id=1, source_target_pairs={{0,1},{1,0},{2,3},{3,2},{4,5},{5,4},{6,7},{7,6},{8,9},{9,8},{10,11... | collective-permute-start | bytes 1966088 | tf_op jit(solution)/shard_map/ppermute | solution.py:34
  48.4 0.0 copy-done.1
  48.4 0.0 copy-done.2
  48.4 0.0 copy-done.3
  48.4 0.0 copy-done.4
  48.4 0.0 copy-done.5
  48.4 0.0 copy-done.6
  48.4 6.4 %inner_terms.1.terms_ref = bf16[256,3200]{1,0:T(8,128)(2,1)S(1)} custom-call(bf16[256,2560]{1,0:T(8,128)(2,1)S(1)} %bitcast.16, bf16[256,2560]{1,0:T(8,128)(2,1)S(1)} %bitcast.23, f32[40,256]{1,0:T(8,128)S(1)} %bitcast.22, f32[40,256]{1,0:T(8,128)S(1)} %bitcast.25, bf16[256,256]{1,0:T(8,128)(2,1)S(1)} %bitcast.20, bf16[2560,128]{1,0:T(8,128)(2,1)S(1)} %bitcast.24), custom_call_target="tpu_custom_call" | custom-call | flops 4000000000 | bytes 6000000 | tf_op jit(solution)/shard_map/inner_terms/pallas_call | solution.py:264
  54.9 3.5 %all-to-all-done.1 = bf16[32,80,128]{2,1,0:T(8,128)(2,1)S(1)} async-done(((bf16[32,80,128]{2,1,0:T(8,128)(2,1)}), bf16[32,80,128]{2,1,0:T(8,128)(2,1)S(1)}, u32[]{:S(2)}, u32[]{:S(2)}) %all-to-all-start.1) | async-done | bytes 655392 | tf_op jit(solution)/shard_map/all_to_all | solution.py:30
  58.4 0.5 finish.1.right_ref.mine_ref
  58.9 5.5 %collective-permute-start.1 = (bf16[264,256]{1,0:T(8,128)(2,1)S(1)}, bf16[264,256]{1,0:T(8,128)(2,1)S(1)}, u32[]{:S(2)}, u32[]{:S(2)}) collective-permute-start(bf16[264,256]{1,0:T(8,128)(2,1)S(1)} %finish.1.right_ref.mine_ref), channel_id=1, source_target_pairs={{0,1},{1,0},{2,3},{3,2},{4,5},{5,4},{6,7},{7,6},{8,9},{9,8},{10,11... | collective-permute-start | bytes 405512 | tf_op jit(solution)/shard_map/ppermute | solution.py:34
  64.4 0.0 collective-permute-done.taken_ref
  64.4 1.8 %own_product.1 = (f32[1280,256]{1,0:T(8,128)S(1)}, bf16[1280,256]{1,0:T(8,128)(2,1)S(1)}, bf16[256,256]{1,0:T(8,128)(2,1)}) custom-call(bf16[1280,256]{1,0:T(8,128)(2,1)S(1)} %bitcast.17, bf16[264,256]{1,0:T(8,128)(2,1)S(1)} %finish.1.right_ref.mine_ref, bf16[1280,256]{1,0:T(8,128)(2,1)} %collective-permute-done.taken_ref), custom_call_target="tpu_custom_call" | custom-call | flops 300000000 | bytes 2000000 | tf_op jit(solution)/shard_map/own_product/pallas_call | solution.py:384
  66.2 0.0 collective-permute-done.1.got_ref
  66.2 0.3 multiply.1
  66.6 14.0 %all_to_all.21.got_ref = bf16[4,320,256]{2,1,0:T(8,128)(2,1)S(1)} all-to-all(bf16[4,320,256]{2,1,0:T(8,128)(2,1)S(1)} %bitcast.18), channel_id=1, replica_groups=mesh['seq_0'=8,'seq_1'=4,'dp_0'=8,'dp_1'=2] {'seq_1'}, dimensions={0} | all-to-all | bytes 1310720 | tf_op jit(solution)/shard_map/all_to_all | solution.py:30
  80.6 0.2 add_split.1
  80.8 23.9 %all_to_all.22.got_ref = bf16[64,8,256]{2,1,0:T(8,128)(2,1)S(1)} all-to-all(bf16[64,8,256]{2,1,0:T(8,128)(2,1)S(1)} %add_split.1), channel_id=1, replica_groups=mesh['seq_0'=8,'seq_1'=4,'dp_0'=8,'dp_1'=2] {'seq_0','dp_0'}, dimensions={0} | all-to-all | bytes 524288 | tf_op jit(solution)/shard_map/all_to_all | solution.py:30
  104.7 0.7 close.1
Async XLA Ops:
  34.0 6.6 %copy-start = (bf16[1,256,2560]{2,1,0:T(8,128)(2,1)S(1)}, bf16[1,256,2560]{2,1,0:T(8,128)(2,1)}, u32[]{:S(2)}) copy-start(bf16[1,256,2560]{2,1,0:T(8,128)(2,1)} %param.7) | copy-start | bytes 3932164
  35.1 23.3 %all-to-all-start.1 = ((bf16[32,80,128]{2,1,0:T(8,128)(2,1)}), bf16[32,80,128]{2,1,0:T(8,128)(2,1)S(1)}, u32[]{:S(2)}, u32[]{:S(2)}) async-start(bf16[32,80,128]{2,1,0:T(8,128)(2,1)} %get-tuple-element.12), calls=%async_computation.1 | async-start | bytes 1310720 | tf_op jit(solution)/shard_map/all_to_all | solution.py:30
  40.6 7.8 %copy-start.1 = (bf16[1,256,2560]{2,1,0:T(8,128)(2,1)S(1)}, bf16[1,256,2560]{2,1,0:T(8,128)(2,1)}, u32[]{:S(2)}) copy-start(bf16[1,256,2560]{2,1,0:T(8,128)(2,1)} %param.9) | copy-start | bytes 3932164
  40.6 7.8 %copy-start.2 = (bf16[1,256,256]{2,1,0:T(8,128)(2,1)S(1)}, bf16[1,256,256]{2,1,0:T(8,128)(2,1)}, u32[]{:S(2)}) copy-start(bf16[1,256,256]{2,1,0:T(8,128)(2,1)} %param.12) | copy-start | bytes 393220
  40.7 7.8 %copy-start.3 = (f32[1,40,256]{2,1,0:T(8,128)S(1)}, f32[1,40,256]{2,1,0:T(8,128)}, u32[]{:S(2)}) copy-start(f32[1,40,256]{2,1,0:T(8,128)} %param.11) | copy-start | bytes 122884
  40.7 7.7 %copy-start.4 = (bf16[1,256,2560]{2,1,0:T(8,128)(2,1)S(1)}, bf16[1,256,2560]{2,1,0:T(8,128)(2,1)}, u32[]{:S(2)}) copy-start(bf16[1,256,2560]{2,1,0:T(8,128)(2,1)} %param.8) | copy-start | bytes 3932164
  40.7 7.7 %copy-start.5 = (bf16[1,1,2560,128]{3,2,1,0:T(8,128)(2,1)S(1)}, bf16[1,1,2560,128]{3,2,1,0:T(8,128)(2,1)}, u32[]{:S(2)}) copy-start(bf16[1,1,2560,128]{3,2,1,0:T(8,128)(2,1)} %param.13) | copy-start | bytes 1966084
  40.7 7.7 %copy-start.6 = (f32[1,40,256]{2,1,0:T(8,128)S(1)}, f32[1,40,256]{2,1,0:T(8,128)}, u32[]{:S(2)}) copy-start(f32[1,40,256]{2,1,0:T(8,128)} %param.10) | copy-start | bytes 122884
  44.4 20.0 %collective-permute-start = (bf16[1280,256]{1,0:T(8,128)(2,1)}, bf16[1280,256]{1,0:T(8,128)(2,1)}, u32[]{:S(2)}, u32[]{:S(2)}) collective-permute-start(bf16[1280,256]{1,0:T(8,128)(2,1)} %bitcast.9), channel_id=1, source_target_pairs={{0,1},{1,0},{2,3},{3,2},{4,5},{5,4},{6,7},{7,6},{8,9},{9,8},{10,11... | collective-permute-start | bytes 1966088 | tf_op jit(solution)/shard_map/ppermute | solution.py:34
  58.9 7.4 %collective-permute-start.1 = (bf16[264,256]{1,0:T(8,128)(2,1)S(1)}, bf16[264,256]{1,0:T(8,128)(2,1)S(1)}, u32[]{:S(2)}, u32[]{:S(2)}) collective-permute-start(bf16[264,256]{1,0:T(8,128)(2,1)S(1)} %finish.1.right_ref.mine_ref), channel_id=1, source_target_pairs={{0,1},{1,0},{2,3},{3,2},{4,5},{5,4},{6,7},{7,6},{8,9},{9,8},{10,11... | collective-permute-start | bytes 405512 | tf_op jit(solution)/shard_map/ppermute | solution.py:34
